TPU v7x, 8 devices: a whole 2x2x1 slice. The times are simulated.
8 devices in a mesh: rep: 2 (over y, z), dp: 4 (over x, core).
Axes of the slice: x: 2, y: 2, z: 1, core: 2. Of those that a mesh axis runs over, the one named last changes fastest.
Arguments:
- x: bfloat16 [8, 2048, 1152], P(('rep', 'dp')), parts along dimension 0
- dy: bfloat16 [8, 2048, 1152], P(('rep', 'dp')), parts along dimension 0
- w_gate: bfloat16 [2, 1152, 4608], replicated
- w_up: bfloat16 [2, 1152, 4608], replicated
- w_down: bfloat16 [2, 4608, 1152], replicated
- m_w_gate: float32 [2, 1152, 4608], P(None, 'dp')
- m_w_up: float32 [2, 1152, 4608], P(None, 'dp')
- m_w_down: float32 [2, 4608, 1152], P(None, 'dp')
- v_w_gate: float32 [2, 1152, 4608], P(None, 'dp')
- v_w_up: float32 [2, 1152, 4608], P(None, 'dp')
- v_w_down: float32 [2, 4608, 1152], P(None, 'dp')
Outputs:
- output 1: bfloat16 [4, 1152, 4608], P('rep'), parts along dimension 0
- output 2: bfloat16 [4, 1152, 4608], P('rep'), parts along dimension 0
- output 3: bfloat16 [4, 4608, 1152], P('rep'), parts along dimension 0
- output 4: float32 [4, 1152, 4608], P('rep', 'dp'), parts along dimension 0
- output 5: float32 [4, 1152, 4608], P('rep', 'dp'), parts along dimension 0
- output 6: float32 [4, 4608, 1152], P('rep', 'dp'), parts along dimension 0
- output 7: float32 [4, 1152, 4608], P('rep', 'dp'), parts along dimension 0
- output 8: float32 [4, 1152, 4608], P('rep', 'dp'), parts along dimension 0
- output 9: float32 [4, 4608, 1152], P('rep', 'dp'), parts along dimension 0
There are 2 independent parts. A program takes and returns all parts, laid end to end along the dimension named above; an argument that names none is the same for every part.
All inputs are finite; a program needn't handle non-finite values.
Results may differ from a plain program's by a relative error of at most 0.022.
Values are sent between devices in bfloat16 or wider.
A program may use at most 2 GiB of HBM per device.

v0:
```python
import functools

import jax
import jax.numpy as jnp
from jax import lax
from jax.experimental import pallas as pl
from jax.experimental.pallas import tpu as pltpu
from jax.sharding import PartitionSpec as P


F32, BF16 = jnp.float32, jnp.bfloat16
DEVICES = 4
LANES = 128
ANY = pl.BlockSpec(memory_space=pl.ANY)
VMEM_BYTES = 67_043_328


def dot(a, b, dims):
    return lax.dot_general(a, b, (dims, ((), ())), preferred_element_type=F32)


NN, NT, TT = ((1,), (0,)), ((1,), (1,)), ((0,), (1,))


def sigmoid(x):
    return 1.0 / (1.0 + jnp.exp(-x))


def loop(n, body):
    lax.fori_loop(0, n, lambda i, c: (body(i), c)[1], 0)


def grads_kernel(
    x, dy, wg, wu, wd,
    gg, gu, gd, factor, gate_s, up_s, a0t_s, ht_s, mate, own, far, cross,
    AT, DD, DT, ACC, GR, ACT, DG, DU, WD, OWNB, MATEB, FARB, SQ, SQS,
    wsem, iosem, d2d_send, d2d_recv, own_sem, far_sem, x_send, x_recv, fsem, sq_send, sq_recv,
):
    T, D = x.shape
    F = wg.shape[2]
    W = DEVICES * LANES
    NT_ = F // W
    H = T // 2
    R = D // DEVICES
    me = lax.axis_index("dp")
    chip, core = me // 2, me % 2
    mate_id, cross_id = {"dp": chip * 2 + 1 - core}, {"dp": (1 - chip) * 2 + core}
    lo, hi = pl.ds(0, H), pl.ds(H, H)

    barrier = pltpu.get_barrier_semaphore()
    for k in range(1, DEVICES):
        pl.semaphore_signal(barrier, inc=1, device_id={"dp": (me + k) % DEVICES}, device_id_type=pl.DeviceIdType.MESH)
    pl.semaphore_wait(barrier, DEVICES - 1)

    def columns(p, j):
        return pl.ds(pl.multiple_of(p * (F // DEVICES) + j * LANES, LANES), LANES)

    def weights(l, j, q, bufs):
        slot = q % 2
        copies = []
        for p in range(DEVICES):
            piece = pl.ds(p * LANES, LANES)
            if bufs is not None:
                copies.append(pltpu.make_async_copy(wg.at[l, :, columns(p, j)], bufs[0].at[slot, :, piece], wsem.at[slot, 0, p]))
                copies.append(pltpu.make_async_copy(wu.at[l, :, columns(p, j)], bufs[1].at[slot, :, piece], wsem.at[slot, 1, p]))
            copies.append(pltpu.make_async_copy(wd.at[l, columns(p, j), :], WD.at[slot, piece, :], wsem.at[slot, 2, p]))
        return copies

    def start(copies):
        for c in copies:
            c.start()

    def wait(copies):
        for c in copies:
            c.wait()

    def d2d(t, k):
        return pltpu.make_async_remote_copy(
            src_ref=GR.at[k, :, 1 - core], dst_ref=mate.at[t, k], send_sem=d2d_send.at[k], recv_sem=d2d_recv.at[t],
            device_id=mate_id, device_id_type=pl.DeviceIdType.MESH)

    def keep(t, k):
        return pltpu.make_async_copy(GR.at[k, :, core], own.at[t, k], own_sem.at[k])

    def across(t):
        return pltpu.make_async_remote_copy(
            src_ref=far.at[t], dst_ref=cross.at[t], send_sem=x_send.at[t], recv_sem=x_recv.at[t],
            device_id=cross_id, device_id_type=pl.DeviceIdType.MESH)

    def far_loads(t):
        return [
            pltpu.make_async_copy(own.at[t, :, 1 - chip], OWNB, far_sem.at[0]),
            pltpu.make_async_copy(mate.at[t, :, 1 - chip], MATEB, far_sem.at[1]),
        ]

    def far_store(t):
        return pltpu.make_async_copy(FARB, far.at[t], far_sem.at[2])

    def mate_arrived(t):
        pltpu.make_async_copy(mate.at[t], mate.at[t], d2d_recv.at[t]).wait()

    def comm1(t):
        mate_arrived(t)
        for k in range(3):
            keep(t, k).wait()
        start(far_loads(t))

    def comm2(t):
        wait(far_loads(t))

    def far_sum():
        for k in range(3):
            for r in range(0, R, 32):
                rows = slice(r, r + 32)
                FARB[k, rows, :] = (OWNB[k, rows, :].astype(F32) + MATEB[k, rows, :].astype(F32)).astype(BF16)

    def comm3(t):
        far_store(t).start()

    def comm4(t):
        far_store(t).wait()
        across(t).start()

    def sent(t):
        for k in range(3):
            d2d(t, k).wait_send()

    def put(k, rows, value):
        n = value.shape[0]
        value = value.astype(BF16)
        if k < 2:
            for i in range(n // R):
                o = rows // R + i
                GR[k, o // 2, o % 2] = value[i * R : (i + 1) * R]
        else:
            for i in range(n // R):
                for o in range(DEVICES):
                    GR[k, o // 2, o % 2, :, (rows // R + i) * LANES : (rows // R + i + 1) * LANES] = value[
                        i * R : (i + 1) * R, o * LANES : (o + 1) * LANES
                    ]

    def ship(t, k):
        d2d(t, k).start()
        keep(t, k).start()

    def product_back(g_ref, u_ref, d_ref, r0):
        step = 16
        for r in range(0, H, step):
            g, u = g_ref(r, step), u_ref(r, step)
            d = d_ref[r : r + step, :].astype(BF16).astype(F32)
            s = sigmoid(g)
            si = g * s
            ACT[r0 + r : r0 + r + step, :] = (si * u).astype(BF16)
            DU[r0 + r : r0 + r + step, :] = (d * si).astype(BF16)
            DG[r0 + r : r0 + r + step, :] = (d * u * (s + si * (1.0 - s))).astype(BF16)

    def scaled(wide):
        return lax.rsqrt(jnp.mean(wide * wide, axis=0, keepdims=True) + 1e-6)

    def first_half(A, WG, WU):
        load_x = pltpu.make_async_copy(x, DD, iosem.at[0])
        load_x.start()
        start(weights(0, 0, 0, (WG, WU)))
        load_x.wait()

        def norm_x(i):
            r = pl.ds(pl.multiple_of(i * LANES, LANES), LANES)
            wide = DD[r, :].astype(F32)
            scale = lax.rsqrt(jnp.mean(wide * wide, axis=1, keepdims=True) + 1e-6)
            a = (wide * scale).astype(BF16)
            A[r, :] = a
            AT[:, r] = a.T
            DT[:, r] = DD[r, :].T
            ACC[:, r] = jnp.zeros((D, LANES), F32)

        loop(T // LANES, norm_x)
        save_a0t = pltpu.make_async_copy(AT, a0t_s, iosem.at[0])
        save_a0t.start()
        load_dy = pltpu.make_async_copy(dy, DD, iosem.at[1])
        load_dy.start()

        def forward(G0, U0, G1, U1):
            S = ((G0, U0), (G1, U1))

            def stores(j, half):
                return [
                    pltpu.make_async_copy(ref, to.at[j, pl.ds(half * H, H), :], iosem.at[2 + 2 * half + n])
                    for n, (ref, to) in enumerate(zip(S[half], (gate_s, up_s)))
                ]

            def projections(half, slot):
                rows = lo if half == 0 else hi
                S[half][0][...] = dot(A[rows, :], WG[slot], NN)
                S[half][1][...] = dot(A[rows, :], WU[slot], NN)

            def product(half):
                g_ref, u_ref = S[half]
                for r in range(0, H, 16):
                    g = g_ref[r : r + 16, :]
                    ACT[half * H + r : half * H + r + 16, :] = (g * sigmoid(g) * u_ref[r : r + 16, :]).astype(BF16)

            def down(rows, slot):
                ACC[:, rows] += dot(WD[slot], ACT[rows, :], TT)

            def tile(j):
                slot = j % 2
                wait(weights(0, j, j, (WG, WU)))

                @pl.when(j < NT_ - 1)
                def _():
                    start(weights(0, j + 1, j + 1, (WG, WU)))

                @pl.when(j == NT_ - 1)
                def _():
                    start(weights(1, 0, NT_, (WG, WU)))

                @pl.when(j > 0)
                def _():
                    wait(stores(j - 1, 0) + stores(j - 1, 1))

                projections(0, slot)
                start(stores(j, 0))
                projections(1, slot)
                product(0)
                start(stores(j, 1))
                down(lo, slot)
                product(1)
                down(hi, slot)

            loop(NT_, tile)
            wait(stores(NT_ - 1, 0) + stores(NT_ - 1, 1))

        pl.run_scoped(forward, *[pltpu.VMEM((H, W), F32)] * 4)
        save_a0t.wait()
        load_dy.wait()

        def norm_h(i):
            r = pl.ds(pl.multiple_of(i * LANES, LANES), LANES)
            h = (DT[:, r].astype(F32) + ACC[:, r].astype(BF16).astype(F32)).astype(BF16)
            ACC[:, r] = jnp.zeros((D, LANES), F32)
            wide = h.astype(F32)
            a = (wide * scaled(wide)).astype(BF16)
            AT[:, r] = a
            A[r, :] = a.T
            DT[:, r] = h

        loop(T // LANES, norm_h)
        save_h = pltpu.make_async_copy(DT, ht_s, iosem.at[0])
        save_h.start()
        save_h.wait()

        def turn_dy(i):
            r = pl.ds(pl.multiple_of(i * LANES, LANES), LANES)
            DT[:, r] = DD[r, :].T

        loop(T // LANES, turn_dy)

        def layer1(G0, U0, D0, G1, U1, D1):
            S = ((G0, U0, D0), (G1, U1, D1))

            def projections(half, slot):
                rows = lo if half == 0 else hi
                S[half][0][...] = dot(A[rows, :], WG[slot], NN)
                S[half][1][...] = dot(A[rows, :], WU[slot], NN)
                S[half][2][...] = dot(DD[rows, :], WD[slot], NT)

            def back(half):
                g_ref, u_ref, d_ref = S[half]
                product_back(lambda r, n: g_ref[r : r + n, :], lambda r, n: u_ref[r : r + n, :], d_ref, half * H)

            def da(rows, slot):
                ACC[:, rows] += dot(WG[slot], DG[rows, :], NT)
                ACC[:, rows] += dot(WU[slot], DU[rows, :], NT)

            def tile(j):
                slot = (NT_ + j) % 2
                wait(weights(1, j, NT_ + j, (WG, WU)))

                @pl.when(j < NT_ - 1)
                def _():
                    start(weights(1, j + 1, NT_ + j + 1, (WG, WU)))

                @pl.when(j == NT_ - 1)
                def _():
                    start(weights(0, 0, 2 * NT_, None))

                projections(0, slot)
                pl.when(j > 0)(lambda: comm1(j - 1))
                projections(1, slot)
                back(0)
                pl.when(j > 0)(lambda: comm2(j - 1))
                da(lo, slot)
                back(1)
                far_sum()
                pl.when(j > 0)(lambda: comm3(j - 1))
                da(hi, slot)

                @pl.when(j > 0)
                def _():
                    comm4(j - 1)
                    sent(j - 1)

                for k, lhs, rhs in ((2, DT, ACT), (0, AT, DG), (1, AT, DU)):
                    for i in range(2):
                        put(k, i * (D // 2), dot(lhs[i * (D // 2) : (i + 1) * (D // 2), :], rhs[...], NN))
                    ship(j, k)

            loop(NT_, tile)

        pl.run_scoped(layer1, *[pltpu.VMEM((H, W), F32)] * 6)

    pl.run_scoped(first_half, pltpu.VMEM((T, D), BF16), pltpu.VMEM((2, D, W), BF16), pltpu.VMEM((2, D, W), BF16))

    load_a0t = pltpu.make_async_copy(a0t_s, AT, iosem.at[0])
    load_a0t.start()

    def norm_back(HT):
        load_h = pltpu.make_async_copy(ht_s, HT, iosem.at[1])
        load_h.start()
        load_h.wait()

        def part(i):
            r = pl.ds(pl.multiple_of(i * LANES, LANES), LANES)
            wide = HT[:, r].astype(F32)
            scale = scaled(wide)
            da = ACC[:, r].astype(BF16).astype(F32)
            along = jnp.mean(da * wide, axis=0, keepdims=True) * (scale * scale * scale)
            dwide = (da * scale - wide * along).astype(BF16).astype(F32)
            dh = (DT[:, r].astype(F32) + dwide).astype(BF16)
            DT[:, r] = dh
            DD[r, :] = dh.T

        loop(T // LANES, part)

    pl.run_scoped(norm_back, pltpu.VMEM((D, T), BF16))
    load_a0t.wait()

    def layer0(GB, UB, D0, D1):
        S = (D0, D1)

        def loads(j):
            return [
                pltpu.make_async_copy(gate_s.at[j], GB.at[j % 2], iosem.at[2 + j % 2]),
                pltpu.make_async_copy(up_s.at[j], UB.at[j % 2], iosem.at[4 + j % 2]),
            ]

        start(loads(0))

        def tile(j):
            t = NT_ + j
            slot = j % 2
            wait(weights(0, j, 2 * NT_ + j, None))

            @pl.when(j < NT_ - 1)
            def _():
                start(weights(0, j + 1, 2 * NT_ + j + 1, None))
                start(loads(j + 1))

            def back(half):
                product_back(
                    lambda r, n: GB[slot, half * H + r : half * H + r + n, :],
                    lambda r, n: UB[slot, half * H + r : half * H + r + n, :],
                    S[half],
                    half * H,
                )

            S[0][...] = dot(DD[lo, :], WD[slot], NT)
            wait(loads(j))
            comm1(t - 1)
            S[1][...] = dot(DD[hi, :], WD[slot], NT)
            back(0)
            comm2(t - 1)
            sent(t - 1)
            half_sum = pl.ds(0, W)
            ACC[:, half_sum] = dot(DT[:, lo], ACT[lo, :], NN)
            back(1)
            far_sum()
            comm3(t - 1)
            for i in range(2):
                rows = slice(i * (D // 2), (i + 1) * (D // 2))
                put(2, i * (D // 2), ACC[rows, half_sum] + dot(DT[rows, hi], ACT[hi, :], NN))
            ship(t, 2)
            comm4(t - 1)
            for k, rhs in ((0, DG), (1, DU)):
                for i in range(2):
                    put(k, i * (D // 2), dot(AT[i * (D // 2) : (i + 1) * (D // 2), :], rhs[...], NN))
                ship(t, k)

        loop(NT_, tile)

    pl.run_scoped(layer0, pltpu.VMEM((2, T, W), F32), pltpu.VMEM((2, T, W), F32), pltpu.VMEM((H, W), F32), pltpu.VMEM((H, W), F32))

    last = 2 * NT_ - 1
    comm1(last)
    comm2(last)
    far_sum()
    comm3(last)
    comm4(last)
    sent(last)

    def finish(GN, UN, DN, CB):
        SQ[...] = jnp.zeros_like(SQ)

        def outs(t):
            l, j = 1 - t // NT_, t % NT_
            copies = []
            for p in range(DEVICES):
                copies.append(pltpu.make_async_copy(GN.at[:, pl.ds(p * LANES, LANES)], gg.at[l, :, columns(p, j)], fsem.at[3 + p]))
                copies.append(pltpu.make_async_copy(UN.at[:, pl.ds(p * LANES, LANES)], gu.at[l, :, columns(p, j)], fsem.at[7 + p]))
            rows = pl.ds(pl.multiple_of(j * LANES, LANES), LANES)
            copies.append(pltpu.make_async_copy(DN, gd.at[l, rows, :], fsem.at[11]))
            return copies

        def one(t):
            across(t).wait()
            ins = [
                pltpu.make_async_copy(own.at[t, :, chip], OWNB, fsem.at[0]),
                pltpu.make_async_copy(mate.at[t, :, chip], MATEB, fsem.at[1]),
                pltpu.make_async_copy(cross.at[t], CB, fsem.at[2]),
            ]
            start(ins)

            @pl.when(t > 0)
            def _():
                wait(outs(t - 1))

            wait(ins)
            for k in range(3):
                total = OWNB[k].astype(F32) + MATEB[k].astype(F32) + CB[k].astype(F32)
                g = total.astype(BF16)
                wide = g.astype(F32)
                SQ[...] += jnp.sum((wide * wide).reshape(R // 8, 8, W), axis=0)
                if k == 0:
                    GN[...] = g
                elif k == 1:
                    UN[...] = g
                else:
                    tall = jnp.concatenate([g[:, q * LANES : (q + 1) * LANES] for q in range(DEVICES)], axis=0)
                    DN[...] = tall.T
            start(outs(t))

        loop(2 * NT_, one)
        wait(outs(last))

    pl.run_scoped(finish, pltpu.VMEM((R, W), BF16), pltpu.VMEM((R, W), BF16), pltpu.VMEM((LANES, D), BF16), pltpu.VMEM((3, R, W), BF16))

    mine = jnp.sum(SQ[...], keepdims=True)
    SQS[DEVICES] = jnp.broadcast_to(mine, (8, LANES))
    copies = [
        pltpu.make_async_remote_copy(
            src_ref=SQS.at[DEVICES], dst_ref=SQS.at[me], send_sem=sq_send.at[k - 1], recv_sem=sq_recv.at[k - 1],
            device_id={"dp": (me + k) % DEVICES}, device_id_type=pl.DeviceIdType.MESH)
        for k in range(1, DEVICES)
    ]
    start(copies)
    SQS[me] = jnp.broadcast_to(mine, (8, LANES))
    for k in range(1, DEVICES):
        pltpu.make_async_copy(SQS.at[(me + DEVICES - k) % DEVICES], SQS.at[(me + DEVICES - k) % DEVICES], sq_recv.at[k - 1]).wait()
        copies[k - 1].wait_send()
    total = (SQS[0] + SQS[1]) + (SQS[2] + SQS[3])
    count = 2.0 * 3.0 * D * F
    factor[...] = jnp.minimum(1.0, 0.5 * lax.rsqrt(total / count + 1e-30))


def gradients(x, dy, wg, wu, wd):
    T, D = x.shape
    F = wg.shape[2]
    W = DEVICES * LANES
    n, R = F // W, D // DEVICES
    tiles = 2 * n
    hbm = lambda *s, d=BF16: jax.ShapeDtypeStruct(s, d)
    outs = [
        hbm(2, R, F), hbm(2, R, F), hbm(2, F // DEVICES, D), hbm(8, LANES, d=F32),
        hbm(n, T, W, d=F32), hbm(n, T, W, d=F32), hbm(D, T), hbm(D, T),
        hbm(tiles, 3, 2, R, W), hbm(tiles, 3, 2, R, W), hbm(tiles, 3, R, W), hbm(tiles, 3, R, W),
    ]
    sem = pltpu.SemaphoreType.DMA
    return pl.pallas_call(
        grads_kernel,
        out_shape=outs,
        in_specs=[ANY] * 5,
        out_specs=[ANY] * 3 + [pl.BlockSpec(memory_space=pltpu.VMEM)] + [ANY] * 8,
        scratch_shapes=[
            pltpu.VMEM((D, T), BF16), pltpu.VMEM((T, D), BF16), pltpu.VMEM((D, T), BF16), pltpu.VMEM((D, T), F32),
            pltpu.VMEM((3, 2, 2, R, W), BF16),
            pltpu.VMEM((T, W), BF16), pltpu.VMEM((T, W), BF16), pltpu.VMEM((T, W), BF16), pltpu.VMEM((2, W, D), BF16),
            pltpu.VMEM((3, R, W), BF16), pltpu.VMEM((3, R, W), BF16), pltpu.VMEM((3, R, W), BF16),
            pltpu.VMEM((8, W), F32), pltpu.VMEM((DEVICES + 1, 8, LANES), F32),
            sem((2, 3, DEVICES)), sem((6,)), sem((3,)), sem((tiles,)), sem((3,)), sem((3,)),
            sem((tiles,)), sem((tiles,)), sem((12,)), sem((DEVICES - 1,)), sem((DEVICES - 1,)),
        ],
        compiler_params=pltpu.CompilerParams(collective_id=0, has_side_effects=True, vmem_limit_bytes=VMEM_BYTES),
        name="gradients",
    )(x, dy, wg, wu, wd)[:4]


def adamw_kernel(me, factor, g, w, m, v, *refs):
    out, send, new_m, new_v, turn = refs[-5:]
    turn[0] = me[0]
    grad = g[...].astype(F32) * factor[0:1, 0:1]
    one = 0.9 * m[...] + 0.1 * grad
    two = 0.95 * v[...] + 0.05 * grad * grad
    wide = w[...].astype(F32)
    new_w = (wide - 0.02 * (one * lax.rsqrt(two + 1e-8) + 0.1 * wide)).astype(BF16)
    out[...] = new_w
    send[...] = new_w
    new_m[...] = one
    new_v[...] = two


def adamw(me, factor, g, w, m, v, so_far, layer, first, steps, by_columns):
    rows = m.shape[1] if by_columns else LANES
    cols = DEVICES * LANES if by_columns else m.shape[2]
    tile = (None, rows, cols)
    if by_columns:
        block = pl.BlockSpec(tile, lambda i, me: (layer, 0, first + i))
        whole = pl.BlockSpec(tile, lambda i, me: (layer, me[0], first + i))
        alone, send = (rows, steps * cols), pl.BlockSpec((rows, cols), lambda i, me: (0, i))
    else:
        n = m.shape[1] // LANES
        block = pl.BlockSpec(tile, lambda i, me: (layer, first + i, 0))
        whole = pl.BlockSpec(tile, lambda i, me: (layer, me[0] * n + first + i, 0))
        alone, send = (steps * rows, cols), pl.BlockSpec((rows, cols), lambda i, me: (i, 0))
    begun = so_far is not None
    shape = lambda a: jax.ShapeDtypeStruct(a.shape, a.dtype)
    out, sent, new_m, new_v, turn = pl.pallas_call(
        adamw_kernel,
        grid_spec=pltpu.PrefetchScalarGridSpec(
            num_scalar_prefetch=1,
            grid=(steps,),
            in_specs=[pl.BlockSpec((8, LANES), lambda i, me: (0, 0)), block, whole, block, block] + [ANY] * (3 * begun),
            out_specs=[whole, send, block, block, pl.BlockSpec(memory_space=pltpu.SMEM)],
        ),
        out_shape=[shape(w), jax.ShapeDtypeStruct(alone, BF16), shape(m), shape(v), shape(me)],
        input_output_aliases={6: 0, 7: 2, 8: 3} if begun else {},
        compiler_params=pltpu.CompilerParams(vmem_limit_bytes=VMEM_BYTES),
        cost_estimate=pl.CostEstimate(flops=20 * steps * rows * cols, bytes_accessed=28 * steps * rows * cols, transcendentals=0),
        name="adamw",
    )(me, factor, g, w, m, v, *(so_far or ()))
    return (out, new_m, new_v), sent, turn


def place_kernel(n, at, me_ref, _, *refs):
    pieces, out, turn, bufs, sems = refs[:n], refs[n], refs[n + 1], refs[n + 2 : 2 * n + 2], refs[2 * n + 2]
    turn[0] = me_ref[0]
    loads = [pltpu.make_async_copy(p, b, sems.at[0, k]) for k, (p, b) in enumerate(zip(pieces, bufs))]
    for c in loads:
        c.start()
    stores = []
    for k in range(n):
        loads[k].wait()
        stores.append(pltpu.make_async_copy(bufs[k], out.at[at(k, me_ref[0])], sems.at[1, k]))
        stores[k].start()
    for c in stores:
        c.wait()


def place(out, me, pieces, owners, layer, first, by_columns):
    rows, cols = pieces[0].shape

    def at(k, me):
        owner = me ^ owners[k]
        if by_columns:
            return layer, pl.ds(pl.multiple_of(owner * rows, 8), rows), pl.ds(first * DEVICES * LANES, cols)
        return layer, pl.ds(pl.multiple_of(owner * (out.shape[1] // DEVICES) + first * LANES, LANES), rows), slice(None)

    n = len(pieces)
    return pl.pallas_call(
        functools.partial(place_kernel, n, at),
        in_specs=[pl.BlockSpec(memory_space=pltpu.SMEM)] + [ANY] * (n + 1),
        out_specs=[ANY, pl.BlockSpec(memory_space=pltpu.SMEM)],
        out_shape=[jax.ShapeDtypeStruct(out.shape, out.dtype), jax.ShapeDtypeStruct(me.shape, me.dtype)],
        scratch_shapes=[pltpu.VMEM((rows, cols), BF16)] * n + [pltpu.SemaphoreType.DMA((2, n))],
        input_output_aliases={1: 0},
        compiler_params=pltpu.CompilerParams(vmem_limit_bytes=VMEM_BYTES),
        cost_estimate=pl.CostEstimate(flops=4 * n * rows * cols, bytes_accessed=4 * n * rows * cols, transcendentals=0),
        name="place",
    )(me, out, *pieces)


def other_chip(a):
    return lax.ppermute(a, "dp", [(i, i ^ 2) for i in range(4)])


def other_core(a):
    return lax.ppermute(a, "dp", [(i, i ^ 1) for i in range(4)])


CHUNKS = (
    (0, 0, 0, 1), (0, 0, 1, 3), (0, 0, 4, 5), (0, 1, 0, 9), (1, 0, 0, 9), (1, 1, 0, 9), (2, 0, 0, 9), (2, 1, 0, 5), (2, 1, 5, 3), (2, 1, 8, 1),
)


def solution(mesh):
    def step(x, dy, *arrays):
        weights, m, v = (arrays[i : i + 3] for i in (0, 3, 6))
        me = lax.axis_index("dp").astype(jnp.int32).reshape(1)
        *g, factor = gradients(x[0], dy[0], *weights)
        new = [None] * 3
        gathered = []
        for k, layer, first, steps in CHUNKS:
            new[k], sent, me = adamw(me, factor, g[k], weights[k], m[k], v[k], new[k], layer, first, steps, k < 2)
            far = other_chip(sent)
            own = other_core(sent)
            gathered.append((far, own, other_core(far)))
        whole = [n[0] for n in new]
        for (k, layer, first, steps), pieces in zip(CHUNKS, gathered):
            whole[k], me = place(whole[k], me, pieces, (2, 1, 3), layer, first, k < 2)
        return (*whole, *(n[1] for n in new), *(n[2] for n in new))

    rows = P(None, "dp", None)
    return jax.shard_map(
        step,
        mesh=mesh,
        in_specs=(P(("rep", "dp")), P(("rep", "dp")), *(P(),) * 3, *(rows,) * 6),
        out_specs=(*(P("rep"),) * 3, *(P("rep", "dp"),) * 6),
        check_vma=False,
    )
```

profile of v0, /device:TPU:0, one launch (start us, length us, event | category | flops | bytes accessed | tf_op | source)
XLA Modules:
  0.0 1007.1 jit_solution(389188327896821041)
XLA Ops:
  0.6 527.1 %gradients.1 = (bf16[2,288,4608]{2,1,0:T(8,128)(2,1)}, bf16[2,288,4608]{2,1,0:T(8,128)(2,1)}, bf16[2,1152,1152]{2,1,0:T(8,128)(2,1)}, f32[8,128]{1,0:T(8,128)}, ...) custom-call(bf16[2048,1152]{1,0:T(8,128)(2,1)} %bitcast.3, ...), custom_call_target="tpu_custom_call" | custom-call | tf_op jit(solution)/shard_map/gradients/pallas_call | solution.py:478
  527.8 3.1 adamw.10
  531.3 7.0 adamw.11
  538.3 10.1 %adamw.12 = (bf16[2,1152,4608]{2,1,0:T(8,128)(2,1)}, bf16[288,2560]{1,0:T(8,128)(2,1)}, f32[2,288,4608]{2,1,0:T(8,128)}, f32[2,288,4608]{2,1,0:T(8,128)}, s32[1]{0:T(128)}) custom-call(s32[1]{0:T(128)} %get-tuple-element.88.me, f32[8,128]{1,0:T(8,128)} %get-tuple-element.82.factor, ...), custom_call_target="tpu_custom_call", output_to_operand_aliasing={{0}: (6, {}), {2}: (7, {}), {3}: (8, {})} | custom-call | flops 14745600 | bytes 20643840 | tf_op jit(solution)/shard_map/adamw/pallas_call | solution.py:526
  550.1 16.7 %adamw.13 = (bf16[2,1152,4608]{2,1,0:T(8,128)(2,1)}, bf16[288,4608]{1,0:T(8,128)(2,1)}, f32[2,288,4608]{2,1,0:T(8,128)}, f32[2,288,4608]{2,1,0:T(8,128)}, s32[1]{0:T(128)}) custom-call(s32[1]{0:T(128)} %get-tuple-element.92.me, f32[8,128]{1,0:T(8,128)} %get-tuple-element.82.factor, ...), custom_call_target="tpu_custom_call", output_to_operand_aliasing={{0}: (6, {}), {2}: (7, {}), {3}: (8, {})} | custom-call | flops 26542080 | bytes 37158912 | tf_op jit(solution)/shard_map/adamw/pallas_call | solution.py:526
  566.8 16.5 %adamw.14 = (bf16[2,1152,4608]{2,1,0:T(8,128)(2,1)}, bf16[288,4608]{1,0:T(8,128)(2,1)}, f32[2,288,4608]{2,1,0:T(8,128)}, f32[2,288,4608]{2,1,0:T(8,128)}, s32[1]{0:T(128)}) custom-call(s32[1]{0:T(128)} %get-tuple-element.96.me, f32[8,128]{1,0:T(8,128)} %get-tuple-element.82.factor, bf16[2,288,4608]{2,1,0:T(8,128)(2,1)} %get-tuple-element.97.g, ...), custom_call_target="tpu_custom_call" | custom-call | flops 26542080 | bytes 37158912 | tf_op jit(solution)/shard_map/adamw/pallas_call | solution.py:526
  583.3 16.5 %adamw.15 = (bf16[2,1152,4608]{2,1,0:T(8,128)(2,1)}, bf16[288,4608]{1,0:T(8,128)(2,1)}, f32[2,288,4608]{2,1,0:T(8,128)}, f32[2,288,4608]{2,1,0:T(8,128)}, s32[1]{0:T(128)}) custom-call(s32[1]{0:T(128)} %get-tuple-element.98.me, f32[8,128]{1,0:T(8,128)} %get-tuple-element.82.factor, ...), custom_call_target="tpu_custom_call", output_to_operand_aliasing={{0}: (6, {}), {2}: (7, {}), {3}: (8, {})} | custom-call | flops 26542080 | bytes 37158912 | tf_op jit(solution)/shard_map/adamw/pallas_call | solution.py:526
  599.8 16.4 %adamw.16 = (bf16[2,4608,1152]{2,1,0:T(8,128)(2,1)}, bf16[1152,1152]{1,0:T(8,128)(2,1)}, f32[2,1152,1152]{2,1,0:T(8,128)}, f32[2,1152,1152]{2,1,0:T(8,128)}, s32[1]{0:T(128)}) custom-call(s32[1]{0:T(128)} %get-tuple-element.102.me, f32[8,128]{1,0:T(8,128)} %get-tuple-element.82.factor, bf16[2,1152,1152]{2,1,0:T(8,128)(2,1)} %get-tuple-element.103.g, ...), custom_call_target="tpu_custom_call" | custom-call | flops 26542080 | bytes 37158912 | tf_op jit(solution)/shard_map/adamw/pallas_call | solution.py:526
  616.2 10.1 %adamw.17 = (bf16[2,4608,1152]{2,1,0:T(8,128)(2,1)}, bf16[640,1152]{1,0:T(8,128)(2,1)}, f32[2,1152,1152]{2,1,0:T(8,128)}, f32[2,1152,1152]{2,1,0:T(8,128)}, s32[1]{0:T(128)}) custom-call(s32[1]{0:T(128)} %get-tuple-element.104.me, f32[8,128]{1,0:T(8,128)} %get-tuple-element.82.factor, ...), custom_call_target="tpu_custom_call", output_to_operand_aliasing={{0}: (6, {}), {2}: (7, {}), {3}: (8, {})} | custom-call | flops 14745600 | bytes 20643840 | tf_op jit(solution)/shard_map/adamw/pallas_call | solution.py:526
  626.3 6.9 adamw.18
  633.3 3.7 adamw.19
  639.6 7.7 collective-permute-done.27.refs_0_
  647.7 18.4 %collective-permute-done.3.refs_0_ = bf16[288,1536]{1,0:T(8,128)(2,1)S(1)} collective-permute-done((bf16[288,1536]{1,0:T(8,128)(2,1)}, bf16[288,1536]{1,0:T(8,128)(2,1)S(1)}, u32[]{:S(2)}, u32[]{:S(2)}) %collective-permute-start.3) | collective-permute-done | bytes 884768 | tf_op jit(solution)/shard_map/ppermute | solution.py:582
  668.1 17.0 %collective-permute-done.24.refs_0_ = bf16[384,1152]{1,0:T(8,128)(2,1)} collective-permute-done((bf16[384,1152]{1,0:T(8,128)(2,1)}, bf16[384,1152]{1,0:T(8,128)(2,1)}, u32[]{:S(2)}, u32[]{:S(2)}) %collective-permute-start.24) | collective-permute-done | bytes 884768 | tf_op jit(solution)/shard_map/ppermute | solution.py:582
  685.8 31.0 %collective-permute-done.21.refs_0_ = bf16[640,1152]{1,0:T(8,128)(2,1)} collective-permute-done((bf16[640,1152]{1,0:T(8,128)(2,1)}, bf16[640,1152]{1,0:T(8,128)(2,1)}, u32[]{:S(2)}, u32[]{:S(2)}) %collective-permute-start.21) | collective-permute-done | bytes 1474592 | tf_op jit(solution)/shard_map/ppermute | solution.py:582
  717.3 1.9 collective-permute-done.5.refs_2_
  720.5 53.0 %collective-permute-done.9.refs_0_ = bf16[288,4608]{1,0:T(8,128)(2,1)S(1)} collective-permute-done((bf16[288,4608]{1,0:T(8,128)(2,1)}, bf16[288,4608]{1,0:T(8,128)(2,1)S(1)}, u32[]{:S(2)}, u32[]{:S(2)}) %collective-permute-start.9) | collective-permute-done | bytes 2654240 | tf_op jit(solution)/shard_map/ppermute | solution.py:582
  774.0 56.5 %collective-permute-done.12.refs_0_ = bf16[288,4608]{1,0:T(8,128)(2,1)S(1)} collective-permute-done((bf16[288,4608]{1,0:T(8,128)(2,1)}, bf16[288,4608]{1,0:T(8,128)(2,1)S(1)}, u32[]{:S(2)}, u32[]{:S(2)}) %collective-permute-start.12) | collective-permute-done | bytes 2654240 | tf_op jit(solution)/shard_map/ppermute | solution.py:582
  831.0 56.3 %collective-permute-done.15.refs_0_ = bf16[288,4608]{1,0:T(8,128)(2,1)S(1)} collective-permute-done((bf16[288,4608]{1,0:T(8,128)(2,1)}, bf16[288,4608]{1,0:T(8,128)(2,1)S(1)}, u32[]{:S(2)}, u32[]{:S(2)}) %collective-permute-start.15) | collective-permute-done | bytes 2654240 | tf_op jit(solution)/shard_map/ppermute | solution.py:582
  887.8 55.9 %collective-permute-done.18.refs_0_ = bf16[1152,1152]{1,0:T(8,128)(2,1)S(1)} collective-permute-done((bf16[1152,1152]{1,0:T(8,128)(2,1)}, bf16[1152,1152]{1,0:T(8,128)(2,1)S(1)}, u32[]{:S(2)}, u32[]{:S(2)}) %collective-permute-start.18) | collective-permute-done | bytes 2654240 | tf_op jit(solution)/shard_map/ppermute | solution.py:582
  944.9 3.8 collective-permute-done.17.refs_2_
  948.8 3.7 collective-permute-done.20.refs_2_
  954.0 3.1 place.10
  957.1 3.9 place.11
  961.0 4.7 place.12
  965.7 7.4 place.13
  973.1 7.4 place.14
  980.5 7.4 place.15
  987.9 7.4 place.16
  995.3 4.7 place.17
  1000.0 3.8 place.18
  1003.8 3.0 place.19
  (85 shorter events, 13.7 us)
Async XLA Ops:
  530.9 108.1 %collective-permute-start = (bf16[288,512]{1,0:T(8,128)(2,1)}, bf16[288,512]{1,0:T(8,128)(2,1)}, u32[]{:S(2)}, u32[]{:S(2)}) collective-permute-start(bf16[288,512]{1,0:T(8,128)(2,1)} %get-tuple-element.118), channel_id=1, source_target_pairs={{0,2},{1,3},{2,0},{3,1},{4,6},{5,7},{6,4},{7,5}} | collective-permute-start | bytes 884744 | tf_op jit(solution)/shard_map/ppermute | solution.py:582
  548.4 136.7 %collective-permute-start.6 = (bf16[288,2560]{1,0:T(8,128)(2,1)}, bf16[288,2560]{1,0:T(8,128)(2,1)}, u32[]{:S(2)}, u32[]{:S(2)}) collective-permute-start(bf16[288,2560]{1,0:T(8,128)(2,1)} %get-tuple-element.124), channel_id=1, source_target_pairs={{0,2},{1,3},{2,0},{3,1},{4,6},{5,7},{6,4},{7,5}} | collective-permute-start | bytes 4423688 | tf_op jit(solution)/shard_map/ppermute | solution.py:582
  550.1 89.0 %collective-permute-start.1 = (bf16[288,512]{1,0:T(8,128)(2,1)}, bf16[288,512]{1,0:T(8,128)(2,1)}, u32[]{:S(2)}, u32[]{:S(2)}) collective-permute-start(bf16[288,512]{1,0:T(8,128)(2,1)} %get-tuple-element.118), channel_id=1, source_target_pairs={{0,1},{1,0},{2,3},{3,2},{4,5},{5,4},{6,7},{7,6}} | collective-permute-start | bytes 884744 | tf_op jit(solution)/shard_map/ppermute | solution.py:586
  637.0 10.2 %collective-permute-start.27 = (bf16[128,1152]{1,0:T(8,128)(2,1)}, bf16[128,1152]{1,0:T(8,128)(2,1)}, u32[]{:S(2)}, u32[]{:S(2)}) collective-permute-start(bf16[128,1152]{1,0:T(8,128)(2,1)} %get-tuple-element.147), channel_id=1, source_target_pairs={{0,2},{1,3},{2,0},{3,1},{4,6},{5,7},{6,4},{7,5}} | collective-permute-start | bytes 884744 | tf_op jit(solution)/shard_map/ppermute | solution.py:582
  637.4 28.7 %collective-permute-start.3 = (bf16[288,1536]{1,0:T(8,128)(2,1)}, bf16[288,1536]{1,0:T(8,128)(2,1)S(1)}, u32[]{:S(2)}, u32[]{:S(2)}) collective-permute-start(bf16[288,1536]{1,0:T(8,128)(2,1)} %get-tuple-element.121), channel_id=1, source_target_pairs={{0,2},{1,3},{2,0},{3,1},{4,6},{5,7},{6,4},{7,5}} | collective-permute-start | bytes 2654216 | tf_op jit(solution)/shard_map/ppermute | solution.py:582
  639.1 8.2 collective-permute-start.2
  639.1 27.4 %collective-permute-start.4 = (bf16[288,1536]{1,0:T(8,128)(2,1)}, bf16[288,1536]{1,0:T(8,128)(2,1)S(1)}, u32[]{:S(2)}, u32[]{:S(2)}) collective-permute-start(bf16[288,1536]{1,0:T(8,128)(2,1)} %get-tuple-element.121), channel_id=1, source_target_pairs={{0,1},{1,0},{2,3},{3,2},{4,5},{5,4},{6,7},{7,6}} | collective-permute-start | bytes 2654216 | tf_op jit(solution)/shard_map/ppermute | solution.py:586
  647.2 38.3 %collective-permute-start.7 = (bf16[288,2560]{1,0:T(8,128)(2,1)}, bf16[288,2560]{1,0:T(8,128)(2,1)S(1)}, u32[]{:S(2)}, u32[]{:S(2)}) collective-permute-start(bf16[288,2560]{1,0:T(8,128)(2,1)} %get-tuple-element.124), channel_id=1, source_target_pairs={{0,1},{1,0},{2,3},{3,2},{4,5},{5,4},{6,7},{7,6}} | collective-permute-start | bytes 4423688 | tf_op jit(solution)/shard_map/ppermute | solution.py:586
  647.3 37.9 %collective-permute-start.24 = (bf16[384,1152]{1,0:T(8,128)(2,1)}, bf16[384,1152]{1,0:T(8,128)(2,1)}, u32[]{:S(2)}, u32[]{:S(2)}) collective-permute-start(bf16[384,1152]{1,0:T(8,128)(2,1)} %get-tuple-element.144), channel_id=1, source_target_pairs={{0,2},{1,3},{2,0},{3,1},{4,6},{5,7},{6,4},{7,5}} | collective-permute-start | bytes 2654216 | tf_op jit(solution)/shard_map/ppermute | solution.py:582
  666.1 50.7 %collective-permute-start.21 = (bf16[640,1152]{1,0:T(8,128)(2,1)}, bf16[640,1152]{1,0:T(8,128)(2,1)}, u32[]{:S(2)}, u32[]{:S(2)}) collective-permute-start(bf16[640,1152]{1,0:T(8,128)(2,1)} %get-tuple-element.141), channel_id=1, source_target_pairs={{0,2},{1,3},{2,0},{3,1},{4,6},{5,7},{6,4},{7,5}} | collective-permute-start | bytes 4423688 | tf_op jit(solution)/shard_map/ppermute | solution.py:582
  666.5 107.1 %collective-permute-start.9 = (bf16[288,4608]{1,0:T(8,128)(2,1)}, bf16[288,4608]{1,0:T(8,128)(2,1)S(1)}, u32[]{:S(2)}, u32[]{:S(2)}) collective-permute-start(bf16[288,4608]{1,0:T(8,128)(2,1)} %get-tuple-element.127), channel_id=1, source_target_pairs={{0,2},{1,3},{2,0},{3,1},{4,6},{5,7},{6,4},{7,5}} | collective-permute-start | bytes 7962632 | tf_op jit(solution)/shard_map/ppermute | solution.py:582
  685.2 88.4 %collective-permute-start.10 = (bf16[288,4608]{1,0:T(8,128)(2,1)}, bf16[288,4608]{1,0:T(8,128)(2,1)S(1)}, u32[]{:S(2)}, u32[]{:S(2)}) collective-permute-start(bf16[288,4608]{1,0:T(8,128)(2,1)} %get-tuple-element.127), channel_id=1, source_target_pairs={{0,1},{1,0},{2,3},{3,2},{4,5},{5,4},{6,7},{7,6}} | collective-permute-start | bytes 7962632 | tf_op jit(solution)/shard_map/ppermute | solution.py:586
  685.2 145.2 %collective-permute-start.12 = (bf16[288,4608]{1,0:T(8,128)(2,1)}, bf16[288,4608]{1,0:T(8,128)(2,1)S(1)}, u32[]{:S(2)}, u32[]{:S(2)}) collective-permute-start(bf16[288,4608]{1,0:T(8,128)(2,1)} %get-tuple-element.131), channel_id=1, source_target_pairs={{0,2},{1,3},{2,0},{3,1},{4,6},{5,7},{6,4},{7,5}} | collective-permute-start | bytes 7962632 | tf_op jit(solution)/shard_map/ppermute | solution.py:582
  685.6 31.2 %collective-permute-start.22 = (bf16[640,1152]{1,0:T(8,128)(2,1)}, bf16[640,1152]{1,0:T(8,128)(2,1)}, u32[]{:S(2)}, u32[]{:S(2)}) collective-permute-start(bf16[640,1152]{1,0:T(8,128)(2,1)} %get-tuple-element.141), channel_id=1, source_target_pairs={{0,1},{1,0},{2,3},{3,2},{4,5},{5,4},{6,7},{7,6}} | collective-permute-start | bytes 4423688 | tf_op jit(solution)/shard_map/ppermute | solution.py:586
  716.8 2.4 collective-permute-start.5
  716.8 113.6 %collective-permute-start.13 = (bf16[288,4608]{1,0:T(8,128)(2,1)}, bf16[288,4608]{1,0:T(8,128)(2,1)S(1)}, u32[]{:S(2)}, u32[]{:S(2)}) collective-permute-start(bf16[288,4608]{1,0:T(8,128)(2,1)} %get-tuple-element.131), channel_id=1, source_target_pairs={{0,1},{1,0},{2,3},{3,2},{4,5},{5,4},{6,7},{7,6}} | collective-permute-start | bytes 7962632 | tf_op jit(solution)/shard_map/ppermute | solution.py:586
  720.1 167.2 %collective-permute-start.15 = (bf16[288,4608]{1,0:T(8,128)(2,1)}, bf16[288,4608]{1,0:T(8,128)(2,1)S(1)}, u32[]{:S(2)}, u32[]{:S(2)}) collective-permute-start(bf16[288,4608]{1,0:T(8,128)(2,1)} %get-tuple-element.134), channel_id=1, source_target_pairs={{0,2},{1,3},{2,0},{3,1},{4,6},{5,7},{6,4},{7,5}} | collective-permute-start | bytes 7962632 | tf_op jit(solution)/shard_map/ppermute | solution.py:582
  773.5 113.8 %collective-permute-start.16 = (bf16[288,4608]{1,0:T(8,128)(2,1)}, bf16[288,4608]{1,0:T(8,128)(2,1)S(1)}, u32[]{:S(2)}, u32[]{:S(2)}) collective-permute-start(bf16[288,4608]{1,0:T(8,128)(2,1)} %get-tuple-element.134), channel_id=1, source_target_pairs={{0,1},{1,0},{2,3},{3,2},{4,5},{5,4},{6,7},{7,6}} | collective-permute-start | bytes 7962632 | tf_op jit(solution)/shard_map/ppermute | solution.py:586
  773.5 170.7 %copy-start.1 = (bf16[288,4608]{1,0:T(8,128)(2,1)}, bf16[288,4608]{1,0:T(8,128)(2,1)S(1)}, u32[]{:S(2)}) copy-start(bf16[288,4608]{1,0:T(8,128)(2,1)S(1)} %collective-permute-done.10.refs_1_) | copy-start | bytes 7962628
  773.6 170.2 %collective-permute-start.18 = (bf16[1152,1152]{1,0:T(8,128)(2,1)}, bf16[1152,1152]{1,0:T(8,128)(2,1)S(1)}, u32[]{:S(2)}, u32[]{:S(2)}) collective-permute-start(bf16[1152,1152]{1,0:T(8,128)(2,1)} %get-tuple-element.138), channel_id=1, source_target_pairs={{0,2},{1,3},{2,0},{3,1},{4,6},{5,7},{6,4},{7,5}} | collective-permute-start | bytes 7962632 | tf_op jit(solution)/shard_map/ppermute | solution.py:582
  830.4 114.4 %copy-start.2 = (bf16[288,4608]{1,0:T(8,128)(2,1)}, bf16[288,4608]{1,0:T(8,128)(2,1)S(1)}, u32[]{:S(2)}) copy-start(bf16[288,4608]{1,0:T(8,128)(2,1)S(1)} %collective-permute-done.12.refs_0_) | copy-start | bytes 7962628
  830.4 113.3 %collective-permute-start.19 = (bf16[1152,1152]{1,0:T(8,128)(2,1)}, bf16[1152,1152]{1,0:T(8,128)(2,1)S(1)}, u32[]{:S(2)}, u32[]{:S(2)}) collective-permute-start(bf16[1152,1152]{1,0:T(8,128)(2,1)} %get-tuple-element.138), channel_id=1, source_target_pairs={{0,1},{1,0},{2,3},{3,2},{4,5},{5,4},{6,7},{7,6}} | collective-permute-start | bytes 7962632 | tf_op jit(solution)/shard_map/ppermute | solution.py:586
  830.4 113.8 %collective-permute-start.11 = (bf16[288,4608]{1,0:T(8,128)(2,1)S(1)}, bf16[288,4608]{1,0:T(8,128)(2,1)S(1)}, u32[]{:S(2)}, u32[]{:S(2)}) collective-permute-start(bf16[288,4608]{1,0:T(8,128)(2,1)S(1)} %collective-permute-done.9.refs_0_), channel_id=1, source_target_pairs={{0,1},{1,0},{2,3},{3,2},{4,5},{5,4},{6,7},{7,6}} | collective-permute-start | bytes 7962632 | tf_op jit(solution)/shard_map/ppermute | solution.py:586
  887.3 57.5 %collective-permute-start.14 = (bf16[288,4608]{1,0:T(8,128)(2,1)S(1)}, bf16[288,4608]{1,0:T(8,128)(2,1)S(1)}, u32[]{:S(2)}, u32[]{:S(2)}) collective-permute-start(bf16[288,4608]{1,0:T(8,128)(2,1)S(1)} %collective-permute-done.12.refs_0_), channel_id=1, source_target_pairs={{0,1},{1,0},{2,3},{3,2},{4,5},{5,4},{6,7},{7,6}} | collective-permute-start | bytes 7962632 | tf_op jit(solution)/shard_map/ppermute | solution.py:586
  887.3 56.9 %collective-permute-start.8 = (bf16[288,2560]{1,0:T(8,128)(2,1)}, bf16[288,2560]{1,0:T(8,128)(2,1)S(1)}, u32[]{:S(2)}, u32[]{:S(2)}) collective-permute-start(bf16[288,2560]{1,0:T(8,128)(2,1)} %collective-permute-done.6.refs_0_), channel_id=1, source_target_pairs={{0,1},{1,0},{2,3},{3,2},{4,5},{5,4},{6,7},{7,6}} | collective-permute-start | bytes 4423688 | tf_op jit(solution)/shard_map/ppermute | solution.py:586
  943.7 5.0 collective-permute-start.17
  943.7 8.7 collective-permute-start.20
  944.2 51.1 %collective-permute-start.23 = (bf16[640,1152]{1,0:T(8,128)(2,1)}, bf16[640,1152]{1,0:T(8,128)(2,1)}, u32[]{:S(2)}, u32[]{:S(2)}) collective-permute-start(bf16[640,1152]{1,0:T(8,128)(2,1)} %collective-permute-done.21.refs_0_), channel_id=1, source_target_pairs={{0,1},{1,0},{2,3},{3,2},{4,5},{5,4},{6,7},{7,6}} | collective-permute-start | bytes 4423688 | tf_op jit(solution)/shard_map/ppermute | solution.py:586
  944.3 55.7 %collective-permute-start.25 = (bf16[384,1152]{1,0:T(8,128)(2,1)}, bf16[384,1152]{1,0:T(8,128)(2,1)}, u32[]{:S(2)}, u32[]{:S(2)}) collective-permute-start(bf16[384,1152]{1,0:T(8,128)(2,1)} %get-tuple-element.144), channel_id=1, source_target_pairs={{0,1},{1,0},{2,3},{3,2},{4,5},{5,4},{6,7},{7,6}} | collective-permute-start | bytes 2654216 | tf_op jit(solution)/shard_map/ppermute | solution.py:586
  944.8 55.2 %collective-permute-start.26 = (bf16[384,1152]{1,0:T(8,128)(2,1)}, bf16[384,1152]{1,0:T(8,128)(2,1)}, u32[]{:S(2)}, u32[]{:S(2)}) collective-permute-start(bf16[384,1152]{1,0:T(8,128)(2,1)} %collective-permute-done.24.refs_0_), channel_id=1, source_target_pairs={{0,1},{1,0},{2,3},{3,2},{4,5},{5,4},{6,7},{7,6}} | collective-permute-start | bytes 2654216 | tf_op jit(solution)/shard_map/ppermute | solution.py:586
  948.7 55.1 %collective-permute-start.28 = (bf16[128,1152]{1,0:T(8,128)(2,1)}, bf16[128,1152]{1,0:T(8,128)(2,1)}, u32[]{:S(2)}, u32[]{:S(2)}) collective-permute-start(bf16[128,1152]{1,0:T(8,128)(2,1)} %get-tuple-element.147), channel_id=1, source_target_pairs={{0,1},{1,0},{2,3},{3,2},{4,5},{5,4},{6,7},{7,6}} | collective-permute-start | bytes 884744 | tf_op jit(solution)/shard_map/ppermute | solution.py:586
  952.5 51.4 %collective-permute-start.29 = (bf16[128,1152]{1,0:T(8,128)(2,1)}, bf16[128,1152]{1,0:T(8,128)(2,1)}, u32[]{:S(2)}, u32[]{:S(2)}) collective-permute-start(bf16[128,1152]{1,0:T(8,128)(2,1)} %collective-permute-done.27.refs_0_), channel_id=1, source_target_pairs={{0,1},{1,0},{2,3},{3,2},{4,5},{5,4},{6,7},{7,6}} | collective-permute-start | bytes 884744 | tf_op jit(solution)/shard_map/ppermute | solution.py:586
  (16 other events, 539.1 us)
where the time goes:
time: 1010 us
  Pallas kernels  687 us (68%)
  waiting for transfers between devices  305 us (30%)
  starting transfers between devices  11.3 us (1%)
    pallas_call x1, Pallas kernels, gradients(): pl.pallas_call(grads_kernel, out_shape=outs, in_specs=[ANY] * 5, out_spec...  527 us
    ppermute x10, waiting for transfers between devices, other_chip(): return lax.ppermute(a, 'dp', [(i, i ^ 2) for i in range(4)])  296 us
    pallas_call x10, Pallas kernels, adamw(): pl.pallas_call(adamw_kernel, grid_spec=pltpu.PrefetchScalarGridSpec(num_s...  107 us
    pallas_call x10, Pallas kernels, place(): pl.pallas_call(functools.partial(place_kernel, n, at), in_specs=[pl.Block...  52.7 us
  transfers between devices with their start and end apart: 30, of which 11 were waited for; matrix products, arithmetic and copies ran while one was open for 0% of the time, Pallas kernels for 15%

commit v1 on v0

v1 whole, which is shorter than its diff:
```python
import functools

import jax
import jax.numpy as jnp
from jax import lax
from jax.experimental import pallas as pl
from jax.experimental.pallas import tpu as pltpu
from jax.sharding import PartitionSpec as P


F32, BF16 = jnp.float32, jnp.bfloat16
DEVICES = 4
LANES = 128
CHUNK = 256
ANY = pl.BlockSpec(memory_space=pl.ANY)
VMEM_BYTES = 67_043_328


def dot(a, b, dims):
    return lax.dot_general(a, b, (dims, ((), ())), preferred_element_type=F32)


NN, NT, TT = ((1,), (0,)), ((1,), (1,)), ((0,), (1,))


def sigmoid(x):
    return 1.0 / (1.0 + jnp.exp(-x))


def loop(n, body):
    lax.fori_loop(0, n, lambda i, c: (body(i), c)[1], 0)


def apart(cond, body):
    lax.fori_loop(0, jnp.where(cond, 1, 0), lambda i, c: (body(), c)[1], 0)


def grads_kernel(
    x, dy, wg, wu, wd,
    gg, gu, gd, factor, gate_s, up_s, a0t_s, ht_s, mate, own, far, cross,
    A, AT, DD, DT, ACC, GR, ACT, DG, DU, WG, WU, WD, G0, U0, D0, G1, U1, D1, MATEB, FB, SQ, SQS,
    wsem, iosem, d2d_send, d2d_recv, near_recv, free, own_sem, far_sem, x_send, x_recv, fsem, sq_send, sq_recv,
):
    T, D = x.shape
    F = wg.shape[2]
    W = DEVICES * LANES
    NT_ = F // W
    FAR, NEAR = 0, 1
    H = T // 2
    R = D // DEVICES
    me = lax.axis_index("dp")
    chip, core = me // 2, me % 2
    mate_id, cross_id = {"dp": chip * 2 + 1 - core}, {"dp": (1 - chip) * 2 + core}
    lo, hi = pl.ds(0, H), pl.ds(H, H)

    barrier = pltpu.get_barrier_semaphore()
    for k in range(1, DEVICES):
        pl.semaphore_signal(barrier, inc=1, device_id={"dp": (me + k) % DEVICES}, device_id_type=pl.DeviceIdType.MESH)

    def columns(p, j):
        return pl.ds(pl.multiple_of(p * (F // DEVICES) + j * LANES, LANES), LANES)

    def weights(l, j, q, down_only=False):
        slot = q % 2
        copies = []
        for p in range(DEVICES):
            piece = pl.ds(p * LANES, LANES)
            if not down_only:
                copies.append(pltpu.make_async_copy(wg.at[l, :, columns(p, j)], WG.at[slot, :, piece], wsem.at[slot, 0, p]))
                copies.append(pltpu.make_async_copy(wu.at[l, :, columns(p, j)], WU.at[slot, :, piece], wsem.at[slot, 1, p]))
            copies.append(pltpu.make_async_copy(wd.at[l, columns(p, j), :], WD.at[slot, piece, :], wsem.at[slot, 2, p]))
        return copies

    def start(copies):
        for c in copies:
            c.start()

    def wait(copies):
        for c in copies:
            c.wait()

    def owner_chip(side):
        return 1 - chip if side == FAR else chip

    def d2d(t, side):
        return pltpu.make_async_remote_copy(
            src_ref=GR.at[:, owner_chip(side), 1 - core], dst_ref=MATEB if side == FAR else mate.at[t],
            send_sem=d2d_send.at[side], recv_sem=d2d_recv if side == FAR else near_recv.at[t],
            device_id=mate_id, device_id_type=pl.DeviceIdType.MESH)

    def keep(t):
        return pltpu.make_async_copy(GR.at[:, chip, core], own.at[t], own_sem)

    def across(t, direct):
        return pltpu.make_async_remote_copy(
            src_ref=FB.at[t % 2] if direct else far.at[t], dst_ref=cross.at[t], send_sem=x_send.at[t], recv_sem=x_recv.at[t],
            device_id=cross_id, device_id_type=pl.DeviceIdType.MESH)

    def far_store(t):
        return pltpu.make_async_copy(FB.at[t % 2], far.at[t], far_sem)

    def send_far(t):
        pl.when(t > 0)(lambda: pl.semaphore_wait(free, 1))
        d2d(t, FAR).start()

    def far_sum(t):
        d2d(t, FAR).wait_recv()

        def some(i):
            rows = pl.ds(pl.multiple_of(i * 96, 96), 96)
            for k in range(3):
                FB[t % 2, k, rows, :] = (GR[k, 1 - chip, core, rows, :].astype(F32) + MATEB[k, rows, :].astype(F32)).astype(BF16)

        loop(R // 96, some)
        pl.semaphore_signal(free, inc=1, device_id=mate_id, device_id_type=pl.DeviceIdType.MESH)

    def sent(t):
        d2d(t, FAR).wait_send()
        d2d(t, NEAR).wait_send()
        keep(t).wait()

    def put(k, h, value, first=0):
        value = value.astype(BF16)
        for o in range(2):
            if k < 2:
                GR[k, h, o] = value[o * R : (o + 1) * R]
            else:
                for q in range(value.shape[0] // R):
                    lanes = slice((first + q) * LANES, (first + q + 1) * LANES)
                    GR[k, h, o, :, lanes] = value[q * R : (q + 1) * R, o * LANES : (o + 1) * LANES]

    def side_of(i):
        return jnp.where(i == 0, 1 - chip, chip)

    def hidden_of(h):
        return pl.ds(pl.multiple_of(h * (W // 2), W // 2), W // 2)

    def half_of(i):
        return pl.ds(pl.multiple_of(i * (D // 2), D // 2), D // 2)

    def product_back(g_ref, u_ref, d_ref, r0):
        step = 16
        for r in range(0, H, step):
            g, u = g_ref(r, step), u_ref(r, step)
            d = d_ref[r : r + step, :].astype(F32)
            s = sigmoid(g)
            si = g * s
            ACT[r0 + r : r0 + r + step, :] = (si * u).astype(BF16)
            DU[r0 + r : r0 + r + step, :] = (d * si).astype(BF16)
            DG[r0 + r : r0 + r + step, :] = (d * u * (s + si * (1.0 - s))).astype(BF16)

    def columns_of(i):
        return pl.ds(pl.multiple_of(i * CHUNK, CHUNK), CHUNK)

    def down_rows(step, body):
        for r in range(0, D, step):
            body(slice(r, r + step))

    def folded(t):
        return jnp.sum(t.reshape(t.shape[0] // 8, 8, t.shape[1]), axis=0)

    def turn(src, rows, dst):
        for c in range(0, T, 2 * LANES):
            dst[rows, c : c + 2 * LANES] = src[c : c + 2 * LANES, rows].T

    def loads(j):
        return [
            pltpu.make_async_copy(to.at[j, pl.ds(half * H, H), :], ref, iosem.at[3 + 2 * half + n])
            for half, refs in enumerate(((G0, U0), (G1, U1)))
            for n, (ref, to) in enumerate(zip(refs, (gate_s, up_s)))
        ]

    def load_h(HB, i):
        return pltpu.make_async_copy(ht_s.at[i], HB.at[i % 2], iosem.at[1 + i % 2])

    load_a0t = pltpu.make_async_copy(a0t_s, AT, iosem.at[0])

    def norm_back(HB):
        n = T // CHUNK

        def part(i):
            r = columns_of(i)
            slot = i % 2
            load_h(HB, i).wait()

            squares, along = [], []

            def add(rows):
                wide = HB[slot, rows, :].astype(F32)
                squares.append(folded(wide * wide))
                along.append(folded(ACC[rows, r].astype(BF16).astype(F32) * wide))

            down_rows(64, add)
            scale = lax.rsqrt(jnp.sum(sum(squares), axis=0, keepdims=True) / D + 1e-6)
            shrink = jnp.sum(sum(along), axis=0, keepdims=True) / D * (scale * scale * scale)

            def back(rows):
                wide = HB[slot, rows, :].astype(F32)
                dwide = ACC[rows, r].astype(BF16).astype(F32) * scale - wide * shrink
                dh = (DT[rows, r].astype(F32) + dwide.astype(BF16).astype(F32)).astype(BF16)
                DT[rows, r] = dh
                DD[r, rows] = dh.T

            down_rows(LANES, back)
            apart(i < n - 2, lambda: load_h(HB, i + 2).start())

        loop(n, part)
        sent(NT_ - 1)
        load_a0t.start()

    def first_half():
        S = ((G0, U0, D0), (G1, U1, D1))

        def forward(TB):
            load_x = [pltpu.make_async_copy(x.at[pl.ds(c * (T // 4), T // 4)], DD.at[pl.ds(c * (T // 4), T // 4)], iosem.at[c]) for c in range(4)]
            start(load_x)
            start(weights(0, 0, 0))

            def zero(i):
                ACC[pl.ds(pl.multiple_of(i * LANES, LANES), LANES), :] = jnp.zeros((LANES, T), F32)

            loop(D // LANES, zero)

            def norm_x(i):
                r = pl.ds(pl.multiple_of(i * LANES, LANES), LANES)
                wide = DD[r, :].astype(F32)
                A[r, :] = (wide * lax.rsqrt(jnp.mean(wide * wide, axis=1, keepdims=True) + 1e-6)).astype(BF16)
                AT[:, r] = DD[r, :].T

            for c in range(4):
                load_x[c].wait()
                loop(T // 4 // LANES, lambda i, c=c: norm_x(c * (T // 4 // LANES) + i))
            load_dy = pltpu.make_async_copy(dy, DD, iosem.at[6])
            load_dy.start()

            def stores(j, half):
                return [
                    pltpu.make_async_copy(ref, to.at[j, pl.ds(half * H, H), :], iosem.at[2 * half + n])
                    for n, (ref, to) in enumerate(zip(S[half][:2], (gate_s, up_s)))
                ]

            def save(j):
                return pltpu.make_async_copy(TB.at[j % 2], a0t_s.at[pl.ds(pl.multiple_of(j * LANES, LANES), LANES), :], iosem.at[4 + j % 2])

            def projections(half, slot):
                rows = lo if half == 0 else hi
                S[half][0][...] = dot(A[rows, :], WG[slot], NN)
                S[half][1][...] = dot(A[rows, :], WU[slot], NN)

            def product(half):
                g_ref, u_ref, _ = S[half]
                for r in range(0, H, 16):
                    g = g_ref[r : r + 16, :]
                    ACT[half * H + r : half * H + r + 16, :] = (g * sigmoid(g) * u_ref[r : r + 16, :]).astype(BF16)

            def down(rows, slot):
                ACC[:, rows] += dot(WD[slot], ACT[rows, :], TT)

            def tile(j):
                slot = j % 2
                some = pl.ds(pl.multiple_of(j * LANES, LANES), LANES)
                wait(weights(0, j, j))

                @pl.when(j < NT_ - 1)
                def _():
                    start(weights(0, j + 1, j + 1))

                @pl.when(j == NT_ - 1)
                def _():
                    start(weights(1, 0, NT_))

                @pl.when(j > 0)
                def _():
                    wait(stores(j - 1, 0) + stores(j - 1, 1))

                @pl.when(j > 1)
                def _():
                    save(j - 2).wait()

                projections(0, slot)
                for c in range(0, T, 2 * LANES):
                    TB[slot, :, c : c + 2 * LANES] = A[c : c + 2 * LANES, some].T
                start(stores(j, 0))
                save(j).start()
                projections(1, slot)
                product(0)
                start(stores(j, 1))

                @pl.when(j == 0)
                def _():
                    load_dy.wait()

                down(lo, slot)
                product(1)
                turn(DD, some, DT)
                down(hi, slot)

            loop(NT_, tile)
            wait(stores(NT_ - 1, 0) + stores(NT_ - 1, 1))
            save(NT_ - 2).wait()
            save(NT_ - 1).wait()

        pl.run_scoped(forward, pltpu.VMEM((2, LANES, T), BF16))

        def norm_h(HB):
            n = T // CHUNK

            def save(i):
                return pltpu.make_async_copy(HB.at[i % 2], ht_s.at[i], iosem.at[i % 2])

            def part(i):
                r = columns_of(i)
                slot = i % 2

                @pl.when(i > 1)
                def _():
                    save(i - 2).wait()

                squares = []

                def add(rows):
                    h = (AT[rows, r].astype(F32) + ACC[rows, r].astype(BF16).astype(F32)).astype(BF16)
                    HB[slot, rows, :] = h
                    ACC[rows, r] = jnp.zeros((h.shape[0], CHUNK), F32)
                    wide = h.astype(F32)
                    squares.append(folded(wide * wide))

                down_rows(64, add)
                save(i).start()
                scale = lax.rsqrt(jnp.sum(sum(squares), axis=0, keepdims=True) / D + 1e-6)

                def norm(rows):
                    a = (HB[slot, rows, :].astype(F32) * scale).astype(BF16)
                    AT[rows, r] = a
                    A[r, rows] = a.T

                down_rows(LANES, norm)

            loop(n, part)
            save(n - 2).wait()
            save(n - 1).wait()

        pl.run_scoped(norm_h, pltpu.VMEM((2, D, CHUNK), BF16))
        pl.semaphore_wait(barrier, DEVICES - 1)

        def layer1(HB):
            def projections(half, slot):
                rows = lo if half == 0 else hi
                S[half][0][...] = dot(A[rows, :], WG[slot], NN)
                S[half][1][...] = dot(A[rows, :], WU[slot], NN)
                S[half][2][...] = dot(DD[rows, :], WD[slot], NT).astype(BF16)

            def back(half):
                g_ref, u_ref, d_ref = S[half]
                product_back(lambda r, n: g_ref[r : r + n, :], lambda r, n: u_ref[r : r + n, :], d_ref, half * H)

            def da(rows, slot):
                ACC[:, rows] += dot(WG[slot], DG[rows, :], NT)
                ACC[:, rows] += dot(WU[slot], DU[rows, :], NT)

            def tile(j):
                slot = (NT_ + j) % 2
                wait(weights(1, j, NT_ + j))

                @pl.when(j < NT_ - 1)
                def _():
                    start(weights(1, j + 1, NT_ + j + 1))

                @pl.when(j == NT_ - 1)
                def _():
                    start(weights(0, 0, 2 * NT_, True))

                projections(0, slot)
                projections(1, slot)
                back(0)
                apart(j > 0, lambda: sent(j - 1))
                da(lo, slot)
                back(1)
                da(hi, slot)
                apart(j == NT_ - 1, lambda: start([load_h(HB, 0), load_h(HB, 1), *loads(0)]))

                def gradients(i):
                    h = side_of(i)
                    for q in (0, 2):
                        put(2, h, dot(DT[q * R : (q + 2) * R, :], ACT[:, hidden_of(h)], NN), q)
                    for k, rhs in ((0, DG), (1, DU)):
                        put(k, h, dot(AT[half_of(h), :], rhs[...], NN))
                    apart(i == 0, lambda: send_far(j))

                loop(2, gradients)
                d2d(j, NEAR).start()
                keep(j).start()
                apart(j > 1, lambda: across(j - 2, True).wait_send())
                far_sum(j)
                across(j, True).start()

            loop(NT_, tile)
            norm_back(HB)

        pl.run_scoped(layer1, pltpu.VMEM((2, D, CHUNK), BF16))

    first_half()

    def layer0():
        S = ((G0, U0, D0), (G1, U1, D1))

        def tile(j):
            t = NT_ + j
            slot = j % 2
            half_sum = pl.ds(0, W)

            def back(half):
                g_ref, u_ref, d_ref = S[half]
                product_back(lambda r, n: g_ref[r : r + n, :], lambda r, n: u_ref[r : r + n, :], d_ref, half * H)

            wait(weights(0, j, 2 * NT_ + j, True))

            @pl.when(j < NT_ - 1)
            def _():
                start(weights(0, j + 1, 2 * NT_ + j + 1, True))

            wait(loads(j))
            D0[...] = dot(DD[lo, :], WD[slot], NT).astype(BF16)
            D1[...] = dot(DD[hi, :], WD[slot], NT).astype(BF16)
            back(0)
            ACC[:, half_sum] = dot(DT[:, lo], ACT[lo, :], NN)
            back(1)
            apart(j < NT_ - 1, lambda: start(loads(j + 1)))
            apart(j == 0, lambda: load_a0t.wait())
            apart(j > 0, lambda: sent(t - 1))

            def gradients(i):
                h = side_of(i)
                for q in (0, 2):
                    rows = slice(q * R, (q + 2) * R)
                    put(2, h, ACC[rows, hidden_of(h)] + dot(DT[rows, hi], ACT[hi, hidden_of(h)], NN), q)
                for k, rhs in ((0, DG), (1, DU)):
                    put(k, h, dot(AT[half_of(h), :], rhs[...], NN))
                apart((j > 1) & (i == 0), lambda: (far_store(t - 1).wait(), across(t - 1, False).start()))
                apart(i == 0, lambda: send_far(t))

            loop(2, gradients)
            d2d(t, NEAR).start()
            keep(t).start()
            apart(j < 3, lambda: across(t - 2, True).wait_send())
            far_sum(t)
            apart(j == 0, lambda: across(t, True).start())
            apart(j > 0, lambda: far_store(t).start())

        loop(NT_, tile)

    layer0()

    last = 2 * NT_ - 1
    far_store(last).wait()
    across(last, False).start()
    sent(last)
    pl.semaphore_wait(free, 1)

    def finish(DN):
        GN, UN, CB = GR.at[0, 1, 0], GR.at[0, 1, 1], GR.at[:, 0, 0]
        SQ[...] = jnp.zeros_like(SQ)

        def outs(t):
            l, j = 1 - t // NT_, t % NT_
            copies = []
            for p in range(DEVICES):
                copies.append(pltpu.make_async_copy(GN.at[:, pl.ds(p * LANES, LANES)], gg.at[l, :, columns(p, j)], fsem.at[3 + p]))
                copies.append(pltpu.make_async_copy(UN.at[:, pl.ds(p * LANES, LANES)], gu.at[l, :, columns(p, j)], fsem.at[7 + p]))
            rows = pl.ds(pl.multiple_of(j * LANES, LANES), LANES)
            copies.append(pltpu.make_async_copy(DN, gd.at[l, rows, :], fsem.at[11]))
            return copies

        def one(t):
            ins = [
                pltpu.make_async_copy(own.at[t], FB.at[0], fsem.at[0]),
                pltpu.make_async_copy(mate.at[t], FB.at[1], fsem.at[1]),
                pltpu.make_async_copy(cross.at[t], CB, fsem.at[2]),
            ]
            d2d(t, NEAR).wait_recv()
            start(ins[:2])
            across(t, False).wait_recv()
            ins[2].start()
            apart(t > NT_, lambda: across(t, False).wait_send())

            @pl.when(t > 0)
            def _():
                wait(outs(t - 1))

            wait(ins)
            for k in range(3):
                total = FB[0, k].astype(F32) + FB[1, k].astype(F32) + CB[k].astype(F32)
                g = total.astype(BF16)
                wide = g.astype(F32)
                SQ[...] += jnp.sum((wide * wide).reshape(R // 8, 8, W), axis=0)
                if k == 0:
                    GN[...] = g
                elif k == 1:
                    UN[...] = g
                else:
                    tall = jnp.concatenate([g[:, q * LANES : (q + 1) * LANES] for q in range(DEVICES)], axis=0)
                    DN[...] = tall.T
            start(outs(t))

        loop(2 * NT_, one)

        mine = jnp.sum(SQ[...], keepdims=True)
        SQS[DEVICES] = jnp.broadcast_to(mine, (8, LANES))
        copies = [
            pltpu.make_async_remote_copy(
                src_ref=SQS.at[DEVICES], dst_ref=SQS.at[me], send_sem=sq_send.at[k - 1], recv_sem=sq_recv.at[k - 1],
                device_id={"dp": (me + k) % DEVICES}, device_id_type=pl.DeviceIdType.MESH)
            for k in range(1, DEVICES)
        ]
        start(copies)
        SQS[me] = jnp.broadcast_to(mine, (8, LANES))
        wait(outs(last))
        for k in range(1, DEVICES):
            came = SQS.at[(me + DEVICES - k) % DEVICES]
            pltpu.make_async_copy(came, came, sq_recv.at[k - 1]).wait()
            copies[k - 1].wait_send()

    pl.run_scoped(finish, pltpu.VMEM((LANES, D), BF16))

    total = (SQS[0] + SQS[1]) + (SQS[2] + SQS[3])
    count = 2.0 * 3.0 * D * F
    factor[...] = jnp.minimum(1.0, 0.5 * lax.rsqrt(total / count + 1e-30))


def gradients(x, dy, wg, wu, wd):
    T, D = x.shape
    F = wg.shape[2]
    W = DEVICES * LANES
    n, R = F // W, D // DEVICES
    tiles = 2 * n
    hbm = lambda *s, d=BF16: jax.ShapeDtypeStruct(s, d)
    outs = [
        hbm(2, R, F), hbm(2, R, F), hbm(2, F // DEVICES, D), hbm(8, LANES, d=F32),
        hbm(n, T, W, d=F32), hbm(n, T, W, d=F32), hbm(D, T), hbm(T // CHUNK, D, CHUNK),
        hbm(tiles, 3, R, W), hbm(tiles, 3, R, W), hbm(tiles, 3, R, W), hbm(tiles, 3, R, W),
    ]
    sem = pltpu.SemaphoreType.DMA
    return pl.pallas_call(
        grads_kernel,
        out_shape=outs,
        in_specs=[ANY] * 5,
        out_specs=[ANY] * 3 + [pl.BlockSpec(memory_space=pltpu.VMEM)] + [ANY] * 8,
        scratch_shapes=[
            pltpu.VMEM((T, D), BF16), pltpu.VMEM((D, T), BF16), pltpu.VMEM((T, D), BF16), pltpu.VMEM((D, T), BF16),
            pltpu.VMEM((D, T), F32), pltpu.VMEM((3, 2, 2, R, W), BF16), *[pltpu.VMEM((T, W), BF16)] * 3,
            pltpu.VMEM((2, D, W), BF16), pltpu.VMEM((2, D, W), BF16), pltpu.VMEM((2, W, D), BF16),
            *[pltpu.VMEM((T // 2, W), F32), pltpu.VMEM((T // 2, W), F32), pltpu.VMEM((T // 2, W), BF16)] * 2,
            pltpu.VMEM((3, R, W), BF16), pltpu.VMEM((2, 3, R, W), BF16),
            pltpu.VMEM((8, W), F32), pltpu.VMEM((DEVICES + 1, 8, LANES), F32),
            sem((2, 3, DEVICES)), sem((7,)), sem((2,)), sem(()), sem((tiles,)), pltpu.SemaphoreType.REGULAR, sem(()), sem(()),
            sem((tiles,)), sem((tiles,)), sem((12,)), sem((DEVICES - 1,)), sem((DEVICES - 1,)),
        ],
        compiler_params=pltpu.CompilerParams(collective_id=0, has_side_effects=True, vmem_limit_bytes=VMEM_BYTES),
        name="gradients",
    )(x, dy, wg, wu, wd)[:4]


def adamw_kernel(me, factor, g, w, m, v, *refs):
    out, send, new_m, new_v, turn = refs[-5:]
    turn[0] = me[0]
    some = 32

    def part(i):
        r = pl.ds(pl.multiple_of(i * some, some), some)
        grad = g[r, :].astype(F32) * factor[0:1, 0:1]
        one = 0.9 * m[r, :] + 0.1 * grad
        two = 0.95 * v[r, :] + 0.05 * grad * grad
        wide = w[r, :].astype(F32)
        new_w = (wide - 0.02 * (one * lax.rsqrt(two + 1e-8) + 0.1 * wide)).astype(BF16)
        out[r, :] = new_w
        send[r, :] = new_w
        new_m[r, :] = one
        new_v[r, :] = two

    loop(m.shape[0] // some, part)


def adamw(me, factor, g, w, m, v, so_far, layer, first, steps, by_columns):
    rows = m.shape[1] if by_columns else LANES
    cols = DEVICES * LANES if by_columns else m.shape[2]
    tile = (None, rows, cols)
    if by_columns:
        block = pl.BlockSpec(tile, lambda i, me: (layer, 0, first + i))
        whole = pl.BlockSpec(tile, lambda i, me: (layer, me[0], first + i))
        alone, send = (rows, steps * cols), pl.BlockSpec((rows, cols), lambda i, me: (0, i))
    else:
        n = m.shape[1] // LANES
        block = pl.BlockSpec(tile, lambda i, me: (layer, first + i, 0))
        whole = pl.BlockSpec(tile, lambda i, me: (layer, me[0] * n + first + i, 0))
        alone, send = (steps * rows, cols), pl.BlockSpec((rows, cols), lambda i, me: (i, 0))
    begun = so_far is not None
    shape = lambda a: jax.ShapeDtypeStruct(a.shape, a.dtype)
    out, sent, new_m, new_v, turn = pl.pallas_call(
        adamw_kernel,
        grid_spec=pltpu.PrefetchScalarGridSpec(
            num_scalar_prefetch=1,
            grid=(steps,),
            in_specs=[pl.BlockSpec((8, LANES), lambda i, me: (0, 0)), block, whole, block, block] + [ANY] * (3 * begun),
            out_specs=[whole, send, block, block, pl.BlockSpec(memory_space=pltpu.SMEM)],
        ),
        out_shape=[shape(w), jax.ShapeDtypeStruct(alone, BF16), shape(m), shape(v), shape(me)],
        input_output_aliases={6: 0, 7: 2, 8: 3} if begun else {},
        compiler_params=pltpu.CompilerParams(vmem_limit_bytes=VMEM_BYTES),
        cost_estimate=pl.CostEstimate(flops=20 * steps * rows * cols, bytes_accessed=28 * steps * rows * cols, transcendentals=0),
        name="adamw",
    )(me, factor, g, w, m, v, *(so_far or ()))
    return (out, new_m, new_v), sent, turn


def place_kernel(n, at, me_ref, _, *refs):
    pieces, out, turn, bufs, sems = refs[:n], refs[n], refs[n + 1], refs[n + 2 : 2 * n + 2], refs[2 * n + 2]
    turn[0] = me_ref[0]
    loads = [pltpu.make_async_copy(p, b, sems.at[0, k]) for k, (p, b) in enumerate(zip(pieces, bufs))]
    for c in loads:
        c.start()
    stores = []
    for k in range(n):
        loads[k].wait()
        stores.append(pltpu.make_async_copy(bufs[k], out.at[at(k, me_ref[0])], sems.at[1, k]))
        stores[k].start()
    for c in stores:
        c.wait()


def place(out, me, pieces, owners, layer, first, by_columns):
    rows, cols = pieces[0].shape

    def at(k, me):
        owner = me ^ owners[k]
        if by_columns:
            return layer, pl.ds(pl.multiple_of(owner * rows, 8), rows), pl.ds(first * DEVICES * LANES, cols)
        return layer, pl.ds(pl.multiple_of(owner * (out.shape[1] // DEVICES) + first * LANES, LANES), rows), slice(None)

    n = len(pieces)
    return pl.pallas_call(
        functools.partial(place_kernel, n, at),
        in_specs=[pl.BlockSpec(memory_space=pltpu.SMEM)] + [ANY] * (n + 1),
        out_specs=[ANY, pl.BlockSpec(memory_space=pltpu.SMEM)],
        out_shape=[jax.ShapeDtypeStruct(out.shape, out.dtype), jax.ShapeDtypeStruct(me.shape, me.dtype)],
        scratch_shapes=[pltpu.VMEM((rows, cols), BF16)] * n + [pltpu.SemaphoreType.DMA((2, n))],
        input_output_aliases={1: 0},
        compiler_params=pltpu.CompilerParams(vmem_limit_bytes=VMEM_BYTES),
        cost_estimate=pl.CostEstimate(flops=4 * n * rows * cols, bytes_accessed=4 * n * rows * cols, transcendentals=0),
        name="place",
    )(me, out, *pieces)


def other_chip(a):
    return lax.ppermute(a, "dp", [(i, i ^ 2) for i in range(4)])


def other_core(a):
    return lax.ppermute(a, "dp", [(i, i ^ 1) for i in range(4)])


CHUNKS = (
    (0, 0, 0, 1), (0, 0, 1, 3), (0, 0, 4, 5), (0, 1, 0, 9), (1, 0, 0, 9), (1, 1, 0, 9), (2, 0, 0, 9), (2, 1, 0, 5), (2, 1, 5, 3), (2, 1, 8, 1),
)


def solution(mesh):
    def step(x, dy, *arrays):
        weights, m, v = (arrays[i : i + 3] for i in (0, 3, 6))
        me = lax.axis_index("dp").astype(jnp.int32).reshape(1)
        *g, factor = gradients(x[0], dy[0], *weights)
        new = [None] * 3
        gathered = []
        for k, layer, first, steps in CHUNKS:
            new[k], sent, me = adamw(me, factor, g[k], weights[k], m[k], v[k], new[k], layer, first, steps, k < 2)
            far = other_chip(sent)
            own = other_core(sent)
            gathered.append((far, own, other_core(far)))
        whole = [n[0] for n in new]
        for (k, layer, first, steps), pieces in zip(CHUNKS, gathered):
            whole[k], me = place(whole[k], me, pieces, (2, 1, 3), layer, first, k < 2)
        return (*whole, *(n[1] for n in new), *(n[2] for n in new))

    rows = P(None, "dp", None)
    return jax.shard_map(
        step,
        mesh=mesh,
        in_specs=(P(("rep", "dp")), P(("rep", "dp")), *(P(),) * 3, *(rows,) * 6),
        out_specs=(*(P("rep"),) * 3, *(P("rep", "dp"),) * 6),
        check_vma=False,
    )
```

time: 1010 us -> 971 us (0.961)
  Pallas kernels: 687 us -> 648 us
    pallas_call x1, Pallas kernels: 527 us -> 483 us  [gradients(): pl.pallas_call(grads_kernel, out_shape=outs, in_specs=[ANY] * 5, out_spec...]
  transfers between devices with their start and end apart: 30 -> 30, of which waited for: 11 -> 11; matrix products, arithmetic and copies ran while one was open for 0% -> 0% of each run, Pallas kernels for 15% -> 16%
where the time goes in v1:
time: 971 us; the launch traced here: 969 us
  Pallas kernels  648 us (67%)
  waiting for transfers between devices  299 us (31%)
  starting transfers between devices  18 us (2%)
    pallas_call x1, Pallas kernels, gradients(): pl.pallas_call(grads_kernel, out_shape=outs, in_specs=[ANY] * 5, out_spec...  483 us
    ppermute x10, waiting for transfers between devices, other_chip(): return lax.ppermute(a, 'dp', [(i, i ^ 2) for i in range(4)])  290 us
    pallas_call x10, Pallas kernels, adamw(): pl.pallas_call(adamw_kernel, grid_spec=pltpu.PrefetchScalarGridSpec(num_s...  112 us
    pallas_call x10, Pallas kernels, place(): pl.pallas_call(functools.partial(place_kernel, n, at), in_specs=[pl.Block...  52.7 us
  transfers between devices with their start and end apart: 30, of which 11 were waited for; matrix products, arithmetic and copies ran while one was open for 0% of the time, Pallas kernels for 16%

profile of v1, /device:TPU:0, one launch (start us, length us, event | category | flops | bytes accessed | tf_op | source)
XLA Modules:
  0.0 968.6 jit_solution(5795306158065696622)
XLA Ops:
  0.6 483.2 %gradients.1 = (bf16[2,288,4608]{2,1,0:T(8,128)(2,1)}, bf16[2,288,4608]{2,1,0:T(8,128)(2,1)}, bf16[2,1152,1152]{2,1,0:T(8,128)(2,1)}, f32[8,128]{1,0:T(8,128)}, ...) custom-call(bf16[2048,1152]{1,0:T(8,128)(2,1)} %bitcast.3, ...), custom_call_target="tpu_custom_call" | custom-call | tf_op jit(solution)/shard_map/gradients/pallas_call | solution.py:543
  483.8 3.3 adamw.10
  487.1 2.3 collective-permute-start
  489.4 7.3 adamw.11
  496.7 10.7 %adamw.12 = (bf16[2,1152,4608]{2,1,0:T(8,128)(2,1)}, bf16[288,2560]{1,0:T(8,128)(2,1)}, f32[2,288,4608]{2,1,0:T(8,128)}, f32[2,288,4608]{2,1,0:T(8,128)}, s32[1]{0:T(128)}) custom-call(s32[1]{0:T(128)} %get-tuple-element.88.me, f32[8,128]{1,0:T(8,128)} %get-tuple-element.82.factor, ...), custom_call_target="tpu_custom_call", output_to_operand_aliasing={{0}: (6, {}), {2}: (7, {}), {3}: (8, {})} | custom-call | flops 14745600 | bytes 20643840 | tf_op jit(solution)/shard_map/adamw/pallas_call | solution.py:598
  507.5 17.5 %adamw.13 = (bf16[2,1152,4608]{2,1,0:T(8,128)(2,1)}, bf16[288,4608]{1,0:T(8,128)(2,1)}, f32[2,288,4608]{2,1,0:T(8,128)}, f32[2,288,4608]{2,1,0:T(8,128)}, s32[1]{0:T(128)}) custom-call(s32[1]{0:T(128)} %get-tuple-element.92.me, f32[8,128]{1,0:T(8,128)} %get-tuple-element.82.factor, ...), custom_call_target="tpu_custom_call", output_to_operand_aliasing={{0}: (6, {}), {2}: (7, {}), {3}: (8, {})} | custom-call | flops 26542080 | bytes 37158912 | tf_op jit(solution)/shard_map/adamw/pallas_call | solution.py:598
  524.9 17.5 %adamw.14 = (bf16[2,1152,4608]{2,1,0:T(8,128)(2,1)}, bf16[288,4608]{1,0:T(8,128)(2,1)}, f32[2,288,4608]{2,1,0:T(8,128)}, f32[2,288,4608]{2,1,0:T(8,128)}, s32[1]{0:T(128)}) custom-call(s32[1]{0:T(128)} %get-tuple-element.96.me, f32[8,128]{1,0:T(8,128)} %get-tuple-element.82.factor, bf16[2,288,4608]{2,1,0:T(8,128)(2,1)} %get-tuple-element.97.g, ...), custom_call_target="tpu_custom_call" | custom-call | flops 26542080 | bytes 37158912 | tf_op jit(solution)/shard_map/adamw/pallas_call | solution.py:598
  542.4 17.5 %adamw.15 = (bf16[2,1152,4608]{2,1,0:T(8,128)(2,1)}, bf16[288,4608]{1,0:T(8,128)(2,1)}, f32[2,288,4608]{2,1,0:T(8,128)}, f32[2,288,4608]{2,1,0:T(8,128)}, s32[1]{0:T(128)}) custom-call(s32[1]{0:T(128)} %get-tuple-element.98.me, f32[8,128]{1,0:T(8,128)} %get-tuple-element.82.factor, ...), custom_call_target="tpu_custom_call", output_to_operand_aliasing={{0}: (6, {}), {2}: (7, {}), {3}: (8, {})} | custom-call | flops 26542080 | bytes 37158912 | tf_op jit(solution)/shard_map/adamw/pallas_call | solution.py:598
  559.8 17.0 %adamw.16 = (bf16[2,4608,1152]{2,1,0:T(8,128)(2,1)}, bf16[1152,1152]{1,0:T(8,128)(2,1)}, f32[2,1152,1152]{2,1,0:T(8,128)}, f32[2,1152,1152]{2,1,0:T(8,128)}, s32[1]{0:T(128)}) custom-call(s32[1]{0:T(128)} %get-tuple-element.102.me, f32[8,128]{1,0:T(8,128)} %get-tuple-element.82.factor, bf16[2,1152,1152]{2,1,0:T(8,128)(2,1)} %get-tuple-element.103.g, ...), custom_call_target="tpu_custom_call" | custom-call | flops 26542080 | bytes 37158912 | tf_op jit(solution)/shard_map/adamw/pallas_call | solution.py:598
  576.9 10.4 %adamw.17 = (bf16[2,4608,1152]{2,1,0:T(8,128)(2,1)}, bf16[640,1152]{1,0:T(8,128)(2,1)}, f32[2,1152,1152]{2,1,0:T(8,128)}, f32[2,1152,1152]{2,1,0:T(8,128)}, s32[1]{0:T(128)}) custom-call(s32[1]{0:T(128)} %get-tuple-element.104.me, f32[8,128]{1,0:T(8,128)} %get-tuple-element.82.factor, ...), custom_call_target="tpu_custom_call", output_to_operand_aliasing={{0}: (6, {}), {2}: (7, {}), {3}: (8, {})} | custom-call | flops 14745600 | bytes 20643840 | tf_op jit(solution)/shard_map/adamw/pallas_call | solution.py:598
  587.3 7.2 adamw.18
  594.5 3.8 adamw.19
  600.9 7.6 collective-permute-done.27.refs_0_
  610.6 16.8 %collective-permute-done.3.refs_0_ = bf16[288,1536]{1,0:T(8,128)(2,1)S(1)} collective-permute-done((bf16[288,1536]{1,0:T(8,128)(2,1)}, bf16[288,1536]{1,0:T(8,128)(2,1)S(1)}, u32[]{:S(2)}, u32[]{:S(2)}) %collective-permute-start.3) | collective-permute-done | bytes 884768 | tf_op jit(solution)/shard_map/ppermute | solution.py:654
  629.5 17.0 %collective-permute-done.24.refs_0_ = bf16[384,1152]{1,0:T(8,128)(2,1)} collective-permute-done((bf16[384,1152]{1,0:T(8,128)(2,1)}, bf16[384,1152]{1,0:T(8,128)(2,1)}, u32[]{:S(2)}, u32[]{:S(2)}) %collective-permute-start.24) | collective-permute-done | bytes 884768 | tf_op jit(solution)/shard_map/ppermute | solution.py:654
  648.7 29.4 %collective-permute-done.21.refs_0_ = bf16[640,1152]{1,0:T(8,128)(2,1)} collective-permute-done((bf16[640,1152]{1,0:T(8,128)(2,1)}, bf16[640,1152]{1,0:T(8,128)(2,1)}, u32[]{:S(2)}, u32[]{:S(2)}) %collective-permute-start.21) | collective-permute-done | bytes 1474592 | tf_op jit(solution)/shard_map/ppermute | solution.py:654
  683.5 51.4 %collective-permute-done.9.refs_0_ = bf16[288,4608]{1,0:T(8,128)(2,1)S(1)} collective-permute-done((bf16[288,4608]{1,0:T(8,128)(2,1)}, bf16[288,4608]{1,0:T(8,128)(2,1)S(1)}, u32[]{:S(2)}, u32[]{:S(2)}) %collective-permute-start.9) | collective-permute-done | bytes 2654240 | tf_op jit(solution)/shard_map/ppermute | solution.py:654
  736.9 54.8 %collective-permute-done.12.refs_0_ = bf16[288,4608]{1,0:T(8,128)(2,1)S(1)} collective-permute-done((bf16[288,4608]{1,0:T(8,128)(2,1)}, bf16[288,4608]{1,0:T(8,128)(2,1)S(1)}, u32[]{:S(2)}, u32[]{:S(2)}) %collective-permute-start.12) | collective-permute-done | bytes 2654240 | tf_op jit(solution)/shard_map/ppermute | solution.py:654
  792.3 56.3 %collective-permute-done.15.refs_0_ = bf16[288,4608]{1,0:T(8,128)(2,1)S(1)} collective-permute-done((bf16[288,4608]{1,0:T(8,128)(2,1)}, bf16[288,4608]{1,0:T(8,128)(2,1)S(1)}, u32[]{:S(2)}, u32[]{:S(2)}) %collective-permute-start.15) | collective-permute-done | bytes 2654240 | tf_op jit(solution)/shard_map/ppermute | solution.py:654
  849.1 56.2 %collective-permute-done.18.refs_0_ = bf16[1152,1152]{1,0:T(8,128)(2,1)S(1)} collective-permute-done((bf16[1152,1152]{1,0:T(8,128)(2,1)}, bf16[1152,1152]{1,0:T(8,128)(2,1)S(1)}, u32[]{:S(2)}, u32[]{:S(2)}) %collective-permute-start.18) | collective-permute-done | bytes 2654240 | tf_op jit(solution)/shard_map/ppermute | solution.py:654
  906.4 3.8 collective-permute-done.17.refs_2_
  910.4 3.7 collective-permute-done.20.refs_2_
  915.5 3.1 place.10
  918.6 3.9 place.11
  922.6 4.7 place.12
  927.2 7.4 place.13
  934.6 7.4 place.14
  942.0 7.4 place.15
  949.4 7.4 place.16
  956.8 4.7 place.17
  961.6 3.8 place.18
  965.4 3.0 place.19
  (85 shorter events, 20.1 us)
Async XLA Ops:
  487.1 113.3 %collective-permute-start = (bf16[288,512]{1,0:T(8,128)(2,1)}, bf16[288,512]{1,0:T(8,128)(2,1)}, u32[]{:S(2)}, u32[]{:S(2)}) collective-permute-start(bf16[288,512]{1,0:T(8,128)(2,1)} %get-tuple-element.118), channel_id=1, source_target_pairs={{0,2},{1,3},{2,0},{3,1},{4,6},{5,7},{6,4},{7,5}} | collective-permute-start | bytes 884744 | tf_op jit(solution)/shard_map/ppermute | solution.py:654
  507.4 139.1 %collective-permute-start.6 = (bf16[288,2560]{1,0:T(8,128)(2,1)}, bf16[288,2560]{1,0:T(8,128)(2,1)}, u32[]{:S(2)}, u32[]{:S(2)}) collective-permute-start(bf16[288,2560]{1,0:T(8,128)(2,1)} %get-tuple-element.124), channel_id=1, source_target_pairs={{0,2},{1,3},{2,0},{3,1},{4,6},{5,7},{6,4},{7,5}} | collective-permute-start | bytes 4423688 | tf_op jit(solution)/shard_map/ppermute | solution.py:654
  507.4 93.2 %collective-permute-start.1 = (bf16[288,512]{1,0:T(8,128)(2,1)}, bf16[288,512]{1,0:T(8,128)(2,1)}, u32[]{:S(2)}, u32[]{:S(2)}) collective-permute-start(bf16[288,512]{1,0:T(8,128)(2,1)} %get-tuple-element.118), channel_id=1, source_target_pairs={{0,1},{1,0},{2,3},{3,2},{4,5},{5,4},{6,7},{7,6}} | collective-permute-start | bytes 884744 | tf_op jit(solution)/shard_map/ppermute | solution.py:658
  598.3 10.2 %collective-permute-start.27 = (bf16[128,1152]{1,0:T(8,128)(2,1)}, bf16[128,1152]{1,0:T(8,128)(2,1)}, u32[]{:S(2)}, u32[]{:S(2)}) collective-permute-start(bf16[128,1152]{1,0:T(8,128)(2,1)} %get-tuple-element.147), channel_id=1, source_target_pairs={{0,2},{1,3},{2,0},{3,1},{4,6},{5,7},{6,4},{7,5}} | collective-permute-start | bytes 884744 | tf_op jit(solution)/shard_map/ppermute | solution.py:654
  600.4 27.1 %collective-permute-start.3 = (bf16[288,1536]{1,0:T(8,128)(2,1)}, bf16[288,1536]{1,0:T(8,128)(2,1)S(1)}, u32[]{:S(2)}, u32[]{:S(2)}) collective-permute-start(bf16[288,1536]{1,0:T(8,128)(2,1)} %get-tuple-element.121), channel_id=1, source_target_pairs={{0,2},{1,3},{2,0},{3,1},{4,6},{5,7},{6,4},{7,5}} | collective-permute-start | bytes 2654216 | tf_op jit(solution)/shard_map/ppermute | solution.py:654
  600.4 8.2 collective-permute-start.2
  600.6 28.8 %collective-permute-start.4 = (bf16[288,1536]{1,0:T(8,128)(2,1)}, bf16[288,1536]{1,0:T(8,128)(2,1)S(1)}, u32[]{:S(2)}, u32[]{:S(2)}) collective-permute-start(bf16[288,1536]{1,0:T(8,128)(2,1)} %get-tuple-element.121), channel_id=1, source_target_pairs={{0,1},{1,0},{2,3},{3,2},{4,5},{5,4},{6,7},{7,6}} | collective-permute-start | bytes 2654216 | tf_op jit(solution)/shard_map/ppermute | solution.py:658
  608.6 39.9 %collective-permute-start.7 = (bf16[288,2560]{1,0:T(8,128)(2,1)}, bf16[288,2560]{1,0:T(8,128)(2,1)S(1)}, u32[]{:S(2)}, u32[]{:S(2)}) collective-permute-start(bf16[288,2560]{1,0:T(8,128)(2,1)} %get-tuple-element.124), channel_id=1, source_target_pairs={{0,1},{1,0},{2,3},{3,2},{4,5},{5,4},{6,7},{7,6}} | collective-permute-start | bytes 4423688 | tf_op jit(solution)/shard_map/ppermute | solution.py:658
  608.6 37.9 %collective-permute-start.24 = (bf16[384,1152]{1,0:T(8,128)(2,1)}, bf16[384,1152]{1,0:T(8,128)(2,1)}, u32[]{:S(2)}, u32[]{:S(2)}) collective-permute-start(bf16[384,1152]{1,0:T(8,128)(2,1)} %get-tuple-element.144), channel_id=1, source_target_pairs={{0,2},{1,3},{2,0},{3,1},{4,6},{5,7},{6,4},{7,5}} | collective-permute-start | bytes 2654216 | tf_op jit(solution)/shard_map/ppermute | solution.py:654
  627.4 50.7 %collective-permute-start.21 = (bf16[640,1152]{1,0:T(8,128)(2,1)}, bf16[640,1152]{1,0:T(8,128)(2,1)}, u32[]{:S(2)}, u32[]{:S(2)}) collective-permute-start(bf16[640,1152]{1,0:T(8,128)(2,1)} %get-tuple-element.141), channel_id=1, source_target_pairs={{0,2},{1,3},{2,0},{3,1},{4,6},{5,7},{6,4},{7,5}} | collective-permute-start | bytes 4423688 | tf_op jit(solution)/shard_map/ppermute | solution.py:654
  629.4 105.4 %collective-permute-start.9 = (bf16[288,4608]{1,0:T(8,128)(2,1)}, bf16[288,4608]{1,0:T(8,128)(2,1)S(1)}, u32[]{:S(2)}, u32[]{:S(2)}) collective-permute-start(bf16[288,4608]{1,0:T(8,128)(2,1)} %get-tuple-element.127), channel_id=1, source_target_pairs={{0,2},{1,3},{2,0},{3,1},{4,6},{5,7},{6,4},{7,5}} | collective-permute-start | bytes 7962632 | tf_op jit(solution)/shard_map/ppermute | solution.py:654
  646.5 88.4 %collective-permute-start.10 = (bf16[288,4608]{1,0:T(8,128)(2,1)}, bf16[288,4608]{1,0:T(8,128)(2,1)S(1)}, u32[]{:S(2)}, u32[]{:S(2)}) collective-permute-start(bf16[288,4608]{1,0:T(8,128)(2,1)} %get-tuple-element.127), channel_id=1, source_target_pairs={{0,1},{1,0},{2,3},{3,2},{4,5},{5,4},{6,7},{7,6}} | collective-permute-start | bytes 7962632 | tf_op jit(solution)/shard_map/ppermute | solution.py:658
  646.5 145.2 %collective-permute-start.12 = (bf16[288,4608]{1,0:T(8,128)(2,1)}, bf16[288,4608]{1,0:T(8,128)(2,1)S(1)}, u32[]{:S(2)}, u32[]{:S(2)}) collective-permute-start(bf16[288,4608]{1,0:T(8,128)(2,1)} %get-tuple-element.131), channel_id=1, source_target_pairs={{0,2},{1,3},{2,0},{3,1},{4,6},{5,7},{6,4},{7,5}} | collective-permute-start | bytes 7962632 | tf_op jit(solution)/shard_map/ppermute | solution.py:654
  648.5 29.6 %collective-permute-start.22 = (bf16[640,1152]{1,0:T(8,128)(2,1)}, bf16[640,1152]{1,0:T(8,128)(2,1)}, u32[]{:S(2)}, u32[]{:S(2)}) collective-permute-start(bf16[640,1152]{1,0:T(8,128)(2,1)} %get-tuple-element.141), channel_id=1, source_target_pairs={{0,1},{1,0},{2,3},{3,2},{4,5},{5,4},{6,7},{7,6}} | collective-permute-start | bytes 4423688 | tf_op jit(solution)/shard_map/ppermute | solution.py:658
  678.1 2.4 collective-permute-start.5
  678.1 113.6 %collective-permute-start.13 = (bf16[288,4608]{1,0:T(8,128)(2,1)}, bf16[288,4608]{1,0:T(8,128)(2,1)S(1)}, u32[]{:S(2)}, u32[]{:S(2)}) collective-permute-start(bf16[288,4608]{1,0:T(8,128)(2,1)} %get-tuple-element.131), channel_id=1, source_target_pairs={{0,1},{1,0},{2,3},{3,2},{4,5},{5,4},{6,7},{7,6}} | collective-permute-start | bytes 7962632 | tf_op jit(solution)/shard_map/ppermute | solution.py:658
  681.5 167.2 %collective-permute-start.15 = (bf16[288,4608]{1,0:T(8,128)(2,1)}, bf16[288,4608]{1,0:T(8,128)(2,1)S(1)}, u32[]{:S(2)}, u32[]{:S(2)}) collective-permute-start(bf16[288,4608]{1,0:T(8,128)(2,1)} %get-tuple-element.134), channel_id=1, source_target_pairs={{0,2},{1,3},{2,0},{3,1},{4,6},{5,7},{6,4},{7,5}} | collective-permute-start | bytes 7962632 | tf_op jit(solution)/shard_map/ppermute | solution.py:654
  734.9 113.8 %collective-permute-start.16 = (bf16[288,4608]{1,0:T(8,128)(2,1)}, bf16[288,4608]{1,0:T(8,128)(2,1)S(1)}, u32[]{:S(2)}, u32[]{:S(2)}) collective-permute-start(bf16[288,4608]{1,0:T(8,128)(2,1)} %get-tuple-element.134), channel_id=1, source_target_pairs={{0,1},{1,0},{2,3},{3,2},{4,5},{5,4},{6,7},{7,6}} | collective-permute-start | bytes 7962632 | tf_op jit(solution)/shard_map/ppermute | solution.py:658
  734.9 171.0 %copy-start.1 = (bf16[288,4608]{1,0:T(8,128)(2,1)}, bf16[288,4608]{1,0:T(8,128)(2,1)S(1)}, u32[]{:S(2)}) copy-start(bf16[288,4608]{1,0:T(8,128)(2,1)S(1)} %collective-permute-done.10.refs_1_) | copy-start | bytes 7962628
  734.9 170.4 %collective-permute-start.18 = (bf16[1152,1152]{1,0:T(8,128)(2,1)}, bf16[1152,1152]{1,0:T(8,128)(2,1)S(1)}, u32[]{:S(2)}, u32[]{:S(2)}) collective-permute-start(bf16[1152,1152]{1,0:T(8,128)(2,1)} %get-tuple-element.138), channel_id=1, source_target_pairs={{0,2},{1,3},{2,0},{3,1},{4,6},{5,7},{6,4},{7,5}} | collective-permute-start | bytes 7962632 | tf_op jit(solution)/shard_map/ppermute | solution.py:654
  791.7 114.6 %copy-start.2 = (bf16[288,4608]{1,0:T(8,128)(2,1)}, bf16[288,4608]{1,0:T(8,128)(2,1)S(1)}, u32[]{:S(2)}) copy-start(bf16[288,4608]{1,0:T(8,128)(2,1)S(1)} %collective-permute-done.12.refs_0_) | copy-start | bytes 7962628
  791.7 113.6 %collective-permute-start.19 = (bf16[1152,1152]{1,0:T(8,128)(2,1)}, bf16[1152,1152]{1,0:T(8,128)(2,1)S(1)}, u32[]{:S(2)}, u32[]{:S(2)}) collective-permute-start(bf16[1152,1152]{1,0:T(8,128)(2,1)} %get-tuple-element.138), channel_id=1, source_target_pairs={{0,1},{1,0},{2,3},{3,2},{4,5},{5,4},{6,7},{7,6}} | collective-permute-start | bytes 7962632 | tf_op jit(solution)/shard_map/ppermute | solution.py:658
  791.8 114.1 %collective-permute-start.11 = (bf16[288,4608]{1,0:T(8,128)(2,1)S(1)}, bf16[288,4608]{1,0:T(8,128)(2,1)S(1)}, u32[]{:S(2)}, u32[]{:S(2)}) collective-permute-start(bf16[288,4608]{1,0:T(8,128)(2,1)S(1)} %collective-permute-done.9.refs_0_), channel_id=1, source_target_pairs={{0,1},{1,0},{2,3},{3,2},{4,5},{5,4},{6,7},{7,6}} | collective-permute-start | bytes 7962632 | tf_op jit(solution)/shard_map/ppermute | solution.py:658
  848.6 57.7 %collective-permute-start.14 = (bf16[288,4608]{1,0:T(8,128)(2,1)S(1)}, bf16[288,4608]{1,0:T(8,128)(2,1)S(1)}, u32[]{:S(2)}, u32[]{:S(2)}) collective-permute-start(bf16[288,4608]{1,0:T(8,128)(2,1)S(1)} %collective-permute-done.12.refs_0_), channel_id=1, source_target_pairs={{0,1},{1,0},{2,3},{3,2},{4,5},{5,4},{6,7},{7,6}} | collective-permute-start | bytes 7962632 | tf_op jit(solution)/shard_map/ppermute | solution.py:658
  848.6 57.2 %collective-permute-start.8 = (bf16[288,2560]{1,0:T(8,128)(2,1)}, bf16[288,2560]{1,0:T(8,128)(2,1)S(1)}, u32[]{:S(2)}, u32[]{:S(2)}) collective-permute-start(bf16[288,2560]{1,0:T(8,128)(2,1)} %collective-permute-done.6.refs_0_), channel_id=1, source_target_pairs={{0,1},{1,0},{2,3},{3,2},{4,5},{5,4},{6,7},{7,6}} | collective-permute-start | bytes 4423688 | tf_op jit(solution)/shard_map/ppermute | solution.py:658
  905.3 5.0 collective-permute-start.17
  905.3 8.7 collective-permute-start.20
  905.8 51.0 %collective-permute-start.23 = (bf16[640,1152]{1,0:T(8,128)(2,1)}, bf16[640,1152]{1,0:T(8,128)(2,1)}, u32[]{:S(2)}, u32[]{:S(2)}) collective-permute-start(bf16[640,1152]{1,0:T(8,128)(2,1)} %collective-permute-done.21.refs_0_), channel_id=1, source_target_pairs={{0,1},{1,0},{2,3},{3,2},{4,5},{5,4},{6,7},{7,6}} | collective-permute-start | bytes 4423688 | tf_op jit(solution)/shard_map/ppermute | solution.py:658
  905.9 55.7 %collective-permute-start.25 = (bf16[384,1152]{1,0:T(8,128)(2,1)}, bf16[384,1152]{1,0:T(8,128)(2,1)}, u32[]{:S(2)}, u32[]{:S(2)}) collective-permute-start(bf16[384,1152]{1,0:T(8,128)(2,1)} %get-tuple-element.144), channel_id=1, source_target_pairs={{0,1},{1,0},{2,3},{3,2},{4,5},{5,4},{6,7},{7,6}} | collective-permute-start | bytes 2654216 | tf_op jit(solution)/shard_map/ppermute | solution.py:658
  906.4 55.2 %collective-permute-start.26 = (bf16[384,1152]{1,0:T(8,128)(2,1)}, bf16[384,1152]{1,0:T(8,128)(2,1)}, u32[]{:S(2)}, u32[]{:S(2)}) collective-permute-start(bf16[384,1152]{1,0:T(8,128)(2,1)} %collective-permute-done.24.refs_0_), channel_id=1, source_target_pairs={{0,1},{1,0},{2,3},{3,2},{4,5},{5,4},{6,7},{7,6}} | collective-permute-start | bytes 2654216 | tf_op jit(solution)/shard_map/ppermute | solution.py:658
  910.3 55.1 %collective-permute-start.28 = (bf16[128,1152]{1,0:T(8,128)(2,1)}, bf16[128,1152]{1,0:T(8,128)(2,1)}, u32[]{:S(2)}, u32[]{:S(2)}) collective-permute-start(bf16[128,1152]{1,0:T(8,128)(2,1)} %get-tuple-element.147), channel_id=1, source_target_pairs={{0,1},{1,0},{2,3},{3,2},{4,5},{5,4},{6,7},{7,6}} | collective-permute-start | bytes 884744 | tf_op jit(solution)/shard_map/ppermute | solution.py:658
  914.1 51.3 %collective-permute-start.29 = (bf16[128,1152]{1,0:T(8,128)(2,1)}, bf16[128,1152]{1,0:T(8,128)(2,1)}, u32[]{:S(2)}, u32[]{:S(2)}) collective-permute-start(bf16[128,1152]{1,0:T(8,128)(2,1)} %collective-permute-done.27.refs_0_), channel_id=1, source_target_pairs={{0,1},{1,0},{2,3},{3,2},{4,5},{5,4},{6,7},{7,6}} | collective-permute-start | bytes 884744 | tf_op jit(solution)/shard_map/ppermute | solution.py:658
  (16 other events, 536.6 us)

commit v2 on v1

--- a/solution.py
+++ b/solution.py
@@ -12,6 +12,7 @@
 DEVICES = 4
 LANES = 128
 CHUNK = 256
+EARLY = 3
 ANY = pl.BlockSpec(memory_space=pl.ANY)
 VMEM_BYTES = 67_043_328
 
@@ -36,10 +37,10 @@
 
 
 def grads_kernel(
-    x, dy, wg, wu, wd,
-    gg, gu, gd, factor, gate_s, up_s, a0t_s, ht_s, mate, own, far, cross,
-    A, AT, DD, DT, ACC, GR, ACT, DG, DU, WG, WU, WD, G0, U0, D0, G1, U1, D1, MATEB, FB, SQ, SQS,
-    wsem, iosem, d2d_send, d2d_recv, near_recv, free, own_sem, far_sem, x_send, x_recv, fsem, sq_send, sq_recv,
+    x, dy, wg, wu, wd, md, vd,
+    gg, gu, gd, factor, mo, vo, go, ge, gate_s, up_s, a0t_s, ht_s, mate, own, far, cross,
+    DN, A, AT, DD, DT, ACC, GR, ACT, DG, DU, WG, WU, WD, G0, U0, D0, G1, U1, D1, MATEB, FB, SQ, SQS,
+    wsem, iosem, d2d_send, d2d_recv, near_recv, free, own_sem, far_sem, x_send, x_recv, fsem, sq_send, sq_recv, e_sem, e_send, e_recv,
 ):
     T, D = x.shape
     F = wg.shape[2]
@@ -96,6 +97,45 @@
             src_ref=FB.at[t % 2] if direct else far.at[t], dst_ref=cross.at[t], send_sem=x_send.at[t], recv_sem=x_recv.at[t],
             device_id=cross_id, device_id_type=pl.DeviceIdType.MESH)
 
+    def moments():
+        rows = pl.ds(0, EARLY * LANES)
+        return [
+            pltpu.make_async_remote_copy(
+                src_ref=src.at[1, rows], dst_ref=dst, send_sem=e_send.at[n], recv_sem=e_recv.at[n],
+                device_id=cross_id, device_id_type=pl.DeviceIdType.MESH)
+            for n, (src, dst) in enumerate(((md, mo), (vd, vo)))
+        ]
+
+    def early_rows(t):
+        return pl.ds(pl.multiple_of(t * LANES, LANES), LANES)
+
+    def early_send(t):
+        return pltpu.make_async_remote_copy(
+            src_ref=ge.at[early_rows(t)], dst_ref=go.at[early_rows(t)], send_sem=e_send.at[2 + t], recv_sem=e_recv.at[2 + t],
+            device_id=cross_id, device_id_type=pl.DeviceIdType.MESH)
+
+    def early_store(t):
+        return pltpu.make_async_copy(DN, ge.at[early_rows(t)], e_sem.at[3])
+
+    def early_loads(t):
+        return [
+            pltpu.make_async_copy(src.at[t, 2], D0.at[pl.ds(n * R, R)], e_sem.at[n]) for n, src in enumerate((own, mate, cross))
+        ]
+
+    def early_begin(t):
+        across(t, True).wait_recv()
+        d2d(t, NEAR).wait_recv()
+        start(early_loads(t))
+
+    def early_sum(t):
+        wait(early_loads(t))
+        g = (D0[0:R, :].astype(F32) + D0[R : 2 * R, :].astype(F32) + D0[2 * R : 3 * R, :].astype(F32)).astype(BF16)
+        DN[...] = tall(g).T
+        early_store(t).start()
+
+    def tall(g):
+        return jnp.concatenate([g[:, q * LANES : (q + 1) * LANES] for q in range(DEVICES)], axis=0)
+
     def far_store(t):
         return pltpu.make_async_copy(FB.at[t % 2], far.at[t], far_sem)
 
@@ -232,6 +272,8 @@
                 loop(T // 4 // LANES, lambda i, c=c: norm_x(c * (T // 4 // LANES) + i))
             load_dy = pltpu.make_async_copy(dy, DD, iosem.at[6])
             load_dy.start()
+            pl.semaphore_wait(barrier, DEVICES - 1)
+            start(moments())
 
             def stores(j, half):
                 return [
@@ -341,7 +383,6 @@
             save(n - 1).wait()
 
         pl.run_scoped(norm_h, pltpu.VMEM((2, D, CHUNK), BF16))
-        pl.semaphore_wait(barrier, DEVICES - 1)
 
         def layer1(HB):
             def projections(half, slot):
@@ -374,6 +415,8 @@
                 projections(1, slot)
                 back(0)
                 apart(j > 0, lambda: sent(j - 1))
+                apart((j > 2) & (j < 3 + EARLY), lambda: (early_store(j - 3).wait(), early_send(j - 3).start()))
+                apart((j > 1) & (j < 2 + EARLY), lambda: early_begin(j - 2))
                 da(lo, slot)
                 back(1)
                 da(hi, slot)
@@ -393,6 +436,7 @@
                 apart(j > 1, lambda: across(j - 2, True).wait_send())
                 far_sum(j)
                 across(j, True).start()
+                apart((j > 1) & (j < 2 + EARLY), lambda: early_sum(j - 2))
 
             loop(NT_, tile)
             norm_back(HB)
@@ -457,7 +501,7 @@
     sent(last)
     pl.semaphore_wait(free, 1)
 
-    def finish(DN):
+    def finish():
         GN, UN, CB = GR.at[0, 1, 0], GR.at[0, 1, 1], GR.at[:, 0, 0]
         SQ[...] = jnp.zeros_like(SQ)
 
@@ -477,9 +521,9 @@
                 pltpu.make_async_copy(mate.at[t], FB.at[1], fsem.at[1]),
                 pltpu.make_async_copy(cross.at[t], CB, fsem.at[2]),
             ]
-            d2d(t, NEAR).wait_recv()
+            apart(t >= EARLY, lambda: d2d(t, NEAR).wait_recv())
             start(ins[:2])
-            across(t, False).wait_recv()
+            apart(t >= EARLY, lambda: across(t, False).wait_recv())
             ins[2].start()
             apart(t > NT_, lambda: across(t, False).wait_send())
 
@@ -498,8 +542,7 @@
                 elif k == 1:
                     UN[...] = g
                 else:
-                    tall = jnp.concatenate([g[:, q * LANES : (q + 1) * LANES] for q in range(DEVICES)], axis=0)
-                    DN[...] = tall.T
+                    DN[...] = tall(g).T
             start(outs(t))
 
         loop(2 * NT_, one)
@@ -520,14 +563,18 @@
             pltpu.make_async_copy(came, came, sq_recv.at[k - 1]).wait()
             copies[k - 1].wait_send()
 
-    pl.run_scoped(finish, pltpu.VMEM((LANES, D), BF16))
+    finish()
+    for c in moments():
+        c.wait()
+    for t in range(EARLY):
+        early_send(t).wait()
 
     total = (SQS[0] + SQS[1]) + (SQS[2] + SQS[3])
     count = 2.0 * 3.0 * D * F
     factor[...] = jnp.minimum(1.0, 0.5 * lax.rsqrt(total / count + 1e-30))
 
 
-def gradients(x, dy, wg, wu, wd):
+def gradients(x, dy, wg, wu, wd, md, vd):
     T, D = x.shape
     F = wg.shape[2]
     W = DEVICES * LANES
@@ -536,6 +583,7 @@
     hbm = lambda *s, d=BF16: jax.ShapeDtypeStruct(s, d)
     outs = [
         hbm(2, R, F), hbm(2, R, F), hbm(2, F // DEVICES, D), hbm(8, LANES, d=F32),
+        hbm(EARLY * LANES, D, d=F32), hbm(EARLY * LANES, D, d=F32), hbm(EARLY * LANES, D), hbm(EARLY * LANES, D),
         hbm(n, T, W, d=F32), hbm(n, T, W, d=F32), hbm(D, T), hbm(T // CHUNK, D, CHUNK),
         hbm(tiles, 3, R, W), hbm(tiles, 3, R, W), hbm(tiles, 3, R, W), hbm(tiles, 3, R, W),
     ]
@@ -543,9 +591,10 @@
     return pl.pallas_call(
         grads_kernel,
         out_shape=outs,
-        in_specs=[ANY] * 5,
-        out_specs=[ANY] * 3 + [pl.BlockSpec(memory_space=pltpu.VMEM)] + [ANY] * 8,
+        in_specs=[ANY] * 7,
+        out_specs=[ANY] * 3 + [pl.BlockSpec(memory_space=pltpu.VMEM)] + [ANY] * 12,
         scratch_shapes=[
+            pltpu.VMEM((LANES, D), BF16),
             pltpu.VMEM((T, D), BF16), pltpu.VMEM((D, T), BF16), pltpu.VMEM((T, D), BF16), pltpu.VMEM((D, T), BF16),
             pltpu.VMEM((D, T), F32), pltpu.VMEM((3, 2, 2, R, W), BF16), *[pltpu.VMEM((T, W), BF16)] * 3,
             pltpu.VMEM((2, D, W), BF16), pltpu.VMEM((2, D, W), BF16), pltpu.VMEM((2, W, D), BF16),
@@ -554,10 +603,11 @@
             pltpu.VMEM((8, W), F32), pltpu.VMEM((DEVICES + 1, 8, LANES), F32),
             sem((2, 3, DEVICES)), sem((7,)), sem((2,)), sem(()), sem((tiles,)), pltpu.SemaphoreType.REGULAR, sem(()), sem(()),
             sem((tiles,)), sem((tiles,)), sem((12,)), sem((DEVICES - 1,)), sem((DEVICES - 1,)),
+            sem((4,)), sem((2 + EARLY,)), sem((2 + EARLY,)),
         ],
         compiler_params=pltpu.CompilerParams(collective_id=0, has_side_effects=True, vmem_limit_bytes=VMEM_BYTES),
         name="gradients",
-    )(x, dy, wg, wu, wd)[:4]
+    )(x, dy, wg, wu, wd, md, vd)[:7]
 
 
 def adamw_kernel(me, factor, g, w, m, v, *refs):
@@ -612,6 +662,38 @@
     return (out, new_m, new_v), sent, turn
 
 
+def other_kernel(me, factor, g, w, m, v, _, out, send, turn):
+    turn[0] = me[0]
+    grad = g[...].astype(F32) * factor[0:1, 0:1]
+    one = 0.9 * m[...] + 0.1 * grad
+    two = 0.95 * v[...] + 0.05 * grad * grad
+    wide = w[...].astype(F32)
+    new_w = (wide - 0.02 * (one * lax.rsqrt(two + 1e-8) + 0.1 * wide)).astype(BF16)
+    out[...] = new_w
+    send[...] = new_w
+
+
+def adamw_of_other(me, factor, g, w, m, v, out, layer):
+    D = m.shape[1]
+    n = w.shape[1] // DEVICES // LANES
+    block = pl.BlockSpec((LANES, D), lambda i, me: (i, 0))
+    whole = pl.BlockSpec((None, LANES, D), lambda i, me: (layer, (me[0] ^ 2) * n + i, 0))
+    return pl.pallas_call(
+        other_kernel,
+        grid_spec=pltpu.PrefetchScalarGridSpec(
+            num_scalar_prefetch=1,
+            grid=(EARLY,),
+            in_specs=[pl.BlockSpec((8, LANES), lambda i, me: (0, 0)), block, whole, block, block, ANY],
+            out_specs=[whole, block, pl.BlockSpec(memory_space=pltpu.SMEM)],
+        ),
+        out_shape=[jax.ShapeDtypeStruct(w.shape, BF16), jax.ShapeDtypeStruct(m.shape, BF16), jax.ShapeDtypeStruct(me.shape, me.dtype)],
+        input_output_aliases={6: 0},
+        compiler_params=pltpu.CompilerParams(vmem_limit_bytes=VMEM_BYTES),
+        cost_estimate=pl.CostEstimate(flops=20 * m.size, bytes_accessed=16 * m.size, transcendentals=0),
+        name="adamw_of_other",
+    )(me, factor, g, w, m, v, out)
+
+
 def place_kernel(n, at, me_ref, _, *refs):
     pieces, out, turn, bufs, sems = refs[:n], refs[n], refs[n + 1], refs[n + 2 : 2 * n + 2], refs[2 * n + 2]
     turn[0] = me_ref[0]
@@ -659,7 +741,7 @@
 
 
 CHUNKS = (
-    (0, 0, 0, 1), (0, 0, 1, 3), (0, 0, 4, 5), (0, 1, 0, 9), (1, 0, 0, 9), (1, 1, 0, 9), (2, 0, 0, 9), (2, 1, 0, 5), (2, 1, 5, 3), (2, 1, 8, 1),
+    (0, 0, 0, 1), (0, 0, 1, 3), (0, 0, 4, 5), (0, 1, 0, 9), (1, 0, 0, 9), (1, 1, 0, 9), (2, 0, 0, 9), (2, 1, 3, 3), (2, 1, 6, 2), (2, 1, 8, 1),
 )
 
 
@@ -667,7 +749,7 @@
     def step(x, dy, *arrays):
         weights, m, v = (arrays[i : i + 3] for i in (0, 3, 6))
         me = lax.axis_index("dp").astype(jnp.int32).reshape(1)
-        *g, factor = gradients(x[0], dy[0], *weights)
+        *g, factor, m_other, v_other, g_other = gradients(x[0], dy[0], *weights, m[2], v[2])
         new = [None] * 3
         gathered = []
         for k, layer, first, steps in CHUNKS:
@@ -675,7 +757,12 @@
             far = other_chip(sent)
             own = other_core(sent)
             gathered.append((far, own, other_core(far)))
+        new[2], sent, me = adamw(me, factor, g[2], weights[2], m[2], v[2], new[2], 1, 0, EARLY, False)
         whole = [n[0] for n in new]
+        whole[2], far, me = adamw_of_other(me, factor, g_other, weights[2], m_other, v_other, whole[2], 1)
+        own = other_core(sent)
+        far = other_core(far)
+        whole[2], me = place(whole[2], me, (own, far), (1, 3), 1, 0, False)
         for (k, layer, first, steps), pieces in zip(CHUNKS, gathered):
             whole[k], me = place(whole[k], me, pieces, (2, 1, 3), layer, first, k < 2)
         return (*whole, *(n[1] for n in new), *(n[2] for n in new))

time: 971 us -> 983 us (1.012)
  Pallas kernels: 648 us -> 659 us
    pallas_call x1 -> x2, Pallas kernels: 483 us -> 491 us  [the longest x1 485 us: gradients(): pl.pallas_call(grads_kernel, out_shape=outs, in_specs=[ANY] * 7, out_spec...]
    pallas_call x10 -> x11, Pallas kernels: 52.7 us -> 55.2 us  [place(): pl.pallas_call(functools.partial(place_kernel, n, at), in_specs=[pl.Block...]
    pallas_call x10 -> x11, Pallas kernels: 112 us -> 114 us  [adamw(): pl.pallas_call(adamw_kernel, grid_spec=pltpu.PrefetchScalarGridSpec(num_s...]
  transfers between devices with their start and end apart: 30 -> 32, of which waited for: 11 -> 10; matrix products, arithmetic and copies ran while one was open for 0% -> 0% of each run, Pallas kernels for 16% -> 17%
where the time goes in v2:
time: 983 us; the launch traced here: 980 us
  Pallas kernels  659 us (67%)
  waiting for transfers between devices  304 us (31%)
  starting transfers between devices  11.5 us (1%)
    pallas_call x1, Pallas kernels, gradients(): pl.pallas_call(grads_kernel, out_shape=outs, in_specs=[ANY] * 7, out_spec...  485 us
    ppermute x10, waiting for transfers between devices, other_chip(): return lax.ppermute(a, 'dp', [(i, i ^ 2) for i in range(4)])  296 us
    pallas_call x11, Pallas kernels, adamw(): pl.pallas_call(adamw_kernel, grid_spec=pltpu.PrefetchScalarGridSpec(num_s...  114 us
    pallas_call x11, Pallas kernels, place(): pl.pallas_call(functools.partial(place_kernel, n, at), in_specs=[pl.Block...  55.2 us
  transfers between devices with their start and end apart: 32, of which 10 were waited for; matrix products, arithmetic and copies ran while one was open for 0% of the time, Pallas kernels for 17%

profile of v2, /device:TPU:0, one launch (start us, length us, event | category | flops | bytes accessed | tf_op | source)
XLA Modules:
  0.0 980.2 jit_solution(8850643335791716391)
XLA Ops:
  0.6 484.6 %gradients.1 = (bf16[2,288,4608]{2,1,0:T(8,128)(2,1)}, bf16[2,288,4608]{2,1,0:T(8,128)(2,1)}, bf16[2,1152,1152]{2,1,0:T(8,128)(2,1)}, f32[8,128]{1,0:T(8,128)}, ...) custom-call(bf16[2048,1152]{1,0:T(8,128)(2,1)} %bitcast.3, ...), custom_call_target="tpu_custom_call" | custom-call | tf_op jit(solution)/shard_map/gradients/pallas_call | solution.py:591
  485.3 3.3 adamw.11
  490.9 7.3 adamw.12
  498.2 10.7 %adamw.13 = (bf16[2,1152,4608]{2,1,0:T(8,128)(2,1)}, bf16[288,2560]{1,0:T(8,128)(2,1)}, f32[2,288,4608]{2,1,0:T(8,128)}, f32[2,288,4608]{2,1,0:T(8,128)}, s32[1]{0:T(128)}) custom-call(s32[1]{0:T(128)} %get-tuple-element.101.me, f32[8,128]{1,0:T(8,128)} %get-tuple-element.95.factor, ...), custom_call_target="tpu_custom_call", output_to_operand_aliasing={{0}: (6, {}), {2}: (7, {}), {3}: (8, {})} | custom-call | flops 14745600 | bytes 20643840 | tf_op jit(solution)/shard_map/adamw/pallas_call | solution.py:648
  508.9 17.5 %adamw.14 = (bf16[2,1152,4608]{2,1,0:T(8,128)(2,1)}, bf16[288,4608]{1,0:T(8,128)(2,1)}, f32[2,288,4608]{2,1,0:T(8,128)}, f32[2,288,4608]{2,1,0:T(8,128)}, s32[1]{0:T(128)}) custom-call(s32[1]{0:T(128)} %get-tuple-element.105.me, f32[8,128]{1,0:T(8,128)} %get-tuple-element.95.factor, ...), custom_call_target="tpu_custom_call", output_to_operand_aliasing={{0}: (6, {}), {2}: (7, {}), {3}: (8, {})} | custom-call | flops 26542080 | bytes 37158912 | tf_op jit(solution)/shard_map/adamw/pallas_call | solution.py:648
  526.4 17.5 %adamw.15 = (bf16[2,1152,4608]{2,1,0:T(8,128)(2,1)}, bf16[288,4608]{1,0:T(8,128)(2,1)}, f32[2,288,4608]{2,1,0:T(8,128)}, f32[2,288,4608]{2,1,0:T(8,128)}, s32[1]{0:T(128)}) custom-call(s32[1]{0:T(128)} %get-tuple-element.109.me, f32[8,128]{1,0:T(8,128)} %get-tuple-element.95.factor, bf16[2,288,4608]{2,1,0:T(8,128)(2,1)} %get-tuple-element.110.g, ...), custom_call_target="tpu_custom_call" | custom-call | flops 26542080 | bytes 37158912 | tf_op jit(solution)/shard_map/adamw/pallas_call | solution.py:648
  543.8 17.5 %adamw.16 = (bf16[2,1152,4608]{2,1,0:T(8,128)(2,1)}, bf16[288,4608]{1,0:T(8,128)(2,1)}, f32[2,288,4608]{2,1,0:T(8,128)}, f32[2,288,4608]{2,1,0:T(8,128)}, s32[1]{0:T(128)}) custom-call(s32[1]{0:T(128)} %get-tuple-element.111.me, f32[8,128]{1,0:T(8,128)} %get-tuple-element.95.factor, ...), custom_call_target="tpu_custom_call", output_to_operand_aliasing={{0}: (6, {}), {2}: (7, {}), {3}: (8, {})} | custom-call | flops 26542080 | bytes 37158912 | tf_op jit(solution)/shard_map/adamw/pallas_call | solution.py:648
  561.3 17.0 %adamw.17 = (bf16[2,4608,1152]{2,1,0:T(8,128)(2,1)}, bf16[1152,1152]{1,0:T(8,128)(2,1)}, f32[2,1152,1152]{2,1,0:T(8,128)}, f32[2,1152,1152]{2,1,0:T(8,128)}, s32[1]{0:T(128)}) custom-call(s32[1]{0:T(128)} %get-tuple-element.115.me, f32[8,128]{1,0:T(8,128)} %get-tuple-element.95.factor, bf16[2,1152,1152]{2,1,0:T(8,128)(2,1)} %get-tuple-element.116.g, ...), custom_call_target="tpu_custom_call" | custom-call | flops 26542080 | bytes 37158912 | tf_op jit(solution)/shard_map/adamw/pallas_call | solution.py:648
  578.3 7.2 adamw.18
  585.5 4.5 adamw.19
  590.0 3.8 adamw.20
  596.2 7.2 adamw.21
  603.4 5.9 adamw_of_other.1
  610.1 6.7 collective-permute-done.26.refs_0_
  618.8 16.8 %collective-permute-done.5.refs_0_ = bf16[288,1536]{1,0:T(8,128)(2,1)S(1)} collective-permute-done((bf16[288,1536]{1,0:T(8,128)(2,1)}, bf16[288,1536]{1,0:T(8,128)(2,1)S(1)}, u32[]{:S(2)}, u32[]{:S(2)}) %collective-permute-start.5) | collective-permute-done | bytes 884768 | tf_op jit(solution)/shard_map/ppermute | solution.py:736
  635.8 18.9 %collective-permute-done.23.refs_0_ = bf16[384,1152]{1,0:T(8,128)(2,1)} collective-permute-done((bf16[384,1152]{1,0:T(8,128)(2,1)}, bf16[384,1152]{1,0:T(8,128)(2,1)}, u32[]{:S(2)}, u32[]{:S(2)}) %collective-permute-start.23) | collective-permute-done | bytes 884768 | tf_op jit(solution)/shard_map/ppermute | solution.py:736
  654.9 31.3 %collective-permute-done.8.refs_0_ = bf16[288,2560]{1,0:T(8,128)(2,1)S(1)} collective-permute-done((bf16[288,2560]{1,0:T(8,128)(2,1)}, bf16[288,2560]{1,0:T(8,128)(2,1)S(1)}, u32[]{:S(2)}, u32[]{:S(2)}) %collective-permute-start.8) | collective-permute-done | bytes 1474592 | tf_op jit(solution)/shard_map/ppermute | solution.py:736
  689.7 53.3 %collective-permute-done.11.refs_0_ = bf16[288,4608]{1,0:T(8,128)(2,1)S(1)} collective-permute-done((bf16[288,4608]{1,0:T(8,128)(2,1)}, bf16[288,4608]{1,0:T(8,128)(2,1)S(1)}, u32[]{:S(2)}, u32[]{:S(2)}) %collective-permute-start.11) | collective-permute-done | bytes 2654240 | tf_op jit(solution)/shard_map/ppermute | solution.py:736
  743.3 56.6 %collective-permute-done.14.refs_0_ = bf16[288,4608]{1,0:T(8,128)(2,1)S(1)} collective-permute-done((bf16[288,4608]{1,0:T(8,128)(2,1)}, bf16[288,4608]{1,0:T(8,128)(2,1)S(1)}, u32[]{:S(2)}, u32[]{:S(2)}) %collective-permute-start.14) | collective-permute-done | bytes 2654240 | tf_op jit(solution)/shard_map/ppermute | solution.py:736
  800.5 56.3 %collective-permute-done.17.refs_0_ = bf16[288,4608]{1,0:T(8,128)(2,1)S(1)} collective-permute-done((bf16[288,4608]{1,0:T(8,128)(2,1)}, bf16[288,4608]{1,0:T(8,128)(2,1)S(1)}, u32[]{:S(2)}, u32[]{:S(2)}) %collective-permute-start.17) | collective-permute-done | bytes 2654240 | tf_op jit(solution)/shard_map/ppermute | solution.py:736
  857.3 55.9 %collective-permute-done.20.refs_0_ = bf16[1152,1152]{1,0:T(8,128)(2,1)S(1)} collective-permute-done((bf16[1152,1152]{1,0:T(8,128)(2,1)}, bf16[1152,1152]{1,0:T(8,128)(2,1)S(1)}, u32[]{:S(2)}, u32[]{:S(2)}) %collective-permute-start.20) | collective-permute-done | bytes 2654240 | tf_op jit(solution)/shard_map/ppermute | solution.py:736
  913.7 6.5 collective-permute-done.10.refs_2_
  924.7 3.6 place.11
  928.3 3.1 place.12
  931.4 3.8 place.13
  935.2 4.7 place.14
  939.9 7.5 place.15
  947.4 7.4 place.16
  954.8 7.5 place.17
  962.3 7.4 place.18
  969.7 3.8 place.19
  973.5 3.5 place.20
  (96 shorter events, 20.5 us)
Async XLA Ops:
  488.6 105.5 %collective-permute-start.2 = (bf16[288,512]{1,0:T(8,128)(2,1)}, bf16[288,512]{1,0:T(8,128)(2,1)}, u32[]{:S(2)}, u32[]{:S(2)}) collective-permute-start(bf16[288,512]{1,0:T(8,128)(2,1)} %get-tuple-element.144), channel_id=1, source_target_pairs={{0,2},{1,3},{2,0},{3,1},{4,6},{5,7},{6,4},{7,5}} | collective-permute-start | bytes 884744 | tf_op jit(solution)/shard_map/ppermute | solution.py:736
  490.9 118.4 %collective-permute-start.3 = (bf16[288,512]{1,0:T(8,128)(2,1)}, bf16[288,512]{1,0:T(8,128)(2,1)}, u32[]{:S(2)}, u32[]{:S(2)}) collective-permute-start(bf16[288,512]{1,0:T(8,128)(2,1)} %get-tuple-element.144), channel_id=1, source_target_pairs={{0,1},{1,0},{2,3},{3,2},{4,5},{5,4},{6,7},{7,6}} | collective-permute-start | bytes 884744 | tf_op jit(solution)/shard_map/ppermute | solution.py:740
  593.9 15.9 %collective-permute-start.29 = (bf16[128,1152]{1,0:T(8,128)(2,1)}, bf16[128,1152]{1,0:T(8,128)(2,1)}, u32[]{:S(2)}, u32[]{:S(2)}) collective-permute-start(bf16[128,1152]{1,0:T(8,128)(2,1)} %get-tuple-element.173), channel_id=1, source_target_pairs={{0,2},{1,3},{2,0},{3,1},{4,6},{5,7},{6,4},{7,5}} | collective-permute-start | bytes 884744 | tf_op jit(solution)/shard_map/ppermute | solution.py:736
  594.1 16.0 %collective-permute-start.4 = (bf16[288,512]{1,0:T(8,128)(2,1)}, bf16[288,512]{1,0:T(8,128)(2,1)}, u32[]{:S(2)}, u32[]{:S(2)}) collective-permute-start(bf16[288,512]{1,0:T(8,128)(2,1)} %collective-permute-done.2.refs_0_), channel_id=1, source_target_pairs={{0,1},{1,0},{2,3},{3,2},{4,5},{5,4},{6,7},{7,6}} | collective-permute-start | bytes 884744 | tf_op jit(solution)/shard_map/ppermute | solution.py:740
  594.5 22.3 %collective-permute-start.26 = (bf16[256,1152]{1,0:T(8,128)(2,1)}, bf16[256,1152]{1,0:T(8,128)(2,1)}, u32[]{:S(2)}, u32[]{:S(2)}) collective-permute-start(bf16[256,1152]{1,0:T(8,128)(2,1)} %get-tuple-element.170), channel_id=1, source_target_pairs={{0,2},{1,3},{2,0},{3,1},{4,6},{5,7},{6,4},{7,5}} | collective-permute-start | bytes 1769480 | tf_op jit(solution)/shard_map/ppermute | solution.py:736
  609.2 7.7 collective-permute-start.1
  609.3 7.7 collective-permute-start
  609.8 25.8 %collective-permute-start.5 = (bf16[288,1536]{1,0:T(8,128)(2,1)}, bf16[288,1536]{1,0:T(8,128)(2,1)S(1)}, u32[]{:S(2)}, u32[]{:S(2)}) collective-permute-start(bf16[288,1536]{1,0:T(8,128)(2,1)} %get-tuple-element.147), channel_id=1, source_target_pairs={{0,2},{1,3},{2,0},{3,1},{4,6},{5,7},{6,4},{7,5}} | collective-permute-start | bytes 2654216 | tf_op jit(solution)/shard_map/ppermute | solution.py:736
  610.1 25.7 %collective-permute-start.6 = (bf16[288,1536]{1,0:T(8,128)(2,1)}, bf16[288,1536]{1,0:T(8,128)(2,1)S(1)}, u32[]{:S(2)}, u32[]{:S(2)}) collective-permute-start(bf16[288,1536]{1,0:T(8,128)(2,1)} %get-tuple-element.147), channel_id=1, source_target_pairs={{0,1},{1,0},{2,3},{3,2},{4,5},{5,4},{6,7},{7,6}} | collective-permute-start | bytes 2654216 | tf_op jit(solution)/shard_map/ppermute | solution.py:740
  616.8 37.9 %collective-permute-start.23 = (bf16[384,1152]{1,0:T(8,128)(2,1)}, bf16[384,1152]{1,0:T(8,128)(2,1)}, u32[]{:S(2)}, u32[]{:S(2)}) collective-permute-start(bf16[384,1152]{1,0:T(8,128)(2,1)} %get-tuple-element.167), channel_id=1, source_target_pairs={{0,2},{1,3},{2,0},{3,1},{4,6},{5,7},{6,4},{7,5}} | collective-permute-start | bytes 2654216 | tf_op jit(solution)/shard_map/ppermute | solution.py:736
  617.0 37.9 %collective-permute-start.24 = (bf16[384,1152]{1,0:T(8,128)(2,1)}, bf16[384,1152]{1,0:T(8,128)(2,1)S(1)}, u32[]{:S(2)}, u32[]{:S(2)}) collective-permute-start(bf16[384,1152]{1,0:T(8,128)(2,1)} %get-tuple-element.167), channel_id=1, source_target_pairs={{0,1},{1,0},{2,3},{3,2},{4,5},{5,4},{6,7},{7,6}} | collective-permute-start | bytes 2654216 | tf_op jit(solution)/shard_map/ppermute | solution.py:740
  617.0 69.2 %collective-permute-start.8 = (bf16[288,2560]{1,0:T(8,128)(2,1)}, bf16[288,2560]{1,0:T(8,128)(2,1)S(1)}, u32[]{:S(2)}, u32[]{:S(2)}) collective-permute-start(bf16[288,2560]{1,0:T(8,128)(2,1)} %get-tuple-element.150), channel_id=1, source_target_pairs={{0,2},{1,3},{2,0},{3,1},{4,6},{5,7},{6,4},{7,5}} | collective-permute-start | bytes 4423688 | tf_op jit(solution)/shard_map/ppermute | solution.py:736
  635.6 107.4 %collective-permute-start.11 = (bf16[288,4608]{1,0:T(8,128)(2,1)}, bf16[288,4608]{1,0:T(8,128)(2,1)S(1)}, u32[]{:S(2)}, u32[]{:S(2)}) collective-permute-start(bf16[288,4608]{1,0:T(8,128)(2,1)} %get-tuple-element.153), channel_id=1, source_target_pairs={{0,2},{1,3},{2,0},{3,1},{4,6},{5,7},{6,4},{7,5}} | collective-permute-start | bytes 7962632 | tf_op jit(solution)/shard_map/ppermute | solution.py:736
  635.8 107.2 %collective-permute-start.12 = (bf16[288,4608]{1,0:T(8,128)(2,1)}, bf16[288,4608]{1,0:T(8,128)(2,1)S(1)}, u32[]{:S(2)}, u32[]{:S(2)}) collective-permute-start(bf16[288,4608]{1,0:T(8,128)(2,1)} %get-tuple-element.153), channel_id=1, source_target_pairs={{0,1},{1,0},{2,3},{3,2},{4,5},{5,4},{6,7},{7,6}} | collective-permute-start | bytes 7962632 | tf_op jit(solution)/shard_map/ppermute | solution.py:740
  654.7 145.3 %collective-permute-start.14 = (bf16[288,4608]{1,0:T(8,128)(2,1)}, bf16[288,4608]{1,0:T(8,128)(2,1)S(1)}, u32[]{:S(2)}, u32[]{:S(2)}) collective-permute-start(bf16[288,4608]{1,0:T(8,128)(2,1)} %get-tuple-element.157), channel_id=1, source_target_pairs={{0,2},{1,3},{2,0},{3,1},{4,6},{5,7},{6,4},{7,5}} | collective-permute-start | bytes 7962632 | tf_op jit(solution)/shard_map/ppermute | solution.py:736
  654.9 31.3 %collective-permute-start.9 = (bf16[288,2560]{1,0:T(8,128)(2,1)}, bf16[288,2560]{1,0:T(8,128)(2,1)}, u32[]{:S(2)}, u32[]{:S(2)}) collective-permute-start(bf16[288,2560]{1,0:T(8,128)(2,1)} %get-tuple-element.150), channel_id=1, source_target_pairs={{0,1},{1,0},{2,3},{3,2},{4,5},{5,4},{6,7},{7,6}} | collective-permute-start | bytes 4423688 | tf_op jit(solution)/shard_map/ppermute | solution.py:740
  686.2 2.4 collective-permute-start.7
  686.2 113.7 %collective-permute-start.15 = (bf16[288,4608]{1,0:T(8,128)(2,1)}, bf16[288,4608]{1,0:T(8,128)(2,1)S(1)}, u32[]{:S(2)}, u32[]{:S(2)}) collective-permute-start(bf16[288,4608]{1,0:T(8,128)(2,1)} %get-tuple-element.157), channel_id=1, source_target_pairs={{0,1},{1,0},{2,3},{3,2},{4,5},{5,4},{6,7},{7,6}} | collective-permute-start | bytes 7962632 | tf_op jit(solution)/shard_map/ppermute | solution.py:740
  689.5 167.3 %collective-permute-start.17 = (bf16[288,4608]{1,0:T(8,128)(2,1)}, bf16[288,4608]{1,0:T(8,128)(2,1)S(1)}, u32[]{:S(2)}, u32[]{:S(2)}) collective-permute-start(bf16[288,4608]{1,0:T(8,128)(2,1)} %get-tuple-element.160), channel_id=1, source_target_pairs={{0,2},{1,3},{2,0},{3,1},{4,6},{5,7},{6,4},{7,5}} | collective-permute-start | bytes 7962632 | tf_op jit(solution)/shard_map/ppermute | solution.py:736
  743.0 113.8 %collective-permute-start.18 = (bf16[288,4608]{1,0:T(8,128)(2,1)}, bf16[288,4608]{1,0:T(8,128)(2,1)S(1)}, u32[]{:S(2)}, u32[]{:S(2)}) collective-permute-start(bf16[288,4608]{1,0:T(8,128)(2,1)} %get-tuple-element.160), channel_id=1, source_target_pairs={{0,1},{1,0},{2,3},{3,2},{4,5},{5,4},{6,7},{7,6}} | collective-permute-start | bytes 7962632 | tf_op jit(solution)/shard_map/ppermute | solution.py:740
  743.1 170.2 %collective-permute-start.20 = (bf16[1152,1152]{1,0:T(8,128)(2,1)}, bf16[1152,1152]{1,0:T(8,128)(2,1)S(1)}, u32[]{:S(2)}, u32[]{:S(2)}) collective-permute-start(bf16[1152,1152]{1,0:T(8,128)(2,1)} %get-tuple-element.164), channel_id=1, source_target_pairs={{0,2},{1,3},{2,0},{3,1},{4,6},{5,7},{6,4},{7,5}} | collective-permute-start | bytes 7962632 | tf_op jit(solution)/shard_map/ppermute | solution.py:736
  799.9 113.3 %collective-permute-start.21 = (bf16[1152,1152]{1,0:T(8,128)(2,1)}, bf16[1152,1152]{1,0:T(8,128)(2,1)S(1)}, u32[]{:S(2)}, u32[]{:S(2)}) collective-permute-start(bf16[1152,1152]{1,0:T(8,128)(2,1)} %get-tuple-element.164), channel_id=1, source_target_pairs={{0,1},{1,0},{2,3},{3,2},{4,5},{5,4},{6,7},{7,6}} | collective-permute-start | bytes 7962632 | tf_op jit(solution)/shard_map/ppermute | solution.py:740
  800.0 120.5 %collective-permute-start.13 = (bf16[288,4608]{1,0:T(8,128)(2,1)S(1)}, bf16[288,4608]{1,0:T(8,128)(2,1)S(1)}, u32[]{:S(2)}, u32[]{:S(2)}) collective-permute-start(bf16[288,4608]{1,0:T(8,128)(2,1)S(1)} %collective-permute-done.11.refs_0_), channel_id=1, source_target_pairs={{0,1},{1,0},{2,3},{3,2},{4,5},{5,4},{6,7},{7,6}} | collective-permute-start | bytes 7962632 | tf_op jit(solution)/shard_map/ppermute | solution.py:740
  856.8 64.0 %collective-permute-start.16 = (bf16[288,4608]{1,0:T(8,128)(2,1)S(1)}, bf16[288,4608]{1,0:T(8,128)(2,1)S(1)}, u32[]{:S(2)}, u32[]{:S(2)}) collective-permute-start(bf16[288,4608]{1,0:T(8,128)(2,1)S(1)} %collective-permute-done.14.refs_0_), channel_id=1, source_target_pairs={{0,1},{1,0},{2,3},{3,2},{4,5},{5,4},{6,7},{7,6}} | collective-permute-start | bytes 7962632 | tf_op jit(solution)/shard_map/ppermute | solution.py:740
  856.8 64.2 %collective-permute-start.19 = (bf16[288,4608]{1,0:T(8,128)(2,1)S(1)}, bf16[288,4608]{1,0:T(8,128)(2,1)S(1)}, u32[]{:S(2)}, u32[]{:S(2)}) collective-permute-start(bf16[288,4608]{1,0:T(8,128)(2,1)S(1)} %collective-permute-done.17.refs_0_), channel_id=1, source_target_pairs={{0,1},{1,0},{2,3},{3,2},{4,5},{5,4},{6,7},{7,6}} | collective-permute-start | bytes 7962632 | tf_op jit(solution)/shard_map/ppermute | solution.py:740
  913.2 8.2 collective-permute-start.22
  913.2 7.0 collective-permute-start.10
  920.3 49.4 %collective-permute-start.25 = (bf16[384,1152]{1,0:T(8,128)(2,1)}, bf16[384,1152]{1,0:T(8,128)(2,1)}, u32[]{:S(2)}, u32[]{:S(2)}) collective-permute-start(bf16[384,1152]{1,0:T(8,128)(2,1)} %collective-permute-done.23.refs_0_), channel_id=1, source_target_pairs={{0,1},{1,0},{2,3},{3,2},{4,5},{5,4},{6,7},{7,6}} | collective-permute-start | bytes 2654216 | tf_op jit(solution)/shard_map/ppermute | solution.py:740
  920.4 53.1 %collective-permute-start.27 = (bf16[256,1152]{1,0:T(8,128)(2,1)}, bf16[256,1152]{1,0:T(8,128)(2,1)}, u32[]{:S(2)}, u32[]{:S(2)}) collective-permute-start(bf16[256,1152]{1,0:T(8,128)(2,1)} %get-tuple-element.170), channel_id=1, source_target_pairs={{0,1},{1,0},{2,3},{3,2},{4,5},{5,4},{6,7},{7,6}} | collective-permute-start | bytes 1769480 | tf_op jit(solution)/shard_map/ppermute | solution.py:740
  920.8 52.7 %collective-permute-start.28 = (bf16[256,1152]{1,0:T(8,128)(2,1)}, bf16[256,1152]{1,0:T(8,128)(2,1)}, u32[]{:S(2)}, u32[]{:S(2)}) collective-permute-start(bf16[256,1152]{1,0:T(8,128)(2,1)} %collective-permute-done.26.refs_0_), channel_id=1, source_target_pairs={{0,1},{1,0},{2,3},{3,2},{4,5},{5,4},{6,7},{7,6}} | collective-permute-start | bytes 1769480 | tf_op jit(solution)/shard_map/ppermute | solution.py:740
  921.0 56.0 %collective-permute-start.30 = (bf16[128,1152]{1,0:T(8,128)(2,1)}, bf16[128,1152]{1,0:T(8,128)(2,1)}, u32[]{:S(2)}, u32[]{:S(2)}) collective-permute-start(bf16[128,1152]{1,0:T(8,128)(2,1)} %get-tuple-element.173), channel_id=1, source_target_pairs={{0,1},{1,0},{2,3},{3,2},{4,5},{5,4},{6,7},{7,6}} | collective-permute-start | bytes 884744 | tf_op jit(solution)/shard_map/ppermute | solution.py:740
  921.4 55.6 %collective-permute-start.31 = (bf16[128,1152]{1,0:T(8,128)(2,1)}, bf16[128,1152]{1,0:T(8,128)(2,1)}, u32[]{:S(2)}, u32[]{:S(2)}) collective-permute-start(bf16[128,1152]{1,0:T(8,128)(2,1)} %collective-permute-done.29.refs_0_), channel_id=1, source_target_pairs={{0,1},{1,0},{2,3},{3,2},{4,5},{5,4},{6,7},{7,6}} | collective-permute-start | bytes 884744 | tf_op jit(solution)/shard_map/ppermute | solution.py:740
  (20 other events, 1096.4 us)

commit v3 on v2

--- a/solution.py
+++ b/solution.py
@@ -11,8 +11,10 @@
 F32, BF16 = jnp.float32, jnp.bfloat16
 DEVICES = 4
 LANES = 128
+SOME = 32
+FACTOR = pl.BlockSpec((8, LANES), lambda i, me: (0, 0))
 CHUNK = 256
-EARLY = 3
+EARLY = 4
 ANY = pl.BlockSpec(memory_space=pl.ANY)
 VMEM_BYTES = 67_043_328
 
@@ -46,6 +48,7 @@
     F = wg.shape[2]
     W = DEVICES * LANES
     NT_ = F // W
+    BOTH, HALF, PART = 2 * NT_, D // 2, 96
     FAR, NEAR = 0, 1
     H = T // 2
     R = D // DEVICES
@@ -92,7 +95,7 @@
     def keep(t):
         return pltpu.make_async_copy(GR.at[:, chip, core], own.at[t], own_sem)
 
-    def across(t, direct):
+    def across(t, direct=True):
         return pltpu.make_async_remote_copy(
             src_ref=FB.at[t % 2] if direct else far.at[t], dst_ref=cross.at[t], send_sem=x_send.at[t], recv_sem=x_recv.at[t],
             device_id=cross_id, device_id_type=pl.DeviceIdType.MESH)
@@ -123,14 +126,14 @@
         ]
 
     def early_begin(t):
-        across(t, True).wait_recv()
+        across(t).wait_recv()
         d2d(t, NEAR).wait_recv()
         start(early_loads(t))
 
     def early_sum(t):
         wait(early_loads(t))
         g = (D0[0:R, :].astype(F32) + D0[R : 2 * R, :].astype(F32) + D0[2 * R : 3 * R, :].astype(F32)).astype(BF16)
-        DN[...] = tall(g).T
+        DN[:] = tall(g).T
         early_store(t).start()
 
     def tall(g):
@@ -147,11 +150,11 @@
         d2d(t, FAR).wait_recv()
 
         def some(i):
-            rows = pl.ds(pl.multiple_of(i * 96, 96), 96)
+            rows = pl.ds(pl.multiple_of(i * PART, PART), PART)
             for k in range(3):
                 FB[t % 2, k, rows, :] = (GR[k, 1 - chip, core, rows, :].astype(F32) + MATEB[k, rows, :].astype(F32)).astype(BF16)
 
-        loop(R // 96, some)
+        loop(R // PART, some)
         pl.semaphore_signal(free, inc=1, device_id=mate_id, device_id_type=pl.DeviceIdType.MESH)
 
     def sent(t):
@@ -176,7 +179,7 @@
         return pl.ds(pl.multiple_of(h * (W // 2), W // 2), W // 2)
 
     def half_of(i):
-        return pl.ds(pl.multiple_of(i * (D // 2), D // 2), D // 2)
+        return pl.ds(pl.multiple_of(i * HALF, HALF), HALF)
 
     def product_back(g_ref, u_ref, d_ref, r0):
         step = 16
@@ -196,6 +199,12 @@
         for r in range(0, D, step):
             body(slice(r, r + step))
 
+    def summed(parts):
+        return jnp.sum(sum(parts), axis=0, keepdims=True)
+
+    def scale_of(mean_square):
+        return lax.rsqrt(mean_square + 1e-6)
+
     def folded(t):
         return jnp.sum(t.reshape(t.shape[0] // 8, 8, t.shape[1]), axis=0)
 
@@ -231,8 +240,8 @@
                 along.append(folded(ACC[rows, r].astype(BF16).astype(F32) * wide))
 
             down_rows(64, add)
-            scale = lax.rsqrt(jnp.sum(sum(squares), axis=0, keepdims=True) / D + 1e-6)
-            shrink = jnp.sum(sum(along), axis=0, keepdims=True) / D * (scale * scale * scale)
+            scale = scale_of(summed(squares) / D)
+            shrink = summed(along) / D * (scale * scale * scale)
 
             def back(rows):
                 wide = HB[slot, rows, :].astype(F32)
@@ -264,7 +273,7 @@
             def norm_x(i):
                 r = pl.ds(pl.multiple_of(i * LANES, LANES), LANES)
                 wide = DD[r, :].astype(F32)
-                A[r, :] = (wide * lax.rsqrt(jnp.mean(wide * wide, axis=1, keepdims=True) + 1e-6)).astype(BF16)
+                A[r, :] = (wide * scale_of(jnp.mean(wide * wide, axis=1, keepdims=True))).astype(BF16)
                 AT[:, r] = DD[r, :].T
 
             for c in range(4):
@@ -286,8 +295,8 @@
 
             def projections(half, slot):
                 rows = lo if half == 0 else hi
-                S[half][0][...] = dot(A[rows, :], WG[slot], NN)
-                S[half][1][...] = dot(A[rows, :], WU[slot], NN)
+                S[half][0][:] = dot(A[rows, :], WG[slot], NN)
+                S[half][1][:] = dot(A[rows, :], WU[slot], NN)
 
             def product(half):
                 g_ref, u_ref, _ = S[half]
@@ -369,7 +378,7 @@
 
                 down_rows(64, add)
                 save(i).start()
-                scale = lax.rsqrt(jnp.sum(sum(squares), axis=0, keepdims=True) / D + 1e-6)
+                scale = scale_of(summed(squares) / D)
 
                 def norm(rows):
                     a = (HB[slot, rows, :].astype(F32) * scale).astype(BF16)
@@ -387,9 +396,9 @@
         def layer1(HB):
             def projections(half, slot):
                 rows = lo if half == 0 else hi
-                S[half][0][...] = dot(A[rows, :], WG[slot], NN)
-                S[half][1][...] = dot(A[rows, :], WU[slot], NN)
-                S[half][2][...] = dot(DD[rows, :], WD[slot], NT).astype(BF16)
+                S[half][0][:] = dot(A[rows, :], WG[slot], NN)
+                S[half][1][:] = dot(A[rows, :], WU[slot], NN)
+                S[half][2][:] = dot(DD[rows, :], WD[slot], NT).astype(BF16)
 
             def back(half):
                 g_ref, u_ref, d_ref = S[half]
@@ -409,13 +418,14 @@
 
                 @pl.when(j == NT_ - 1)
                 def _():
-                    start(weights(0, 0, 2 * NT_, True))
+                    start(weights(0, 0, BOTH, True))
 
                 projections(0, slot)
                 projections(1, slot)
                 back(0)
                 apart(j > 0, lambda: sent(j - 1))
-                apart((j > 2) & (j < 3 + EARLY), lambda: (early_store(j - 3).wait(), early_send(j - 3).start()))
+                apart((j > 2) & (j < 3 + EARLY), lambda: early_store(j - 3).wait())
+                apart((j > 2) & (j < 2 + EARLY), lambda: early_send(j - 3).start())
                 apart((j > 1) & (j < 2 + EARLY), lambda: early_begin(j - 2))
                 da(lo, slot)
                 back(1)
@@ -427,15 +437,15 @@
                     for q in (0, 2):
                         put(2, h, dot(DT[q * R : (q + 2) * R, :], ACT[:, hidden_of(h)], NN), q)
                     for k, rhs in ((0, DG), (1, DU)):
-                        put(k, h, dot(AT[half_of(h), :], rhs[...], NN))
+                        put(k, h, dot(AT[half_of(h), :], rhs[:], NN))
                     apart(i == 0, lambda: send_far(j))
 
                 loop(2, gradients)
                 d2d(j, NEAR).start()
                 keep(j).start()
-                apart(j > 1, lambda: across(j - 2, True).wait_send())
+                apart(j > 1, lambda: across(j - 2).wait_send())
                 far_sum(j)
-                across(j, True).start()
+                across(j).start()
                 apart((j > 1) & (j < 2 + EARLY), lambda: early_sum(j - 2))
 
             loop(NT_, tile)
@@ -457,15 +467,15 @@
                 g_ref, u_ref, d_ref = S[half]
                 product_back(lambda r, n: g_ref[r : r + n, :], lambda r, n: u_ref[r : r + n, :], d_ref, half * H)
 
-            wait(weights(0, j, 2 * NT_ + j, True))
+            wait(weights(0, j, BOTH + j, True))
 
             @pl.when(j < NT_ - 1)
             def _():
-                start(weights(0, j + 1, 2 * NT_ + j + 1, True))
+                start(weights(0, j + 1, BOTH + j + 1, True))
 
             wait(loads(j))
-            D0[...] = dot(DD[lo, :], WD[slot], NT).astype(BF16)
-            D1[...] = dot(DD[hi, :], WD[slot], NT).astype(BF16)
+            D0[:] = dot(DD[lo, :], WD[slot], NT).astype(BF16)
+            D1[:] = dot(DD[hi, :], WD[slot], NT).astype(BF16)
             back(0)
             ACC[:, half_sum] = dot(DT[:, lo], ACT[lo, :], NN)
             back(1)
@@ -479,31 +489,32 @@
                     rows = slice(q * R, (q + 2) * R)
                     put(2, h, ACC[rows, hidden_of(h)] + dot(DT[rows, hi], ACT[hi, hidden_of(h)], NN), q)
                 for k, rhs in ((0, DG), (1, DU)):
-                    put(k, h, dot(AT[half_of(h), :], rhs[...], NN))
+                    put(k, h, dot(AT[half_of(h), :], rhs[:], NN))
                 apart((j > 1) & (i == 0), lambda: (far_store(t - 1).wait(), across(t - 1, False).start()))
                 apart(i == 0, lambda: send_far(t))
 
             loop(2, gradients)
             d2d(t, NEAR).start()
             keep(t).start()
-            apart(j < 3, lambda: across(t - 2, True).wait_send())
+            apart(j < 3, lambda: across(t - 2).wait_send())
             far_sum(t)
-            apart(j == 0, lambda: across(t, True).start())
+            apart(j == 0, lambda: across(t).start())
             apart(j > 0, lambda: far_store(t).start())
 
         loop(NT_, tile)
 
     layer0()
 
-    last = 2 * NT_ - 1
+    last = BOTH - 1
     far_store(last).wait()
     across(last, False).start()
+    early_send(EARLY - 1).start()
     sent(last)
     pl.semaphore_wait(free, 1)
 
     def finish():
         GN, UN, CB = GR.at[0, 1, 0], GR.at[0, 1, 1], GR.at[:, 0, 0]
-        SQ[...] = jnp.zeros_like(SQ)
+        SQ[:] = jnp.zeros_like(SQ)
 
         def outs(t):
             l, j = 1 - t // NT_, t % NT_
@@ -536,18 +547,18 @@
                 total = FB[0, k].astype(F32) + FB[1, k].astype(F32) + CB[k].astype(F32)
                 g = total.astype(BF16)
                 wide = g.astype(F32)
-                SQ[...] += jnp.sum((wide * wide).reshape(R // 8, 8, W), axis=0)
+                SQ[:] += jnp.sum((wide * wide).reshape(R // 8, 8, W), axis=0)
                 if k == 0:
-                    GN[...] = g
+                    GN[:] = g
                 elif k == 1:
-                    UN[...] = g
+                    UN[:] = g
                 else:
-                    DN[...] = tall(g).T
+                    DN[:] = tall(g).T
             start(outs(t))
 
-        loop(2 * NT_, one)
-
-        mine = jnp.sum(SQ[...], keepdims=True)
+        loop(BOTH, one)
+
+        mine = jnp.sum(SQ[:], keepdims=True)
         SQS[DEVICES] = jnp.broadcast_to(mine, (8, LANES))
         copies = [
             pltpu.make_async_remote_copy(
@@ -569,9 +580,9 @@
     for t in range(EARLY):
         early_send(t).wait()
 
-    total = (SQS[0] + SQS[1]) + (SQS[2] + SQS[3])
+    total = sum(SQS[k] for k in range(DEVICES))
     count = 2.0 * 3.0 * D * F
-    factor[...] = jnp.minimum(1.0, 0.5 * lax.rsqrt(total / count + 1e-30))
+    factor[:] = jnp.minimum(1.0, 0.5 * lax.rsqrt(total / count + 1e-30))
 
 
 def gradients(x, dy, wg, wu, wd, md, vd):
@@ -610,24 +621,28 @@
     )(x, dy, wg, wu, wd, md, vd)[:7]
 
 
+def cost(n):
+    return pl.CostEstimate(flops=4 * n, bytes_accessed=4 * n, transcendentals=0)
+
+
+def stepped(factor, g, w, m, v):
+    grad = g.astype(F32) * factor[:1, :1]
+    m = 0.9 * m + 0.1 * grad
+    v = 0.95 * v + 0.05 * grad * grad
+    wide = w.astype(F32)
+    return (wide - 0.02 * (m * lax.rsqrt(v + 1e-8) + 0.1 * wide)).astype(BF16), m, v
+
+
 def adamw_kernel(me, factor, g, w, m, v, *refs):
     out, send, new_m, new_v, turn = refs[-5:]
     turn[0] = me[0]
-    some = 32
 
     def part(i):
-        r = pl.ds(pl.multiple_of(i * some, some), some)
-        grad = g[r, :].astype(F32) * factor[0:1, 0:1]
-        one = 0.9 * m[r, :] + 0.1 * grad
-        two = 0.95 * v[r, :] + 0.05 * grad * grad
-        wide = w[r, :].astype(F32)
-        new_w = (wide - 0.02 * (one * lax.rsqrt(two + 1e-8) + 0.1 * wide)).astype(BF16)
-        out[r, :] = new_w
-        send[r, :] = new_w
-        new_m[r, :] = one
-        new_v[r, :] = two
-
-    loop(m.shape[0] // some, part)
+        r = pl.ds(pl.multiple_of(i * SOME, SOME), SOME)
+        out[r, :], new_m[r, :], new_v[r, :] = stepped(factor, g[r, :], w[r, :], m[r, :], v[r, :])
+        send[r, :] = out[r, :]
+
+    loop(m.shape[0] // SOME, part)
 
 
 def adamw(me, factor, g, w, m, v, so_far, layer, first, steps, by_columns):
@@ -650,13 +665,13 @@
         grid_spec=pltpu.PrefetchScalarGridSpec(
             num_scalar_prefetch=1,
             grid=(steps,),
-            in_specs=[pl.BlockSpec((8, LANES), lambda i, me: (0, 0)), block, whole, block, block] + [ANY] * (3 * begun),
+            in_specs=[FACTOR, block, whole, block, block] + [ANY] * (3 * begun),
             out_specs=[whole, send, block, block, pl.BlockSpec(memory_space=pltpu.SMEM)],
         ),
         out_shape=[shape(w), jax.ShapeDtypeStruct(alone, BF16), shape(m), shape(v), shape(me)],
         input_output_aliases={6: 0, 7: 2, 8: 3} if begun else {},
         compiler_params=pltpu.CompilerParams(vmem_limit_bytes=VMEM_BYTES),
-        cost_estimate=pl.CostEstimate(flops=20 * steps * rows * cols, bytes_accessed=28 * steps * rows * cols, transcendentals=0),
+        cost_estimate=cost(5 * steps * rows * cols),
         name="adamw",
     )(me, factor, g, w, m, v, *(so_far or ()))
     return (out, new_m, new_v), sent, turn
@@ -664,13 +679,8 @@
 
 def other_kernel(me, factor, g, w, m, v, _, out, send, turn):
     turn[0] = me[0]
-    grad = g[...].astype(F32) * factor[0:1, 0:1]
-    one = 0.9 * m[...] + 0.1 * grad
-    two = 0.95 * v[...] + 0.05 * grad * grad
-    wide = w[...].astype(F32)
-    new_w = (wide - 0.02 * (one * lax.rsqrt(two + 1e-8) + 0.1 * wide)).astype(BF16)
-    out[...] = new_w
-    send[...] = new_w
+    out[:], *_ = stepped(factor, g[:], w[:], m[:], v[:])
+    send[:] = out[:]
 
 
 def adamw_of_other(me, factor, g, w, m, v, out, layer):
@@ -683,13 +693,13 @@
         grid_spec=pltpu.PrefetchScalarGridSpec(
             num_scalar_prefetch=1,
             grid=(EARLY,),
-            in_specs=[pl.BlockSpec((8, LANES), lambda i, me: (0, 0)), block, whole, block, block, ANY],
+            in_specs=[FACTOR, block, whole, block, block, ANY],
             out_specs=[whole, block, pl.BlockSpec(memory_space=pltpu.SMEM)],
         ),
         out_shape=[jax.ShapeDtypeStruct(w.shape, BF16), jax.ShapeDtypeStruct(m.shape, BF16), jax.ShapeDtypeStruct(me.shape, me.dtype)],
         input_output_aliases={6: 0},
         compiler_params=pltpu.CompilerParams(vmem_limit_bytes=VMEM_BYTES),
-        cost_estimate=pl.CostEstimate(flops=20 * m.size, bytes_accessed=16 * m.size, transcendentals=0),
+        cost_estimate=cost(m.size),
         name="adamw_of_other",
     )(me, factor, g, w, m, v, out)
 
@@ -727,7 +737,7 @@
         scratch_shapes=[pltpu.VMEM((rows, cols), BF16)] * n + [pltpu.SemaphoreType.DMA((2, n))],
         input_output_aliases={1: 0},
         compiler_params=pltpu.CompilerParams(vmem_limit_bytes=VMEM_BYTES),
-        cost_estimate=pl.CostEstimate(flops=4 * n * rows * cols, bytes_accessed=4 * n * rows * cols, transcendentals=0),
+        cost_estimate=cost(n * rows * cols),
         name="place",
     )(me, out, *pieces)
 
@@ -740,9 +750,20 @@
     return lax.ppermute(a, "dp", [(i, i ^ 1) for i in range(4)])
 
 
-CHUNKS = (
-    (0, 0, 0, 1), (0, 0, 1, 3), (0, 0, 4, 5), (0, 1, 0, 9), (1, 0, 0, 9), (1, 1, 0, 9), (2, 0, 0, 9), (2, 1, 3, 3), (2, 1, 6, 2), (2, 1, 8, 1),
-)
+ORDER = ((0, 0, (1, 2, 6)), (0, 1, (9,)), (1, 0, (9,)), (1, 1, (9,)), (2, 0, (9,)), (2, 1, (2, 2, 1)))
+
+
+def chunks():
+    listed = []
+    for k, layer, sizes in ORDER:
+        first = EARLY if (k, layer) == ORDER[-1][:2] else 0
+        for n in sizes:
+            listed.append((k, layer, first, n))
+            first += n
+    return listed
+
+
+CHUNKS = chunks()
 
 
 def solution(mesh):

time: 983 us -> 977 us (level)
  waiting for transfers between devices: 304 us -> 293 us
    ppermute x10, waiting for transfers between devices: 296 us -> 284 us  [other_chip(): return lax.ppermute(a, 'dp', [(i, i ^ 2) for i in range(4)])]
  transfers between devices with their start and end apart: 32 -> 32, of which waited for: 10 -> 7; matrix products, arithmetic and copies ran while one was open for 0% -> 0% of each run, Pallas kernels for 17% -> 17%
where the time goes in v3:
time: 977 us; the launch traced here: 975 us
  Pallas kernels  660 us (68%)
  waiting for transfers between devices  293 us (30%)
  starting transfers between devices  14.6 us (1%)
    pallas_call x1, Pallas kernels, gradients(): pl.pallas_call(grads_kernel, out_shape=outs, in_specs=[ANY] * 7, out_spec...  488 us
    ppermute x10, waiting for transfers between devices, other_chip(): return lax.ppermute(a, 'dp', [(i, i ^ 2) for i in range(4)])  284 us
    pallas_call x11, Pallas kernels, adamw(): pl.pallas_call(adamw_kernel, grid_spec=pltpu.PrefetchScalarGridSpec(num_s...  110 us
    pallas_call x11, Pallas kernels, place(): pl.pallas_call(functools.partial(place_kernel, n, at), in_specs=[pl.Block...  55.3 us
  transfers between devices with their start and end apart: 32, of which 7 were waited for; matrix products, arithmetic and copies ran while one was open for 0% of the time, Pallas kernels for 17%

profile of v3, /device:TPU:0, one launch (start us, length us, event | category | flops | bytes accessed | tf_op | source)
XLA Modules:
  0.0 974.9 jit_solution(10437721774065524909)
XLA Ops:
  0.6 487.9 %gradients.1 = (bf16[2,288,4608]{2,1,0:T(8,128)(2,1)}, bf16[2,288,4608]{2,1,0:T(8,128)(2,1)}, bf16[2,1152,1152]{2,1,0:T(8,128)(2,1)}, f32[8,128]{1,0:T(8,128)}, ...) custom-call(bf16[2048,1152]{1,0:T(8,128)(2,1)} %bitcast.3, ...), custom_call_target="tpu_custom_call" | custom-call | tf_op jit(solution)/shard_map/gradients/pallas_call | solution.py:602
  488.5 3.3 adamw.11
  491.8 4.7 adamw.12
  496.5 2.0 collective-permute-start.5
  499.1 11.5 %adamw.13 = (bf16[2,1152,4608]{2,1,0:T(8,128)(2,1)}, bf16[288,3072]{1,0:T(8,128)(2,1)}, f32[2,288,4608]{2,1,0:T(8,128)}, f32[2,288,4608]{2,1,0:T(8,128)}, s32[1]{0:T(128)}) custom-call(s32[1]{0:T(128)} %get-tuple-element.101.me, f32[8,128]{1,0:T(8,128)} %get-tuple-element.95.factor, ...), custom_call_target="tpu_custom_call", output_to_operand_aliasing={{0}: (6, {}), {2}: (7, {}), {3}: (8, {})} | custom-call | flops 17694720 | bytes 17694720 | tf_op jit(solution)/shard_map/adamw/pallas_call | solution.py:663
  510.5 17.5 %adamw.14 = (bf16[2,1152,4608]{2,1,0:T(8,128)(2,1)}, bf16[288,4608]{1,0:T(8,128)(2,1)}, f32[2,288,4608]{2,1,0:T(8,128)}, f32[2,288,4608]{2,1,0:T(8,128)}, s32[1]{0:T(128)}) custom-call(s32[1]{0:T(128)} %get-tuple-element.105.me, f32[8,128]{1,0:T(8,128)} %get-tuple-element.95.factor, ...), custom_call_target="tpu_custom_call", output_to_operand_aliasing={{0}: (6, {}), {2}: (7, {}), {3}: (8, {})} | custom-call | flops 26542080 | bytes 26542080 | tf_op jit(solution)/shard_map/adamw/pallas_call | solution.py:663
  528.0 17.5 %adamw.15 = (bf16[2,1152,4608]{2,1,0:T(8,128)(2,1)}, bf16[288,4608]{1,0:T(8,128)(2,1)}, f32[2,288,4608]{2,1,0:T(8,128)}, f32[2,288,4608]{2,1,0:T(8,128)}, s32[1]{0:T(128)}) custom-call(s32[1]{0:T(128)} %get-tuple-element.109.me, f32[8,128]{1,0:T(8,128)} %get-tuple-element.95.factor, bf16[2,288,4608]{2,1,0:T(8,128)(2,1)} %get-tuple-element.110.g, ...), custom_call_target="tpu_custom_call" | custom-call | flops 26542080 | bytes 26542080 | tf_op jit(solution)/shard_map/adamw/pallas_call | solution.py:663
  545.4 17.5 %adamw.16 = (bf16[2,1152,4608]{2,1,0:T(8,128)(2,1)}, bf16[288,4608]{1,0:T(8,128)(2,1)}, f32[2,288,4608]{2,1,0:T(8,128)}, f32[2,288,4608]{2,1,0:T(8,128)}, s32[1]{0:T(128)}) custom-call(s32[1]{0:T(128)} %get-tuple-element.111.me, f32[8,128]{1,0:T(8,128)} %get-tuple-element.95.factor, ...), custom_call_target="tpu_custom_call", output_to_operand_aliasing={{0}: (6, {}), {2}: (7, {}), {3}: (8, {})} | custom-call | flops 26542080 | bytes 26542080 | tf_op jit(solution)/shard_map/adamw/pallas_call | solution.py:663
  562.9 17.3 %adamw.17 = (bf16[2,4608,1152]{2,1,0:T(8,128)(2,1)}, bf16[1152,1152]{1,0:T(8,128)(2,1)}, f32[2,1152,1152]{2,1,0:T(8,128)}, f32[2,1152,1152]{2,1,0:T(8,128)}, s32[1]{0:T(128)}) custom-call(s32[1]{0:T(128)} %get-tuple-element.115.me, f32[8,128]{1,0:T(8,128)} %get-tuple-element.95.factor, bf16[2,1152,1152]{2,1,0:T(8,128)(2,1)} %get-tuple-element.116.g, ...), custom_call_target="tpu_custom_call" | custom-call | flops 26542080 | bytes 26542080 | tf_op jit(solution)/shard_map/adamw/pallas_call | solution.py:663
  580.1 4.6 adamw.18
  584.7 4.6 adamw.19
  589.3 3.8 adamw.20
  593.2 7.9 adamw.21
  601.1 6.8 adamw_of_other.1
  611.0 14.0 %collective-permute-done.23.refs_0_ = bf16[256,1152]{1,0:T(8,128)(2,1)} collective-permute-done((bf16[256,1152]{1,0:T(8,128)(2,1)}, bf16[256,1152]{1,0:T(8,128)(2,1)}, u32[]{:S(2)}, u32[]{:S(2)}) %collective-permute-start.23) | collective-permute-done | bytes 589856 | tf_op jit(solution)/shard_map/ppermute | solution.py:746
  625.1 2.0 collective-permute-start.11
  627.1 10.6 %collective-permute-done.26.refs_0_ = bf16[256,1152]{1,0:T(8,128)(2,1)} collective-permute-done((bf16[256,1152]{1,0:T(8,128)(2,1)}, bf16[256,1152]{1,0:T(8,128)(2,1)}, u32[]{:S(2)}, u32[]{:S(2)}) %collective-permute-start.26) | collective-permute-done | bytes 589856 | tf_op jit(solution)/shard_map/ppermute | solution.py:746
  642.0 147.1 %collective-permute-done.8.refs_0_ = bf16[288,3072]{1,0:T(8,128)(2,1)S(1)} collective-permute-done((bf16[288,3072]{1,0:T(8,128)(2,1)}, bf16[288,3072]{1,0:T(8,128)(2,1)S(1)}, u32[]{:S(2)}, u32[]{:S(2)}) %collective-permute-start.8) | collective-permute-done | bytes 1769504 | tf_op jit(solution)/shard_map/ppermute | solution.py:746
  794.3 56.6 %collective-permute-done.17.refs_0_ = bf16[288,4608]{1,0:T(8,128)(2,1)S(1)} collective-permute-done((bf16[288,4608]{1,0:T(8,128)(2,1)}, bf16[288,4608]{1,0:T(8,128)(2,1)S(1)}, u32[]{:S(2)}, u32[]{:S(2)}) %collective-permute-start.17) | collective-permute-done | bytes 2654240 | tf_op jit(solution)/shard_map/ppermute | solution.py:746
  851.5 55.8 %collective-permute-done.20.refs_0_ = bf16[1152,1152]{1,0:T(8,128)(2,1)S(1)} collective-permute-done((bf16[1152,1152]{1,0:T(8,128)(2,1)}, bf16[1152,1152]{1,0:T(8,128)(2,1)S(1)}, u32[]{:S(2)}, u32[]{:S(2)}) %collective-permute-start.20) | collective-permute-done | bytes 2654240 | tf_op jit(solution)/shard_map/ppermute | solution.py:746
  907.9 7.0 collective-permute-done.10.refs_2_
  919.3 3.8 place.11
  923.1 3.1 place.12
  926.2 3.5 place.13
  929.7 5.2 place.14
  934.8 7.5 place.15
  942.3 7.5 place.16
  949.8 7.5 place.17
  957.2 7.5 place.18
  964.7 3.4 place.19
  968.2 3.5 place.20
  971.7 3.1 place.21
  (94 shorter events, 18.7 us)
Async XLA Ops:
  491.8 101.4 %collective-permute-start.2 = (bf16[288,512]{1,0:T(8,128)(2,1)}, bf16[288,512]{1,0:T(8,128)(2,1)}, u32[]{:S(2)}, u32[]{:S(2)}) collective-permute-start(bf16[288,512]{1,0:T(8,128)(2,1)} %get-tuple-element.144), channel_id=1, source_target_pairs={{0,2},{1,3},{2,0},{3,1},{4,6},{5,7},{6,4},{7,5}} | collective-permute-start | bytes 884744 | tf_op jit(solution)/shard_map/ppermute | solution.py:746
  496.5 114.0 %collective-permute-start.5 = (bf16[288,1024]{1,0:T(8,128)(2,1)}, bf16[288,1024]{1,0:T(8,128)(2,1)}, u32[]{:S(2)}, u32[]{:S(2)}) collective-permute-start(bf16[288,1024]{1,0:T(8,128)(2,1)} %get-tuple-element.147), channel_id=1, source_target_pairs={{0,2},{1,3},{2,0},{3,1},{4,6},{5,7},{6,4},{7,5}} | collective-permute-start | bytes 1769480 | tf_op jit(solution)/shard_map/ppermute | solution.py:746
  498.5 112.2 %collective-permute-start.6 = (bf16[288,1024]{1,0:T(8,128)(2,1)}, bf16[288,1024]{1,0:T(8,128)(2,1)}, u32[]{:S(2)}, u32[]{:S(2)}) collective-permute-start(bf16[288,1024]{1,0:T(8,128)(2,1)} %get-tuple-element.147), channel_id=1, source_target_pairs={{0,1},{1,0},{2,3},{3,2},{4,5},{5,4},{6,7},{7,6}} | collective-permute-start | bytes 1769480 | tf_op jit(solution)/shard_map/ppermute | solution.py:750
  498.6 109.4 %collective-permute-start.3 = (bf16[288,512]{1,0:T(8,128)(2,1)}, bf16[288,512]{1,0:T(8,128)(2,1)}, u32[]{:S(2)}, u32[]{:S(2)}) collective-permute-start(bf16[288,512]{1,0:T(8,128)(2,1)} %get-tuple-element.144), channel_id=1, source_target_pairs={{0,1},{1,0},{2,3},{3,2},{4,5},{5,4},{6,7},{7,6}} | collective-permute-start | bytes 884744 | tf_op jit(solution)/shard_map/ppermute | solution.py:750
  593.2 15.3 %collective-permute-start.29 = (bf16[128,1152]{1,0:T(8,128)(2,1)}, bf16[128,1152]{1,0:T(8,128)(2,1)}, u32[]{:S(2)}, u32[]{:S(2)}) collective-permute-start(bf16[128,1152]{1,0:T(8,128)(2,1)} %get-tuple-element.173), channel_id=1, source_target_pairs={{0,2},{1,3},{2,0},{3,1},{4,6},{5,7},{6,4},{7,5}} | collective-permute-start | bytes 884744 | tf_op jit(solution)/shard_map/ppermute | solution.py:746
  593.2 15.3 %collective-permute-start.4 = (bf16[288,512]{1,0:T(8,128)(2,1)}, bf16[288,512]{1,0:T(8,128)(2,1)}, u32[]{:S(2)}, u32[]{:S(2)}) collective-permute-start(bf16[288,512]{1,0:T(8,128)(2,1)} %collective-permute-done.2.refs_0_), channel_id=1, source_target_pairs={{0,1},{1,0},{2,3},{3,2},{4,5},{5,4},{6,7},{7,6}} | collective-permute-start | bytes 884744 | tf_op jit(solution)/shard_map/ppermute | solution.py:750
  608.0 29.7 %collective-permute-start.1 = (bf16[512,1152]{1,0:T(8,128)(2,1)}, bf16[512,1152]{1,0:T(8,128)(2,1)S(1)}, u32[]{:S(2)}, u32[]{:S(2)}) collective-permute-start(bf16[512,1152]{1,0:T(8,128)(2,1)} %get-tuple-element.141), channel_id=1, source_target_pairs={{0,1},{1,0},{2,3},{3,2},{4,5},{5,4},{6,7},{7,6}} | collective-permute-start | bytes 3538952 | tf_op jit(solution)/shard_map/ppermute | solution.py:750
  608.5 32.2 %collective-permute-start = (bf16[512,1152]{1,0:T(8,128)(2,1)}, bf16[512,1152]{1,0:T(8,128)(2,1)S(1)}, u32[]{:S(2)}, u32[]{:S(2)}) collective-permute-start(bf16[512,1152]{1,0:T(8,128)(2,1)} %get-tuple-element.140), channel_id=1, source_target_pairs={{0,1},{1,0},{2,3},{3,2},{4,5},{5,4},{6,7},{7,6}} | collective-permute-start | bytes 3538952 | tf_op jit(solution)/shard_map/ppermute | solution.py:750
  608.5 16.5 %collective-permute-start.23 = (bf16[256,1152]{1,0:T(8,128)(2,1)}, bf16[256,1152]{1,0:T(8,128)(2,1)}, u32[]{:S(2)}, u32[]{:S(2)}) collective-permute-start(bf16[256,1152]{1,0:T(8,128)(2,1)} %get-tuple-element.167), channel_id=1, source_target_pairs={{0,2},{1,3},{2,0},{3,1},{4,6},{5,7},{6,4},{7,5}} | collective-permute-start | bytes 1769480 | tf_op jit(solution)/shard_map/ppermute | solution.py:746
  610.5 14.5 %collective-permute-start.24 = (bf16[256,1152]{1,0:T(8,128)(2,1)}, bf16[256,1152]{1,0:T(8,128)(2,1)S(1)}, u32[]{:S(2)}, u32[]{:S(2)}) collective-permute-start(bf16[256,1152]{1,0:T(8,128)(2,1)} %get-tuple-element.167), channel_id=1, source_target_pairs={{0,1},{1,0},{2,3},{3,2},{4,5},{5,4},{6,7},{7,6}} | collective-permute-start | bytes 1769480 | tf_op jit(solution)/shard_map/ppermute | solution.py:750
  610.7 27.0 %collective-permute-start.26 = (bf16[256,1152]{1,0:T(8,128)(2,1)}, bf16[256,1152]{1,0:T(8,128)(2,1)}, u32[]{:S(2)}, u32[]{:S(2)}) collective-permute-start(bf16[256,1152]{1,0:T(8,128)(2,1)} %get-tuple-element.170), channel_id=1, source_target_pairs={{0,2},{1,3},{2,0},{3,1},{4,6},{5,7},{6,4},{7,5}} | collective-permute-start | bytes 1769480 | tf_op jit(solution)/shard_map/ppermute | solution.py:746
  625.1 15.7 %collective-permute-start.7 = (bf16[288,1024]{1,0:T(8,128)(2,1)}, bf16[288,1024]{1,0:T(8,128)(2,1)S(1)}, u32[]{:S(2)}, u32[]{:S(2)}) collective-permute-start(bf16[288,1024]{1,0:T(8,128)(2,1)} %collective-permute-done.5.refs_0_), channel_id=1, source_target_pairs={{0,1},{1,0},{2,3},{3,2},{4,5},{5,4},{6,7},{7,6}} | collective-permute-start | bytes 1769480 | tf_op jit(solution)/shard_map/ppermute | solution.py:750
  625.1 167.0 %collective-permute-start.11 = (bf16[288,4608]{1,0:T(8,128)(2,1)}, bf16[288,4608]{1,0:T(8,128)(2,1)S(1)}, u32[]{:S(2)}, u32[]{:S(2)}) collective-permute-start(bf16[288,4608]{1,0:T(8,128)(2,1)} %get-tuple-element.153), channel_id=1, source_target_pairs={{0,2},{1,3},{2,0},{3,1},{4,6},{5,7},{6,4},{7,5}} | collective-permute-start | bytes 7962632 | tf_op jit(solution)/shard_map/ppermute | solution.py:746
  637.7 154.5 %collective-permute-start.12 = (bf16[288,4608]{1,0:T(8,128)(2,1)}, bf16[288,4608]{1,0:T(8,128)(2,1)S(1)}, u32[]{:S(2)}, u32[]{:S(2)}) collective-permute-start(bf16[288,4608]{1,0:T(8,128)(2,1)} %get-tuple-element.153), channel_id=1, source_target_pairs={{0,1},{1,0},{2,3},{3,2},{4,5},{5,4},{6,7},{7,6}} | collective-permute-start | bytes 7962632 | tf_op jit(solution)/shard_map/ppermute | solution.py:750
  638.7 153.8 %collective-permute-start.14 = (bf16[288,4608]{1,0:T(8,128)(2,1)}, bf16[288,4608]{1,0:T(8,128)(2,1)S(1)}, u32[]{:S(2)}, u32[]{:S(2)}) collective-permute-start(bf16[288,4608]{1,0:T(8,128)(2,1)} %get-tuple-element.157), channel_id=1, source_target_pairs={{0,2},{1,3},{2,0},{3,1},{4,6},{5,7},{6,4},{7,5}} | collective-permute-start | bytes 7962632 | tf_op jit(solution)/shard_map/ppermute | solution.py:746
  640.7 148.3 %collective-permute-start.8 = (bf16[288,3072]{1,0:T(8,128)(2,1)}, bf16[288,3072]{1,0:T(8,128)(2,1)S(1)}, u32[]{:S(2)}, u32[]{:S(2)}) collective-permute-start(bf16[288,3072]{1,0:T(8,128)(2,1)} %get-tuple-element.150), channel_id=1, source_target_pairs={{0,2},{1,3},{2,0},{3,1},{4,6},{5,7},{6,4},{7,5}} | collective-permute-start | bytes 5308424 | tf_op jit(solution)/shard_map/ppermute | solution.py:746
  640.8 148.3 %collective-permute-start.9 = (bf16[288,3072]{1,0:T(8,128)(2,1)}, bf16[288,3072]{1,0:T(8,128)(2,1)S(1)}, u32[]{:S(2)}, u32[]{:S(2)}) collective-permute-start(bf16[288,3072]{1,0:T(8,128)(2,1)} %get-tuple-element.150), channel_id=1, source_target_pairs={{0,1},{1,0},{2,3},{3,2},{4,5},{5,4},{6,7},{7,6}} | collective-permute-start | bytes 5308424 | tf_op jit(solution)/shard_map/ppermute | solution.py:750
  789.0 5.2 collective-permute-start.15
  790.3 60.6 %collective-permute-start.17 = (bf16[288,4608]{1,0:T(8,128)(2,1)}, bf16[288,4608]{1,0:T(8,128)(2,1)S(1)}, u32[]{:S(2)}, u32[]{:S(2)}) collective-permute-start(bf16[288,4608]{1,0:T(8,128)(2,1)} %get-tuple-element.160), channel_id=1, source_target_pairs={{0,2},{1,3},{2,0},{3,1},{4,6},{5,7},{6,4},{7,5}} | collective-permute-start | bytes 7962632 | tf_op jit(solution)/shard_map/ppermute | solution.py:746
  792.1 58.9 %collective-permute-start.18 = (bf16[288,4608]{1,0:T(8,128)(2,1)}, bf16[288,4608]{1,0:T(8,128)(2,1)S(1)}, u32[]{:S(2)}, u32[]{:S(2)}) collective-permute-start(bf16[288,4608]{1,0:T(8,128)(2,1)} %get-tuple-element.160), channel_id=1, source_target_pairs={{0,1},{1,0},{2,3},{3,2},{4,5},{5,4},{6,7},{7,6}} | collective-permute-start | bytes 7962632 | tf_op jit(solution)/shard_map/ppermute | solution.py:750
  792.2 115.1 %collective-permute-start.20 = (bf16[1152,1152]{1,0:T(8,128)(2,1)}, bf16[1152,1152]{1,0:T(8,128)(2,1)S(1)}, u32[]{:S(2)}, u32[]{:S(2)}) collective-permute-start(bf16[1152,1152]{1,0:T(8,128)(2,1)} %get-tuple-element.164), channel_id=1, source_target_pairs={{0,2},{1,3},{2,0},{3,1},{4,6},{5,7},{6,4},{7,5}} | collective-permute-start | bytes 7962632 | tf_op jit(solution)/shard_map/ppermute | solution.py:746
  792.6 114.8 %collective-permute-start.21 = (bf16[1152,1152]{1,0:T(8,128)(2,1)}, bf16[1152,1152]{1,0:T(8,128)(2,1)S(1)}, u32[]{:S(2)}, u32[]{:S(2)}) collective-permute-start(bf16[1152,1152]{1,0:T(8,128)(2,1)} %get-tuple-element.164), channel_id=1, source_target_pairs={{0,1},{1,0},{2,3},{3,2},{4,5},{5,4},{6,7},{7,6}} | collective-permute-start | bytes 7962632 | tf_op jit(solution)/shard_map/ppermute | solution.py:750
  794.2 120.8 %collective-permute-start.13 = (bf16[288,4608]{1,0:T(8,128)(2,1)S(1)}, bf16[288,4608]{1,0:T(8,128)(2,1)S(1)}, u32[]{:S(2)}, u32[]{:S(2)}) collective-permute-start(bf16[288,4608]{1,0:T(8,128)(2,1)S(1)} %collective-permute-done.11.refs_0_), channel_id=1, source_target_pairs={{0,1},{1,0},{2,3},{3,2},{4,5},{5,4},{6,7},{7,6}} | collective-permute-start | bytes 7962632 | tf_op jit(solution)/shard_map/ppermute | solution.py:750
  851.0 64.4 %collective-permute-start.16 = (bf16[288,4608]{1,0:T(8,128)(2,1)S(1)}, bf16[288,4608]{1,0:T(8,128)(2,1)S(1)}, u32[]{:S(2)}, u32[]{:S(2)}) collective-permute-start(bf16[288,4608]{1,0:T(8,128)(2,1)S(1)} %collective-permute-done.14.refs_0_), channel_id=1, source_target_pairs={{0,1},{1,0},{2,3},{3,2},{4,5},{5,4},{6,7},{7,6}} | collective-permute-start | bytes 7962632 | tf_op jit(solution)/shard_map/ppermute | solution.py:750
  851.0 64.6 %collective-permute-start.19 = (bf16[288,4608]{1,0:T(8,128)(2,1)S(1)}, bf16[288,4608]{1,0:T(8,128)(2,1)S(1)}, u32[]{:S(2)}, u32[]{:S(2)}) collective-permute-start(bf16[288,4608]{1,0:T(8,128)(2,1)S(1)} %collective-permute-done.17.refs_0_), channel_id=1, source_target_pairs={{0,1},{1,0},{2,3},{3,2},{4,5},{5,4},{6,7},{7,6}} | collective-permute-start | bytes 7962632 | tf_op jit(solution)/shard_map/ppermute | solution.py:750
  907.3 8.6 collective-permute-start.22
  907.4 7.5 collective-permute-start.10
  914.8 49.9 %collective-permute-start.25 = (bf16[256,1152]{1,0:T(8,128)(2,1)}, bf16[256,1152]{1,0:T(8,128)(2,1)}, u32[]{:S(2)}, u32[]{:S(2)}) collective-permute-start(bf16[256,1152]{1,0:T(8,128)(2,1)} %collective-permute-done.23.refs_0_), channel_id=1, source_target_pairs={{0,1},{1,0},{2,3},{3,2},{4,5},{5,4},{6,7},{7,6}} | collective-permute-start | bytes 1769480 | tf_op jit(solution)/shard_map/ppermute | solution.py:750
  915.0 53.2 %collective-permute-start.27 = (bf16[256,1152]{1,0:T(8,128)(2,1)}, bf16[256,1152]{1,0:T(8,128)(2,1)}, u32[]{:S(2)}, u32[]{:S(2)}) collective-permute-start(bf16[256,1152]{1,0:T(8,128)(2,1)} %get-tuple-element.170), channel_id=1, source_target_pairs={{0,1},{1,0},{2,3},{3,2},{4,5},{5,4},{6,7},{7,6}} | collective-permute-start | bytes 1769480 | tf_op jit(solution)/shard_map/ppermute | solution.py:750
  915.4 52.8 %collective-permute-start.28 = (bf16[256,1152]{1,0:T(8,128)(2,1)}, bf16[256,1152]{1,0:T(8,128)(2,1)}, u32[]{:S(2)}, u32[]{:S(2)}) collective-permute-start(bf16[256,1152]{1,0:T(8,128)(2,1)} %collective-permute-done.26.refs_0_), channel_id=1, source_target_pairs={{0,1},{1,0},{2,3},{3,2},{4,5},{5,4},{6,7},{7,6}} | collective-permute-start | bytes 1769480 | tf_op jit(solution)/shard_map/ppermute | solution.py:750
  915.6 56.1 %collective-permute-start.30 = (bf16[128,1152]{1,0:T(8,128)(2,1)}, bf16[128,1152]{1,0:T(8,128)(2,1)}, u32[]{:S(2)}, u32[]{:S(2)}) collective-permute-start(bf16[128,1152]{1,0:T(8,128)(2,1)} %get-tuple-element.173), channel_id=1, source_target_pairs={{0,1},{1,0},{2,3},{3,2},{4,5},{5,4},{6,7},{7,6}} | collective-permute-start | bytes 884744 | tf_op jit(solution)/shard_map/ppermute | solution.py:750
  916.0 55.7 %collective-permute-start.31 = (bf16[128,1152]{1,0:T(8,128)(2,1)}, bf16[128,1152]{1,0:T(8,128)(2,1)}, u32[]{:S(2)}, u32[]{:S(2)}) collective-permute-start(bf16[128,1152]{1,0:T(8,128)(2,1)} %collective-permute-done.29.refs_0_), channel_id=1, source_target_pairs={{0,1},{1,0},{2,3},{3,2},{4,5},{5,4},{6,7},{7,6}} | collective-permute-start | bytes 884744 | tf_op jit(solution)/shard_map/ppermute | solution.py:750
  (19 other events, 676.4 us)

commit v4 on v3

--- a/solution.py
+++ b/solution.py
@@ -271,16 +271,16 @@
             loop(D // LANES, zero)
 
             def norm_x(i):
-                r = pl.ds(pl.multiple_of(i * LANES, LANES), LANES)
-                wide = DD[r, :].astype(F32)
-                A[r, :] = (wide * scale_of(jnp.mean(wide * wide, axis=1, keepdims=True))).astype(BF16)
-                AT[:, r] = DD[r, :].T
-
-            for c in range(4):
-                load_x[c].wait()
-                loop(T // 4 // LANES, lambda i, c=c: norm_x(c * (T // 4 // LANES) + i))
+                for n in range(2):
+                    r = pl.ds(pl.multiple_of(i * CHUNK + n * LANES, LANES), LANES)
+                    wide = DD[r, :].astype(F32)
+                    A[r, :] = (wide * scale_of(jnp.mean(wide * wide, axis=1, keepdims=True))).astype(BF16)
+
+            quarter = T // 4 // CHUNK
+            for c, load in enumerate(load_x):
+                load.wait()
+                loop(quarter, lambda i, c=c: norm_x(c * quarter + i))
             load_dy = pltpu.make_async_copy(dy, DD, iosem.at[6])
-            load_dy.start()
             pl.semaphore_wait(barrier, DEVICES - 1)
             start(moments())
 
@@ -335,21 +335,18 @@
                 save(j).start()
                 projections(1, slot)
                 product(0)
+                turn(DD, some, AT)
                 start(stores(j, 1))
-
-                @pl.when(j == 0)
-                def _():
-                    load_dy.wait()
-
+                apart(j == NT_ - 1, load_dy.start)
                 down(lo, slot)
                 product(1)
-                turn(DD, some, DT)
                 down(hi, slot)
 
             loop(NT_, tile)
             wait(stores(NT_ - 1, 0) + stores(NT_ - 1, 1))
             save(NT_ - 2).wait()
             save(NT_ - 1).wait()
+            load_dy.wait()
 
         pl.run_scoped(forward, pltpu.VMEM((2, LANES, T), BF16))
 
@@ -378,6 +375,9 @@
 
                 down_rows(64, add)
                 save(i).start()
+                for q in range(D // LANES):
+                    rows = slice(q * LANES, (q + 1) * LANES)
+                    DT[rows, r] = DD[r, rows].T
                 scale = scale_of(summed(squares) / D)
 
                 def norm(rows):

time: 977 us -> 976 us (level)
  no operation moved by 1% of the time
where the time goes in v4:
time: 976 us; the launch traced here: 974 us
  Pallas kernels  659 us (68%)
  waiting for transfers between devices  293 us (30%)
  starting transfers between devices  14.6 us (1%)
    pallas_call x1, Pallas kernels, gradients(): pl.pallas_call(grads_kernel, out_shape=outs, in_specs=[ANY] * 7, out_spec...  487 us
    ppermute x10, waiting for transfers between devices, other_chip(): return lax.ppermute(a, 'dp', [(i, i ^ 2) for i in range(4)])  284 us
    pallas_call x11, Pallas kernels, adamw(): pl.pallas_call(adamw_kernel, grid_spec=pltpu.PrefetchScalarGridSpec(num_s...  110 us
    pallas_call x11, Pallas kernels, place(): pl.pallas_call(functools.partial(place_kernel, n, at), in_specs=[pl.Block...  55.3 us
  transfers between devices with their start and end apart: 32, of which 7 were waited for; matrix products, arithmetic and copies ran while one was open for 0% of the time, Pallas kernels for 17%

profile of v4, /device:TPU:0, one launch (start us, length us, event | category | flops | bytes accessed | tf_op | source)
XLA Modules:
  0.0 974.0 jit_solution(2366128954400585772)
XLA Ops:
  0.6 487.0 %gradients.1 = (bf16[2,288,4608]{2,1,0:T(8,128)(2,1)}, bf16[2,288,4608]{2,1,0:T(8,128)(2,1)}, bf16[2,1152,1152]{2,1,0:T(8,128)(2,1)}, f32[8,128]{1,0:T(8,128)}, ...) custom-call(bf16[2048,1152]{1,0:T(8,128)(2,1)} %bitcast.3, ...), custom_call_target="tpu_custom_call" | custom-call | tf_op jit(solution)/shard_map/gradients/pallas_call | solution.py:602
  487.7 3.3 adamw.11
  491.0 4.7 adamw.12
  495.7 2.0 collective-permute-start.5
  498.2 11.5 %adamw.13 = (bf16[2,1152,4608]{2,1,0:T(8,128)(2,1)}, bf16[288,3072]{1,0:T(8,128)(2,1)}, f32[2,288,4608]{2,1,0:T(8,128)}, f32[2,288,4608]{2,1,0:T(8,128)}, s32[1]{0:T(128)}) custom-call(s32[1]{0:T(128)} %get-tuple-element.101.me, f32[8,128]{1,0:T(8,128)} %get-tuple-element.95.factor, ...), custom_call_target="tpu_custom_call", output_to_operand_aliasing={{0}: (6, {}), {2}: (7, {}), {3}: (8, {})} | custom-call | flops 17694720 | bytes 17694720 | tf_op jit(solution)/shard_map/adamw/pallas_call | solution.py:663
  509.7 17.5 %adamw.14 = (bf16[2,1152,4608]{2,1,0:T(8,128)(2,1)}, bf16[288,4608]{1,0:T(8,128)(2,1)}, f32[2,288,4608]{2,1,0:T(8,128)}, f32[2,288,4608]{2,1,0:T(8,128)}, s32[1]{0:T(128)}) custom-call(s32[1]{0:T(128)} %get-tuple-element.105.me, f32[8,128]{1,0:T(8,128)} %get-tuple-element.95.factor, ...), custom_call_target="tpu_custom_call", output_to_operand_aliasing={{0}: (6, {}), {2}: (7, {}), {3}: (8, {})} | custom-call | flops 26542080 | bytes 26542080 | tf_op jit(solution)/shard_map/adamw/pallas_call | solution.py:663
  527.1 17.5 %adamw.15 = (bf16[2,1152,4608]{2,1,0:T(8,128)(2,1)}, bf16[288,4608]{1,0:T(8,128)(2,1)}, f32[2,288,4608]{2,1,0:T(8,128)}, f32[2,288,4608]{2,1,0:T(8,128)}, s32[1]{0:T(128)}) custom-call(s32[1]{0:T(128)} %get-tuple-element.109.me, f32[8,128]{1,0:T(8,128)} %get-tuple-element.95.factor, bf16[2,288,4608]{2,1,0:T(8,128)(2,1)} %get-tuple-element.110.g, ...), custom_call_target="tpu_custom_call" | custom-call | flops 26542080 | bytes 26542080 | tf_op jit(solution)/shard_map/adamw/pallas_call | solution.py:663
  544.6 17.5 %adamw.16 = (bf16[2,1152,4608]{2,1,0:T(8,128)(2,1)}, bf16[288,4608]{1,0:T(8,128)(2,1)}, f32[2,288,4608]{2,1,0:T(8,128)}, f32[2,288,4608]{2,1,0:T(8,128)}, s32[1]{0:T(128)}) custom-call(s32[1]{0:T(128)} %get-tuple-element.111.me, f32[8,128]{1,0:T(8,128)} %get-tuple-element.95.factor, ...), custom_call_target="tpu_custom_call", output_to_operand_aliasing={{0}: (6, {}), {2}: (7, {}), {3}: (8, {})} | custom-call | flops 26542080 | bytes 26542080 | tf_op jit(solution)/shard_map/adamw/pallas_call | solution.py:663
  562.0 17.3 %adamw.17 = (bf16[2,4608,1152]{2,1,0:T(8,128)(2,1)}, bf16[1152,1152]{1,0:T(8,128)(2,1)}, f32[2,1152,1152]{2,1,0:T(8,128)}, f32[2,1152,1152]{2,1,0:T(8,128)}, s32[1]{0:T(128)}) custom-call(s32[1]{0:T(128)} %get-tuple-element.115.me, f32[8,128]{1,0:T(8,128)} %get-tuple-element.95.factor, bf16[2,1152,1152]{2,1,0:T(8,128)(2,1)} %get-tuple-element.116.g, ...), custom_call_target="tpu_custom_call" | custom-call | flops 26542080 | bytes 26542080 | tf_op jit(solution)/shard_map/adamw/pallas_call | solution.py:663
  579.3 4.6 adamw.18
  583.9 4.6 adamw.19
  588.5 3.8 adamw.20
  592.4 7.9 adamw.21
  600.3 6.8 adamw_of_other.1
  610.2 14.0 %collective-permute-done.23.refs_0_ = bf16[256,1152]{1,0:T(8,128)(2,1)} collective-permute-done((bf16[256,1152]{1,0:T(8,128)(2,1)}, bf16[256,1152]{1,0:T(8,128)(2,1)}, u32[]{:S(2)}, u32[]{:S(2)}) %collective-permute-start.23) | collective-permute-done | bytes 589856 | tf_op jit(solution)/shard_map/ppermute | solution.py:746
  624.2 2.0 collective-permute-start.11
  626.2 10.6 %collective-permute-done.26.refs_0_ = bf16[256,1152]{1,0:T(8,128)(2,1)} collective-permute-done((bf16[256,1152]{1,0:T(8,128)(2,1)}, bf16[256,1152]{1,0:T(8,128)(2,1)}, u32[]{:S(2)}, u32[]{:S(2)}) %collective-permute-start.26) | collective-permute-done | bytes 589856 | tf_op jit(solution)/shard_map/ppermute | solution.py:746
  641.1 147.1 %collective-permute-done.8.refs_0_ = bf16[288,3072]{1,0:T(8,128)(2,1)S(1)} collective-permute-done((bf16[288,3072]{1,0:T(8,128)(2,1)}, bf16[288,3072]{1,0:T(8,128)(2,1)S(1)}, u32[]{:S(2)}, u32[]{:S(2)}) %collective-permute-start.8) | collective-permute-done | bytes 1769504 | tf_op jit(solution)/shard_map/ppermute | solution.py:746
  793.5 56.6 %collective-permute-done.17.refs_0_ = bf16[288,4608]{1,0:T(8,128)(2,1)S(1)} collective-permute-done((bf16[288,4608]{1,0:T(8,128)(2,1)}, bf16[288,4608]{1,0:T(8,128)(2,1)S(1)}, u32[]{:S(2)}, u32[]{:S(2)}) %collective-permute-start.17) | collective-permute-done | bytes 2654240 | tf_op jit(solution)/shard_map/ppermute | solution.py:746
  850.6 55.8 %collective-permute-done.20.refs_0_ = bf16[1152,1152]{1,0:T(8,128)(2,1)S(1)} collective-permute-done((bf16[1152,1152]{1,0:T(8,128)(2,1)}, bf16[1152,1152]{1,0:T(8,128)(2,1)S(1)}, u32[]{:S(2)}, u32[]{:S(2)}) %collective-permute-start.20) | collective-permute-done | bytes 2654240 | tf_op jit(solution)/shard_map/ppermute | solution.py:746
  907.0 7.0 collective-permute-done.10.refs_2_
  918.5 3.8 place.11
  922.3 3.1 place.12
  925.3 3.5 place.13
  928.8 5.2 place.14
  934.0 7.5 place.15
  941.5 7.5 place.16
  948.9 7.5 place.17
  956.4 7.5 place.18
  963.9 3.4 place.19
  967.3 3.5 place.20
  970.8 3.1 place.21
  (94 shorter events, 18.7 us)
Async XLA Ops:
  490.9 101.4 %collective-permute-start.2 = (bf16[288,512]{1,0:T(8,128)(2,1)}, bf16[288,512]{1,0:T(8,128)(2,1)}, u32[]{:S(2)}, u32[]{:S(2)}) collective-permute-start(bf16[288,512]{1,0:T(8,128)(2,1)} %get-tuple-element.144), channel_id=1, source_target_pairs={{0,2},{1,3},{2,0},{3,1},{4,6},{5,7},{6,4},{7,5}} | collective-permute-start | bytes 884744 | tf_op jit(solution)/shard_map/ppermute | solution.py:746
  495.7 114.0 %collective-permute-start.5 = (bf16[288,1024]{1,0:T(8,128)(2,1)}, bf16[288,1024]{1,0:T(8,128)(2,1)}, u32[]{:S(2)}, u32[]{:S(2)}) collective-permute-start(bf16[288,1024]{1,0:T(8,128)(2,1)} %get-tuple-element.147), channel_id=1, source_target_pairs={{0,2},{1,3},{2,0},{3,1},{4,6},{5,7},{6,4},{7,5}} | collective-permute-start | bytes 1769480 | tf_op jit(solution)/shard_map/ppermute | solution.py:746
  497.7 112.2 %collective-permute-start.6 = (bf16[288,1024]{1,0:T(8,128)(2,1)}, bf16[288,1024]{1,0:T(8,128)(2,1)}, u32[]{:S(2)}, u32[]{:S(2)}) collective-permute-start(bf16[288,1024]{1,0:T(8,128)(2,1)} %get-tuple-element.147), channel_id=1, source_target_pairs={{0,1},{1,0},{2,3},{3,2},{4,5},{5,4},{6,7},{7,6}} | collective-permute-start | bytes 1769480 | tf_op jit(solution)/shard_map/ppermute | solution.py:750
  497.7 109.4 %collective-permute-start.3 = (bf16[288,512]{1,0:T(8,128)(2,1)}, bf16[288,512]{1,0:T(8,128)(2,1)}, u32[]{:S(2)}, u32[]{:S(2)}) collective-permute-start(bf16[288,512]{1,0:T(8,128)(2,1)} %get-tuple-element.144), channel_id=1, source_target_pairs={{0,1},{1,0},{2,3},{3,2},{4,5},{5,4},{6,7},{7,6}} | collective-permute-start | bytes 884744 | tf_op jit(solution)/shard_map/ppermute | solution.py:750
  592.3 15.3 %collective-permute-start.29 = (bf16[128,1152]{1,0:T(8,128)(2,1)}, bf16[128,1152]{1,0:T(8,128)(2,1)}, u32[]{:S(2)}, u32[]{:S(2)}) collective-permute-start(bf16[128,1152]{1,0:T(8,128)(2,1)} %get-tuple-element.173), channel_id=1, source_target_pairs={{0,2},{1,3},{2,0},{3,1},{4,6},{5,7},{6,4},{7,5}} | collective-permute-start | bytes 884744 | tf_op jit(solution)/shard_map/ppermute | solution.py:746
  592.4 15.3 %collective-permute-start.4 = (bf16[288,512]{1,0:T(8,128)(2,1)}, bf16[288,512]{1,0:T(8,128)(2,1)}, u32[]{:S(2)}, u32[]{:S(2)}) collective-permute-start(bf16[288,512]{1,0:T(8,128)(2,1)} %collective-permute-done.2.refs_0_), channel_id=1, source_target_pairs={{0,1},{1,0},{2,3},{3,2},{4,5},{5,4},{6,7},{7,6}} | collective-permute-start | bytes 884744 | tf_op jit(solution)/shard_map/ppermute | solution.py:750
  607.1 29.7 %collective-permute-start.1 = (bf16[512,1152]{1,0:T(8,128)(2,1)}, bf16[512,1152]{1,0:T(8,128)(2,1)S(1)}, u32[]{:S(2)}, u32[]{:S(2)}) collective-permute-start(bf16[512,1152]{1,0:T(8,128)(2,1)} %get-tuple-element.141), channel_id=1, source_target_pairs={{0,1},{1,0},{2,3},{3,2},{4,5},{5,4},{6,7},{7,6}} | collective-permute-start | bytes 3538952 | tf_op jit(solution)/shard_map/ppermute | solution.py:750
  607.6 32.2 %collective-permute-start = (bf16[512,1152]{1,0:T(8,128)(2,1)}, bf16[512,1152]{1,0:T(8,128)(2,1)S(1)}, u32[]{:S(2)}, u32[]{:S(2)}) collective-permute-start(bf16[512,1152]{1,0:T(8,128)(2,1)} %get-tuple-element.140), channel_id=1, source_target_pairs={{0,1},{1,0},{2,3},{3,2},{4,5},{5,4},{6,7},{7,6}} | collective-permute-start | bytes 3538952 | tf_op jit(solution)/shard_map/ppermute | solution.py:750
  607.7 16.5 %collective-permute-start.23 = (bf16[256,1152]{1,0:T(8,128)(2,1)}, bf16[256,1152]{1,0:T(8,128)(2,1)}, u32[]{:S(2)}, u32[]{:S(2)}) collective-permute-start(bf16[256,1152]{1,0:T(8,128)(2,1)} %get-tuple-element.167), channel_id=1, source_target_pairs={{0,2},{1,3},{2,0},{3,1},{4,6},{5,7},{6,4},{7,5}} | collective-permute-start | bytes 1769480 | tf_op jit(solution)/shard_map/ppermute | solution.py:746
  609.7 14.5 %collective-permute-start.24 = (bf16[256,1152]{1,0:T(8,128)(2,1)}, bf16[256,1152]{1,0:T(8,128)(2,1)S(1)}, u32[]{:S(2)}, u32[]{:S(2)}) collective-permute-start(bf16[256,1152]{1,0:T(8,128)(2,1)} %get-tuple-element.167), channel_id=1, source_target_pairs={{0,1},{1,0},{2,3},{3,2},{4,5},{5,4},{6,7},{7,6}} | collective-permute-start | bytes 1769480 | tf_op jit(solution)/shard_map/ppermute | solution.py:750
  609.9 27.0 %collective-permute-start.26 = (bf16[256,1152]{1,0:T(8,128)(2,1)}, bf16[256,1152]{1,0:T(8,128)(2,1)}, u32[]{:S(2)}, u32[]{:S(2)}) collective-permute-start(bf16[256,1152]{1,0:T(8,128)(2,1)} %get-tuple-element.170), channel_id=1, source_target_pairs={{0,2},{1,3},{2,0},{3,1},{4,6},{5,7},{6,4},{7,5}} | collective-permute-start | bytes 1769480 | tf_op jit(solution)/shard_map/ppermute | solution.py:746
  624.2 15.7 %collective-permute-start.7 = (bf16[288,1024]{1,0:T(8,128)(2,1)}, bf16[288,1024]{1,0:T(8,128)(2,1)S(1)}, u32[]{:S(2)}, u32[]{:S(2)}) collective-permute-start(bf16[288,1024]{1,0:T(8,128)(2,1)} %collective-permute-done.5.refs_0_), channel_id=1, source_target_pairs={{0,1},{1,0},{2,3},{3,2},{4,5},{5,4},{6,7},{7,6}} | collective-permute-start | bytes 1769480 | tf_op jit(solution)/shard_map/ppermute | solution.py:750
  624.2 167.0 %collective-permute-start.11 = (bf16[288,4608]{1,0:T(8,128)(2,1)}, bf16[288,4608]{1,0:T(8,128)(2,1)S(1)}, u32[]{:S(2)}, u32[]{:S(2)}) collective-permute-start(bf16[288,4608]{1,0:T(8,128)(2,1)} %get-tuple-element.153), channel_id=1, source_target_pairs={{0,2},{1,3},{2,0},{3,1},{4,6},{5,7},{6,4},{7,5}} | collective-permute-start | bytes 7962632 | tf_op jit(solution)/shard_map/ppermute | solution.py:746
  636.8 154.5 %collective-permute-start.12 = (bf16[288,4608]{1,0:T(8,128)(2,1)}, bf16[288,4608]{1,0:T(8,128)(2,1)S(1)}, u32[]{:S(2)}, u32[]{:S(2)}) collective-permute-start(bf16[288,4608]{1,0:T(8,128)(2,1)} %get-tuple-element.153), channel_id=1, source_target_pairs={{0,1},{1,0},{2,3},{3,2},{4,5},{5,4},{6,7},{7,6}} | collective-permute-start | bytes 7962632 | tf_op jit(solution)/shard_map/ppermute | solution.py:750
  637.9 153.8 %collective-permute-start.14 = (bf16[288,4608]{1,0:T(8,128)(2,1)}, bf16[288,4608]{1,0:T(8,128)(2,1)S(1)}, u32[]{:S(2)}, u32[]{:S(2)}) collective-permute-start(bf16[288,4608]{1,0:T(8,128)(2,1)} %get-tuple-element.157), channel_id=1, source_target_pairs={{0,2},{1,3},{2,0},{3,1},{4,6},{5,7},{6,4},{7,5}} | collective-permute-start | bytes 7962632 | tf_op jit(solution)/shard_map/ppermute | solution.py:746
  639.9 148.3 %collective-permute-start.8 = (bf16[288,3072]{1,0:T(8,128)(2,1)}, bf16[288,3072]{1,0:T(8,128)(2,1)S(1)}, u32[]{:S(2)}, u32[]{:S(2)}) collective-permute-start(bf16[288,3072]{1,0:T(8,128)(2,1)} %get-tuple-element.150), channel_id=1, source_target_pairs={{0,2},{1,3},{2,0},{3,1},{4,6},{5,7},{6,4},{7,5}} | collective-permute-start | bytes 5308424 | tf_op jit(solution)/shard_map/ppermute | solution.py:746
  639.9 148.3 %collective-permute-start.9 = (bf16[288,3072]{1,0:T(8,128)(2,1)}, bf16[288,3072]{1,0:T(8,128)(2,1)S(1)}, u32[]{:S(2)}, u32[]{:S(2)}) collective-permute-start(bf16[288,3072]{1,0:T(8,128)(2,1)} %get-tuple-element.150), channel_id=1, source_target_pairs={{0,1},{1,0},{2,3},{3,2},{4,5},{5,4},{6,7},{7,6}} | collective-permute-start | bytes 5308424 | tf_op jit(solution)/shard_map/ppermute | solution.py:750
  788.2 5.2 collective-permute-start.15
  789.5 60.6 %collective-permute-start.17 = (bf16[288,4608]{1,0:T(8,128)(2,1)}, bf16[288,4608]{1,0:T(8,128)(2,1)S(1)}, u32[]{:S(2)}, u32[]{:S(2)}) collective-permute-start(bf16[288,4608]{1,0:T(8,128)(2,1)} %get-tuple-element.160), channel_id=1, source_target_pairs={{0,2},{1,3},{2,0},{3,1},{4,6},{5,7},{6,4},{7,5}} | collective-permute-start | bytes 7962632 | tf_op jit(solution)/shard_map/ppermute | solution.py:746
  791.2 58.9 %collective-permute-start.18 = (bf16[288,4608]{1,0:T(8,128)(2,1)}, bf16[288,4608]{1,0:T(8,128)(2,1)S(1)}, u32[]{:S(2)}, u32[]{:S(2)}) collective-permute-start(bf16[288,4608]{1,0:T(8,128)(2,1)} %get-tuple-element.160), channel_id=1, source_target_pairs={{0,1},{1,0},{2,3},{3,2},{4,5},{5,4},{6,7},{7,6}} | collective-permute-start | bytes 7962632 | tf_op jit(solution)/shard_map/ppermute | solution.py:750
  791.4 115.1 %collective-permute-start.20 = (bf16[1152,1152]{1,0:T(8,128)(2,1)}, bf16[1152,1152]{1,0:T(8,128)(2,1)S(1)}, u32[]{:S(2)}, u32[]{:S(2)}) collective-permute-start(bf16[1152,1152]{1,0:T(8,128)(2,1)} %get-tuple-element.164), channel_id=1, source_target_pairs={{0,2},{1,3},{2,0},{3,1},{4,6},{5,7},{6,4},{7,5}} | collective-permute-start | bytes 7962632 | tf_op jit(solution)/shard_map/ppermute | solution.py:746
  791.7 114.8 %collective-permute-start.21 = (bf16[1152,1152]{1,0:T(8,128)(2,1)}, bf16[1152,1152]{1,0:T(8,128)(2,1)S(1)}, u32[]{:S(2)}, u32[]{:S(2)}) collective-permute-start(bf16[1152,1152]{1,0:T(8,128)(2,1)} %get-tuple-element.164), channel_id=1, source_target_pairs={{0,1},{1,0},{2,3},{3,2},{4,5},{5,4},{6,7},{7,6}} | collective-permute-start | bytes 7962632 | tf_op jit(solution)/shard_map/ppermute | solution.py:750
  793.3 120.8 %collective-permute-start.13 = (bf16[288,4608]{1,0:T(8,128)(2,1)S(1)}, bf16[288,4608]{1,0:T(8,128)(2,1)S(1)}, u32[]{:S(2)}, u32[]{:S(2)}) collective-permute-start(bf16[288,4608]{1,0:T(8,128)(2,1)S(1)} %collective-permute-done.11.refs_0_), channel_id=1, source_target_pairs={{0,1},{1,0},{2,3},{3,2},{4,5},{5,4},{6,7},{7,6}} | collective-permute-start | bytes 7962632 | tf_op jit(solution)/shard_map/ppermute | solution.py:750
  850.1 64.4 %collective-permute-start.16 = (bf16[288,4608]{1,0:T(8,128)(2,1)S(1)}, bf16[288,4608]{1,0:T(8,128)(2,1)S(1)}, u32[]{:S(2)}, u32[]{:S(2)}) collective-permute-start(bf16[288,4608]{1,0:T(8,128)(2,1)S(1)} %collective-permute-done.14.refs_0_), channel_id=1, source_target_pairs={{0,1},{1,0},{2,3},{3,2},{4,5},{5,4},{6,7},{7,6}} | collective-permute-start | bytes 7962632 | tf_op jit(solution)/shard_map/ppermute | solution.py:750
  850.1 64.6 %collective-permute-start.19 = (bf16[288,4608]{1,0:T(8,128)(2,1)S(1)}, bf16[288,4608]{1,0:T(8,128)(2,1)S(1)}, u32[]{:S(2)}, u32[]{:S(2)}) collective-permute-start(bf16[288,4608]{1,0:T(8,128)(2,1)S(1)} %collective-permute-done.17.refs_0_), channel_id=1, source_target_pairs={{0,1},{1,0},{2,3},{3,2},{4,5},{5,4},{6,7},{7,6}} | collective-permute-start | bytes 7962632 | tf_op jit(solution)/shard_map/ppermute | solution.py:750
  906.5 8.6 collective-permute-start.22
  906.5 7.5 collective-permute-start.10
  914.0 49.9 %collective-permute-start.25 = (bf16[256,1152]{1,0:T(8,128)(2,1)}, bf16[256,1152]{1,0:T(8,128)(2,1)}, u32[]{:S(2)}, u32[]{:S(2)}) collective-permute-start(bf16[256,1152]{1,0:T(8,128)(2,1)} %collective-permute-done.23.refs_0_), channel_id=1, source_target_pairs={{0,1},{1,0},{2,3},{3,2},{4,5},{5,4},{6,7},{7,6}} | collective-permute-start | bytes 1769480 | tf_op jit(solution)/shard_map/ppermute | solution.py:750
  914.1 53.2 %collective-permute-start.27 = (bf16[256,1152]{1,0:T(8,128)(2,1)}, bf16[256,1152]{1,0:T(8,128)(2,1)}, u32[]{:S(2)}, u32[]{:S(2)}) collective-permute-start(bf16[256,1152]{1,0:T(8,128)(2,1)} %get-tuple-element.170), channel_id=1, source_target_pairs={{0,1},{1,0},{2,3},{3,2},{4,5},{5,4},{6,7},{7,6}} | collective-permute-start | bytes 1769480 | tf_op jit(solution)/shard_map/ppermute | solution.py:750
  914.5 52.8 %collective-permute-start.28 = (bf16[256,1152]{1,0:T(8,128)(2,1)}, bf16[256,1152]{1,0:T(8,128)(2,1)}, u32[]{:S(2)}, u32[]{:S(2)}) collective-permute-start(bf16[256,1152]{1,0:T(8,128)(2,1)} %collective-permute-done.26.refs_0_), channel_id=1, source_target_pairs={{0,1},{1,0},{2,3},{3,2},{4,5},{5,4},{6,7},{7,6}} | collective-permute-start | bytes 1769480 | tf_op jit(solution)/shard_map/ppermute | solution.py:750
  914.7 56.1 %collective-permute-start.30 = (bf16[128,1152]{1,0:T(8,128)(2,1)}, bf16[128,1152]{1,0:T(8,128)(2,1)}, u32[]{:S(2)}, u32[]{:S(2)}) collective-permute-start(bf16[128,1152]{1,0:T(8,128)(2,1)} %get-tuple-element.173), channel_id=1, source_target_pairs={{0,1},{1,0},{2,3},{3,2},{4,5},{5,4},{6,7},{7,6}} | collective-permute-start | bytes 884744 | tf_op jit(solution)/shard_map/ppermute | solution.py:750
  915.1 55.7 %collective-permute-start.31 = (bf16[128,1152]{1,0:T(8,128)(2,1)}, bf16[128,1152]{1,0:T(8,128)(2,1)}, u32[]{:S(2)}, u32[]{:S(2)}) collective-permute-start(bf16[128,1152]{1,0:T(8,128)(2,1)} %collective-permute-done.29.refs_0_), channel_id=1, source_target_pairs={{0,1},{1,0},{2,3},{3,2},{4,5},{5,4},{6,7},{7,6}} | collective-permute-start | bytes 884744 | tf_op jit(solution)/shard_map/ppermute | solution.py:750
  (19 other events, 676.4 us)
